TPU v7x, 16 devices: a whole 2x2x2 slice. The times are simulated.
16 devices in a mesh: tp: 2 (over z), dp: 8 (over y, x, core).
Axes of the slice: x: 2, y: 2, z: 2, core: 2. Of those that a mesh axis runs over, the one named last changes fastest.
Arguments:
- hidden: bfloat16 [32, 512, 3072], P('dp', 'tp')
- norm_gain: bfloat16 [3072], P('dp')
- w_query: bfloat16 [3072, 3072], P('dp', 'tp')
- w_key: bfloat16 [3072, 1024], P('dp', 'tp')
- w_value: bfloat16 [3072, 1024], P('dp', 'tp')
- w_out: bfloat16 [3072, 3072], P('tp', 'dp')
- grad_out: bfloat16 [32, 512, 3072], P('dp', 'tp')
Outputs:
- output 1: bfloat16 [32, 512, 3072], P('dp', 'tp')
- output 2: bfloat16 [32, 512, 3072], P('dp', 'tp')
- output 3: float32 [3072], P('dp')
- output 4: float32 [3072, 3072], P('dp', 'tp')
- output 5: float32 [3072, 1024], P('dp', 'tp')
- output 6: float32 [3072, 1024], P('dp', 'tp')
- output 7: float32 [3072, 3072], P('tp', 'dp')
All inputs are finite; a program needn't handle non-finite values.
Results may differ from a plain program's by a relative error of at most 0.02.
Values are sent between devices in bfloat16 or wider.
A program may use at most 1 GiB of HBM per device.

v0:
```python
import jax
import jax.numpy as jnp
from jax import lax
from jax.sharding import PartitionSpec as P, NamedSharding

HEAD_DIM = 128
NORM_EPS = 1e-5
ROPE_BASE = 500000.0
SCORE_SCALE = HEAD_DIM ** -0.5
MASK_VALUE = -1e30


def rope_tables(seq_len):
    half_dim = HEAD_DIM // 2
    inv_freq = ROPE_BASE ** (-jnp.arange(half_dim, dtype=jnp.float32) * 2.0 / HEAD_DIM)
    angles = jnp.arange(seq_len, dtype=jnp.float32)[:, None] * inv_freq[None, :]
    return jnp.cos(angles), jnp.sin(angles)


def rotate(values, cos_t, sin_t):
    half_dim = values.shape[-1] // 2
    lower_half = values[..., :half_dim]
    upper_half = values[..., half_dim:]
    return jnp.concatenate([lower_half * cos_t - upper_half * sin_t, upper_half * cos_t + lower_half * sin_t], axis=-1)


def solution(mesh):
    def local_block(hidden, norm_gain, w_query, w_key, w_value, w_out, grad_out):
        gain_full = lax.all_gather(norm_gain, "dp", axis=0, tiled=True).astype(jnp.float32)
        wq_full = lax.all_gather(w_query, "dp", axis=0, tiled=True)
        wk_full = lax.all_gather(w_key, "dp", axis=0, tiled=True)
        wv_full = lax.all_gather(w_value, "dp", axis=0, tiled=True)
        wo_full = lax.all_gather(w_out, "dp", axis=1, tiled=True)
        batch_loc = hidden.shape[0]
        kv_loc = wk_full.shape[1] // HEAD_DIM
        group_size = wq_full.shape[1] // wk_full.shape[1]

        hidden_f32 = hidden.astype(jnp.float32)
        inv_rms = lax.rsqrt(jnp.mean(hidden_f32 * hidden_f32, axis=-1, keepdims=True) + NORM_EPS)
        x_hat = hidden_f32 * inv_rms
        normed = lax.all_gather((x_hat * gain_full).astype(jnp.bfloat16), "tp", axis=1, tiled=True)
        seq_len = normed.shape[1]
        q_shape = (batch_loc, seq_len, kv_loc, group_size, HEAD_DIM)
        k_shape = (batch_loc, seq_len, kv_loc, HEAD_DIM)
        cos_t, sin_t = rope_tables(seq_len)
        cos_q, sin_q = cos_t[:, None, None, :], sin_t[:, None, None, :]
        cos_k, sin_k = cos_t[:, None, :], sin_t[:, None, :]

        q_lin = jnp.einsum("bsd,de->bse", normed, wq_full, preferred_element_type=jnp.float32).astype(jnp.bfloat16)
        k_lin = jnp.einsum("bsd,de->bse", normed, wk_full, preferred_element_type=jnp.float32).astype(jnp.bfloat16)
        v_heads = jnp.einsum("bsd,de->bse", normed, wv_full, preferred_element_type=jnp.float32).astype(jnp.bfloat16).reshape(k_shape)
        q_heads = rotate(q_lin.reshape(q_shape).astype(jnp.float32), cos_q, sin_q).astype(jnp.bfloat16)
        k_heads = rotate(k_lin.reshape(k_shape).astype(jnp.float32), cos_k, sin_k).astype(jnp.bfloat16)

        causal = jnp.arange(seq_len)[:, None] >= jnp.arange(seq_len)[None, :]
        scores = jnp.einsum("bqgrd,bkgd->bgrqk", q_heads, k_heads, preferred_element_type=jnp.float32) * SCORE_SCALE
        attn_prob = jax.nn.softmax(jnp.where(causal, scores, MASK_VALUE), axis=-1)
        prob_bf16 = attn_prob.astype(jnp.bfloat16)
        attn_out = jnp.einsum("bgrqk,bkgd->bqgrd", prob_bf16, v_heads, preferred_element_type=jnp.float32).astype(jnp.bfloat16).reshape(batch_loc, seq_len, -1)
        out_part = jnp.einsum("bse,ed->bsd", attn_out, wo_full, preferred_element_type=jnp.float32).astype(jnp.bfloat16)
        out_loc = lax.psum_scatter(out_part, "tp", scatter_dimension=1, tiled=True)
        hidden_out = (hidden_f32 + out_loc.astype(jnp.float32)).astype(jnp.bfloat16)

        grad_full = lax.all_gather(grad_out, "tp", axis=1, tiled=True)
        grad_wo = jnp.einsum("bse,bsd->ed", attn_out, grad_full, preferred_element_type=jnp.float32)
        grad_attn = jnp.einsum("bsd,ed->bse", grad_full, wo_full, preferred_element_type=jnp.float32).astype(jnp.bfloat16).reshape(q_shape)
        grad_v = jnp.einsum("bgrqk,bqgrd->bkgd", prob_bf16, grad_attn, preferred_element_type=jnp.float32).astype(jnp.bfloat16)
        grad_prob = jnp.einsum("bqgrd,bkgd->bgrqk", grad_attn, v_heads, preferred_element_type=jnp.float32).astype(jnp.bfloat16).astype(jnp.float32)
        grad_scores = attn_prob * (grad_prob - jnp.sum(grad_prob * attn_prob, axis=-1, keepdims=True))
        grad_scores = (grad_scores * SCORE_SCALE).astype(jnp.bfloat16)
        grad_q = jnp.einsum("bgrqk,bkgd->bqgrd", grad_scores, k_heads, preferred_element_type=jnp.float32).astype(jnp.bfloat16)
        grad_k = jnp.einsum("bgrqk,bqgrd->bkgd", grad_scores, q_heads, preferred_element_type=jnp.float32).astype(jnp.bfloat16)
        grad_q_lin = rotate(grad_q.astype(jnp.float32), cos_q, -sin_q).astype(jnp.bfloat16).reshape(batch_loc, seq_len, -1)
        grad_k_lin = rotate(grad_k.astype(jnp.float32), cos_k, -sin_k).astype(jnp.bfloat16).reshape(batch_loc, seq_len, -1)
        grad_v_lin = grad_v.reshape(batch_loc, seq_len, -1)
        grad_normed_part = (
            jnp.einsum("bse,de->bsd", grad_q_lin, wq_full, preferred_element_type=jnp.float32)
            + jnp.einsum("bse,de->bsd", grad_k_lin, wk_full, preferred_element_type=jnp.float32)
            + jnp.einsum("bse,de->bsd", grad_v_lin, wv_full, preferred_element_type=jnp.float32)
        ).astype(jnp.bfloat16)
        grad_normed = lax.psum_scatter(grad_normed_part, "tp", scatter_dimension=1, tiled=True).astype(jnp.float32)
        grad_wq = jnp.einsum("bsd,bse->de", normed, grad_q_lin, preferred_element_type=jnp.float32)
        grad_wk = jnp.einsum("bsd,bse->de", normed, grad_k_lin, preferred_element_type=jnp.float32)
        grad_wv = jnp.einsum("bsd,bse->de", normed, grad_v_lin, preferred_element_type=jnp.float32)
        gain_part = jnp.sum(grad_normed * x_hat, axis=(0, 1))
        grad_gain = lax.psum(lax.psum_scatter(gain_part, "dp", scatter_dimension=0, tiled=True), "tp")
        value_a9 = grad_normed * gain_full
        grad_hidden = (grad_out.astype(jnp.float32) + inv_rms * (value_a9 - x_hat * jnp.mean(value_a9 * x_hat, axis=-1, keepdims=True))).astype(jnp.bfloat16)
        return (
            hidden_out,
            grad_hidden,
            grad_gain,
            lax.psum_scatter(grad_wq, "dp", scatter_dimension=0, tiled=True),
            lax.psum_scatter(grad_wk, "dp", scatter_dimension=0, tiled=True),
            lax.psum_scatter(grad_wv, "dp", scatter_dimension=0, tiled=True),
            lax.psum_scatter(grad_wo, "dp", scatter_dimension=1, tiled=True),
        )

    act_spec = P("dp", "tp", None)
    col_spec = P("dp", "tp")
    row_spec = P("tp", "dp")
    return jax.shard_map(
        local_block,
        mesh=mesh,
        in_specs=(act_spec, P("dp"), col_spec, col_spec, col_spec, row_spec, act_spec),
        out_specs=(act_spec, act_spec, P("dp"), col_spec, col_spec, col_spec, row_spec),
        check_vma=False,
    )
```

profile of v0, /device:TPU:0, one launch (start us, length us, event | category | flops | bytes accessed | tf_op | source)
XLA Modules:
  0.0 1507.3 jit_solution(3387067326716969771)
XLA Ops:
  42.0 152.2 %all-gather.8.cloned.1.call-done = bf16[4,512,3072]{2,1,0:T(8,128)(2,1)} async-done(((bf16[4,256,3072]{2,1,0:T(8,128)(2,1)}), bf16[4,512,3072]{2,1,0:T(8,128)(2,1)}) %all-gather.8.cloned.1.call-update) | async-done | bytes 12582928 | tf_op jit(solution)/shard_map/all_gather | solution.py:41
  236.1 140.7 %all-gather.18.cloned.1.call-done = bf16[4,512,3072]{2,1,0:T(8,128)(2,1)} async-done(((bf16[4,256,3072]{2,1,0:T(8,128)(2,1)}), bf16[4,512,3072]{2,1,0:T(8,128)(2,1)}) %all-gather.18.cloned.1.call-update) | async-done | bytes 12582928 | tf_op jit(solution)/shard_map/all_gather | solution.py:64
  376.8 58.3 %all-gather.16.cloned.1.call-done = bf16[1536,3072]{1,0:T(8,128)(2,1)} async-done(((bf16[1536,384]{1,0:T(8,128)(2,1)}), bf16[1536,3072]{1,0:T(8,128)(2,1)}) %all-gather.16.cloned.1.call-update) | async-done | bytes 9437200 | tf_op jit(solution)/shard_map/all_gather | solution.py:33
  435.1 26.3 %fusion.41 = bf16[4,512,1536]{2,1,0:T(8,128)(2,1)} fusion(bf16[4,512,3072]{2,1,0:T(8,128)(2,1)} %all-gather.18.cloned.1.call-done, bf16[1536,3072]{1,0:T(8,128)(2,1)} %all-gather.16.cloned.1.call-done), kind=kOutput, calls=%fused_computation.58 | convolution fusion | flops 19330498560 | bytes 28311552 | tf_op jit(solution)/shard_map/bsd,ed->bse/dot_general | solution.py:66
  470.0 21.6 %all-gather.14.cloned.1.call-done = bf16[3072,1536]{1,0:T(8,128)(2,1)} async-done(((bf16[384,1536]{1,0:T(8,128)(2,1)}), bf16[3072,1536]{1,0:T(8,128)(2,1)}) %all-gather.14.cloned.1.call-update) | async-done | bytes 9437200 | tf_op jit(solution)/shard_map/all_gather | solution.py:30
  491.6 26.6 %convert_convert_fusion = f32[4,512,1536]{2,1,0:T(8,128)} fusion(bf16[4,512,3072]{2,1,0:T(8,128)(2,1)} %all-gather.8.cloned.1.call-done, bf16[3072,1536]{1,0:T(8,128)(2,1)} %all-gather.14.cloned.1.call-done), kind=kOutput, calls=%fused_computation.57 | convolution fusion | flops 19333644288 | bytes 34603008 | tf_op jit(solution)/shard_map/bsd,de->bse/dot_general | solution.py:49
  576.8 14.7 convolution_convert_fusion
  591.5 28.9 %fusion.76 = (f32[4,4,3,512]{3,2,1,0:T(4,128)S(1)}, f32[4,4,3,512,512]{3,4,2,1,0:T(8,128)}) fusion(pred[512,512]{0,1:T(8,128)(4,1)S(1)} %copy-done.11, bf16[4,512,4,64]{3,1,2,0:T(8,128)(2,1)} %get-tuple-element.16, bf16[4,512,4,64]{3,1,2,0:T(8,128)(2,1)} %get-tuple-element.15, bf16[4,512,4,3,64]{4,1,3,2,0:T(8,128)(2,1)} %get-tuple-element.10, ...), kind=kOutput, calls=%fused_computation.98 | convolution fusion | flops 3288334848 | bytes 59080704 | tf_op jit(solution)/shard_map/sub | solution.py:57
  620.4 52.6 %convert_bitcast_fusion.1 = f32[4,512,4,128]{3,1,2,0:T(8,128)} fusion(bf16[4,4,512,512,3]{3,2,4,1,0:T(8,128)(2,1)} %convolution_convert_fusion, bf16[4,512,4,3,64]{4,1,3,2,0:T(8,128)(2,1)} %get-tuple-element.10, bf16[4,512,4,3,64]{4,1,3,2,0:T(8,128)(2,1)} %get-tuple-element.9, f32[4,4,3,512,512]{3,4,2,1,0:T(8,128)} %get-tuple-element.27, ...), kind=kOutput, calls=%fused_computation.64 | convolution fusion | flops 3349176832 | bytes 86081536 | tf_op jit(solution)/shard_map/bgrqk,bqgrd->bkgd/dot_general | solution.py:72
  673.0 53.9 %convert_bitcast_fusion = f32[4,512,4,3,128]{4,1,3,2,0:T(8,128)} fusion(bf16[4,4,512,512,3]{3,2,4,1,0:T(8,128)(2,1)} %convolution_convert_fusion, bf16[4,512,4,64]{3,1,2,0:T(8,128)(2,1)} %get-tuple-element.16, bf16[4,512,4,64]{3,1,2,0:T(8,128)(2,1)S(1)} %copy-done.7, f32[4,4,3,512,512]{3,4,2,1,0:T(8,128)} %get-tuple-element.27, ...), kind=kOutput, calls=%fused_computation.38 | convolution fusion | flops 3344982528 | bytes 90275840 | tf_op jit(solution)/shard_map/bgrqk,bkgd->bqgrd/dot_general | solution.py:71
  726.9 21.8 %bitcast_convert_fusion = bf16[4,4,128,512]{3,2,1,0:T(8,128)(2,1)} fusion(bf16[4,512,4,3,128]{1,4,3,2,0:T(8,128)(2,1)} %bitcast.160, f32[4,4,3,512,512]{3,4,2,1,0:T(8,128)} %get-tuple-element.27, f32[4,4,3,512]{3,2,1,0:T(4,128)S(1)} %get-tuple-element.26), kind=kOutput, calls=%fused_computation.62 | convolution fusion | flops 3247439872 | bytes 58818560 | tf_op jit(solution)/shard_map/bgrqk,bqgrd->bkgd/dot_general | solution.py:67
  748.7 15.2 %subtract_convert_fusion = (bf16[4,512,4,3,64]{4,1,3,2,0:T(8,128)(2,1)}, bf16[4,512,4,3,64]{4,1,3,2,0:T(8,128)(2,1)}) fusion(f32[4,512,4,3,128]{4,1,3,2,0:T(8,128)} %convert_bitcast_fusion, f32[512,64]{1,0:T(8,128)S(1)} %copy-done.4, f32[512,64]{1,0:T(8,128)S(1)} %copy-done.3), kind=kLoop, calls=%fused_computation.40 | loop fusion | flops 12582912 | bytes 19136512 | tf_op jit(solution)/shard_map/convert.7
  812.9 33.1 %add_convert_fusion = bf16[4,512,3072]{2,1,0:T(8,128)(2,1)} fusion(f32[4,512,3072]{2,1,0:T(8,128)} %fusion.53, f32[4,512,3072]{2,1,0:T(8,128)} %fusion.49, bf16[4,512,1536]{1,2,0:T(8,128)(2,1)} %bitcast.162, bf16[3072,1536]{1,0:T(8,128)(2,1)} %all-gather.14.cloned.1.call-done), kind=kOutput, calls=%fused_computation.11 | convolution fusion | flops 19346227200 | bytes 78643200 | tf_op jit(solution)/shard_map/bse,de->bsd/dot_general | solution.py:77
  847.7 19.9 %fusion.46 = bf16[4,4,128,3,512]{4,2,3,1,0:T(8,128)(2,1)} fusion(bf16[4,512,4,128,1]{1,3,4,2,0:T(8,128)(2,1)S(1)} %bitcast.165, f32[4,4,3,512,512]{3,4,2,1,0:T(8,128)} %get-tuple-element.27, f32[4,4,3,512]{3,2,1,0:T(4,128)S(1)} %get-tuple-element.26), kind=kOutput, calls=%fused_computation.69 | convolution fusion | flops 3249537024 | bytes 58818560 | tf_op jit(solution)/shard_map/bgrqk,bkgd->bqgrd/dot_general | solution.py:59
  867.5 26.1 %fusion.36 = bf16[4,512,3072]{2,1,0:T(8,128)(2,1)} fusion(bf16[4,512,1536]{1,2,0:T(8,128)(2,1)} %bitcast.171, bf16[1536,3072]{1,0:T(8,128)(2,1)} %all-gather.16.cloned.1.call-done), kind=kOutput, calls=%fused_computation.54 | convolution fusion | flops 19333644288 | bytes 28311552 | tf_op jit(solution)/shard_map/bse,ed->bsd/dot_general | solution.py:60
  920.2 26.3 %convolution_bitcast_fusion = f32[1536,3072]{1,0:T(8,128)} fusion(bf16[4,512,1536]{1,2,0:T(8,128)(2,1)} %bitcast.172, bf16[4,512,3072]{2,1,0:T(8,128)(2,1)} %all-gather.18.cloned.1.call-done), kind=kOutput, calls=%fused_computation.28 | convolution fusion | flops 19327352832 | bytes 37748736 | tf_op jit(solution)/shard_map/bse,bsd->ed/dot_general | solution.py:65
  946.5 26.5 %convolution_bitcast_fusion.1 = f32[3072,1536]{1,0:T(8,128)} fusion(bf16[4,512,3072]{2,1,0:T(8,128)(2,1)} %all-gather.8.cloned.1.call-done, bf16[4,512,1536]{1,2,0:T(8,128)(2,1)} %bitcast.163), kind=kOutput, calls=%fused_computation.29 | convolution fusion | flops 19327352832 | bytes 37748736 | tf_op jit(solution)/shard_map/bsd,bse->de/dot_general | solution.py:82
  996.8 23.7 %all-reduce = f32[3072]{0:T(1024)S(1)} all-reduce(f32[3072]{0:T(1024)S(1)} %get-tuple-element.7), channel_id=4, replica_groups=mesh['tp'=2,'dp'=8] {'dp'}, use_global_device_ids=true, to_apply=%region_8.9.clone | all-reduce | flops 3072 | bytes 24576
  1026.2 107.6 %reduce-scatter.7.cloned.1.call-done = bf16[4,256,3072]{2,1,0:T(8,128)(2,1)} async-done(((bf16[4,512,3072]{2,1,0:T(8,128)(2,1)}), bf16[4,256,3072]{2,1,0:T(8,128)(2,1)}) %reduce-scatter.7.cloned.1.call-update) | async-done | bytes 6291472 | tf_op jit(solution)/shard_map/reduce_scatter | solution.py:61
  1133.8 14.8 fusion.19
  1148.6 44.7 %reduce-scatter.13.cloned.1.call-done = f32[384,512]{1,0:T(8,128)} async-done(((f32[3072,512]{1,0:T(8,128)}), f32[384,512]{1,0:T(8,128)}) %reduce-scatter.13.cloned.1.call-update) | async-done | bytes 786448 | tf_op jit(solution)/shard_map/reduce_scatter | solution.py:94
  1193.2 59.3 %reduce-scatter.15.cloned.1.call-done = f32[384,512]{1,0:T(8,128)} async-done(((f32[3072,512]{1,0:T(8,128)}), f32[384,512]{1,0:T(8,128)}) %reduce-scatter.15.cloned.1.call-update) | async-done | bytes 786448 | tf_op jit(solution)/shard_map/reduce_scatter | solution.py:95
  1252.6 124.0 %reduce-scatter.17.cloned.1.call-done = f32[1536,384]{1,0:T(8,128)} async-done(((f32[1536,3072]{1,0:T(8,128)}), f32[1536,384]{1,0:T(8,128)}) %reduce-scatter.17.cloned.1.call-update) | async-done | bytes 2359312 | tf_op jit(solution)/shard_map/reduce_scatter | solution.py:96
  1376.5 123.8 %reduce-scatter.11.cloned.1.call-done = f32[384,1536]{1,0:T(8,128)} async-done(((f32[3072,1536]{1,0:T(8,128)}), f32[384,1536]{1,0:T(8,128)}) %reduce-scatter.11.cloned.1.call-update) | async-done | bytes 2359312 | tf_op jit(solution)/shard_map/reduce_scatter | solution.py:93
  (104 shorter events, 249.6 us)
Async XLA Ops:
  7.2 34.8 %all-gather.12.cloned.1.call-start = ((), (), s32[]{:S(2)}) async-start(), calls=%async_computation.8 | async-start | bytes 3538944 | tf_op jit(solution)/shard_map/all_gather | solution.py:31
  9.2 185.0 %all-gather.8.cloned.1.call-start = ((), (), s32[]{:S(2)}) async-start(), calls=%async_computation.6 | async-start | bytes 18874368 | tf_op jit(solution)/shard_map/all_gather | solution.py:41
  9.2 16.4 %copy-start = (bf16[4,256,3072]{2,1,0:T(8,128)(2,1)S(1)}, bf16[4,256,3072]{2,1,0:T(8,128)(2,1)}, u32[]{:S(2)}) copy-start(bf16[4,256,3072]{2,1,0:T(8,128)(2,1)} %param.7) | copy-start | bytes 18874372
  31.0 194.3 %all-gather.10.cloned.1.call-start = ((), (), s32[]{:S(2)}) async-start(), calls=%async_computation.7 | async-start | bytes 3538944 | tf_op jit(solution)/shard_map/all_gather | solution.py:32
  33.0 343.8 %all-gather.18.cloned.1.call-start = ((), (), s32[]{:S(2)}) async-start(), calls=%async_computation.12 | async-start | bytes 18874368 | tf_op jit(solution)/shard_map/all_gather | solution.py:64
  33.5 401.5 %all-gather.16.cloned.1.call-start = ((), (), s32[]{:S(2)}) async-start(), calls=%async_computation.10 | async-start | bytes 10616832 | tf_op jit(solution)/shard_map/all_gather | solution.py:33
  34.1 457.4 %all-gather.14.cloned.1.call-start = ((), (), s32[]{:S(2)}) async-start(), calls=%async_computation.9 | async-start | bytes 10616832 | tf_op jit(solution)/shard_map/all_gather | solution.py:30
  34.7 954.1 %reduce-scatter.9.cloned.1.call-start = ((), (), s32[]{:S(2)}) async-start(), calls=%async_computation.13 | async-start | bytes 18874368 | tf_op jit(solution)/shard_map/reduce_scatter | solution.py:81
  37.7 524.4 %copy-start.2 = (f32[512,64]{1,0:T(8,128)}, f32[512,64]{1,0:T(8,128)S(1)}, u32[]{:S(2)}) copy-start(f32[512,64]{1,0:T(8,128)S(1)} %get-tuple-element.25) | copy-start | bytes 393220
  236.1 340.7 %copy-start.5 = (bf16[4,512,512]{1,2,0:T(8,128)(2,1)}, bf16[4,512,512]{1,2,0:T(8,128)(2,1)S(1)}, u32[]{:S(2)}) copy-start(bf16[4,512,512]{1,2,0:T(8,128)(2,1)S(1)} %fusion.59) | copy-start | bytes 6291460
  576.8 14.7 copy-start.11
  620.4 52.6 %copy-start.7 = (bf16[4,512,4,64]{3,1,2,0:T(8,128)(2,1)S(1)}, bf16[4,512,4,64]{3,1,2,0:T(8,128)(2,1)}, u32[]{:S(2)}) copy-start(bf16[4,512,4,64]{3,1,2,0:T(8,128)(2,1)} %get-tuple-element.15) | copy-start | bytes 3145732
  726.9 21.8 %copy-start.3 = (f32[512,64]{1,0:T(8,128)S(1)}, f32[512,64]{1,0:T(8,128)}, u32[]{:S(2)}) copy-start(f32[512,64]{1,0:T(8,128)} %copy-done.2) | copy-start | bytes 393220
  726.9 21.8 %copy-start.4 = (f32[512,64]{1,0:T(8,128)S(1)}, f32[512,64]{1,0:T(8,128)}, u32[]{:S(2)}) copy-start(f32[512,64]{1,0:T(8,128)} %get-tuple-element.23) | copy-start | bytes 393220
  748.7 15.2 %copy-start.1 = (f32[4,512,4,128]{3,1,2,0:T(8,128)S(1)}, f32[4,512,4,128]{3,1,2,0:T(8,128)}, u32[]{:S(2)}) copy-start(f32[4,512,4,128]{3,1,2,0:T(8,128)} %convert_bitcast_fusion.1) | copy-start | bytes 12582916
  787.3 13.8 copy-start.8
  787.3 13.8 copy-start.16
  846.1 287.7 %reduce-scatter.7.cloned.1.call-start = ((), (), s32[]{:S(2)}) async-start(), calls=%async_computation.11 | async-start | bytes 18874368 | tf_op jit(solution)/shard_map/reduce_scatter | solution.py:61
  893.6 299.6 %reduce-scatter.13.cloned.1.call-start = ((), (), s32[]{:S(2)}) async-start(), calls=%async_computation.15 | async-start | bytes 7077888 | tf_op jit(solution)/shard_map/reduce_scatter | solution.py:94
  906.7 345.9 %reduce-scatter.15.cloned.1.call-start = ((), (), s32[]{:S(2)}) async-start(), calls=%async_computation.16 | async-start | bytes 7077888 | tf_op jit(solution)/shard_map/reduce_scatter | solution.py:95
  920.1 456.4 %reduce-scatter.17.cloned.1.call-start = ((), (), s32[]{:S(2)}) async-start(), calls=%async_computation.17 | async-start | bytes 21233664 | tf_op jit(solution)/shard_map/reduce_scatter | solution.py:96
  946.5 553.8 %reduce-scatter.11.cloned.1.call-start = ((), (), s32[]{:S(2)}) async-start(), calls=%async_computation.14 | async-start | bytes 21233664 | tf_op jit(solution)/shard_map/reduce_scatter | solution.py:93
  973.1 15.7 %copy-start.13 = (f32[8,1,384]{2,1,0:T(1,128)S(1)}, f32[8,1,384]{2,1,0:T(1,128)}, u32[]{:S(2)}) copy-start(f32[8,1,384]{2,1,0:T(1,128)} %copy-done.12) | copy-start | bytes 36868
  973.1 15.7 %copy-start.15 = (f32[4,256]{1,0:T(4,128)S(1)}, f32[4,256]{1,0:T(4,128)}, u32[]{:S(2)}) copy-start(f32[4,256]{1,0:T(4,128)} %copy-done.14) | copy-start | bytes 12292
  (8 other events, 19.9 us)
Sparse Core Ops, SparseCore 0:
  10.4 31.5 all-gather.11
  44.1 150.0 all-gather.7
  196.6 28.6 all-gather.9
  226.7 150.0 all-gather.17
  378.5 56.5 all-gather.15
  436.8 54.7 all-gather.13
  846.2 142.5 reduce-scatter.8
  991.1 142.6 reduce-scatter.6
  1137.7 55.4 reduce-scatter.12
  1197.0 55.5 reduce-scatter.14
  1256.7 119.7 reduce-scatter.16
  1380.5 119.7 reduce-scatter.10
where the time goes:
time: 1510 us
  waiting for transfers between devices  857 us (57%)
  matrix products  427 us (28%)
  other arithmetic  83.5 us (6%)
  local copies, waits for them, and re-layouts  83.3 us (6%)
  blocking collectives  40.1 us (3%)
  between operations  15.2 us (1%)
    all_gather x1, waiting for transfers between devices, local_block(): lax.all_gather((x_hat * gain_full).astype(jnp.bfloat16), 'tp', axis=1, ti...  152 us
    all_gather x1, waiting for transfers between devices, local_block(): grad_full = lax.all_gather(grad_out, 'tp', axis=1, tiled=True)  141 us
    reduce_scatter x1, waiting for transfers between devices, local_block(): lax.psum_scatter(grad_wo, 'dp', scatter_dimension=1, tiled=True)  124 us
    reduce_scatter x1, waiting for transfers between devices, local_block(): lax.psum_scatter(grad_wq, 'dp', scatter_dimension=0, tiled=True)  124 us
    reduce_scatter x1, waiting for transfers between devices, local_block(): out_loc = lax.psum_scatter(out_part, 'tp', scatter_dimension=1, tiled=True)  108 us
    reduce_scatter x1, waiting for transfers between devices, local_block(): lax.psum_scatter(grad_wv, 'dp', scatter_dimension=0, tiled=True)  59.3 us
    all_gather x1, waiting for transfers between devices, local_block(): wo_full = lax.all_gather(w_out, 'dp', axis=1, tiled=True)  58.3 us
    dot_general x1, matrix products, local_block(): jnp.einsum('bgrqk,bkgd->bqgrd', grad_scores, k_heads, preferred_element_t...  53.9 us
  transfers between devices with their start and end apart: 12, of which 12 were waited for; matrix products, arithmetic and copies ran while one was open for 15% of the time, Pallas kernels for 0%

commit v1 on v0

v1 whole, which is shorter than its diff:
```python
import functools

import jax
import jax.numpy as jnp
from jax import lax
from jax.experimental import pallas as pl
from jax.experimental.pallas import tpu as pltpu
from jax.sharding import PartitionSpec as P


HEAD_DIM = 128
NORM_EPS = 1e-5
ROPE_BASE = 500000.0
SCORE_SCALE = HEAD_DIM ** -0.5
MASK_VALUE = -1e30
F32 = jnp.float32
BF16 = jnp.bfloat16
NT = (((1,), (1,)), ((), ()))
NN = (((1,), (0,)), ((), ()))
TN = (((0,), (0,)), ((), ()))


def rope_tables(seq_len):
    half_dim = HEAD_DIM // 2
    inv_freq = ROPE_BASE ** (-jnp.arange(half_dim, dtype=F32) * 2.0 / HEAD_DIM)
    angles = jnp.arange(seq_len, dtype=F32)[:, None] * inv_freq[None, :]
    cos_t, sin_t = jnp.cos(angles), jnp.sin(angles)
    return jnp.concatenate([cos_t, cos_t], axis=1), jnp.concatenate([-sin_t, sin_t], axis=1)


def dot(lhs, rhs, dims):
    return lax.dot_general(lhs, rhs, dims, preferred_element_type=F32)


def turn(values, cos_t, sin_t):
    return values * cos_t + pltpu.roll(values, HEAD_DIM // 2, 1) * sin_t


def pick_halves(first, own, rec):
    own, rec = own.astype(F32), rec.astype(F32)
    return jnp.where(first, own, rec), jnp.where(first, rec, own)


def heads_of(group_size, block, cos_t, sin_t):
    cut = [block[:, i * HEAD_DIM:(i + 1) * HEAD_DIM] for i in range(group_size + 2)]
    queries = jnp.concatenate([turn(cut[i], cos_t, sin_t).astype(BF16) for i in range(group_size)], axis=0)
    return queries, turn(cut[group_size], cos_t, sin_t).astype(BF16), cut[group_size + 1].astype(BF16)


def store_halves(first, own_ref, rec_ref, columns, lower, upper):
    own_ref[0, :, columns] = jnp.where(first, lower, upper).astype(own_ref.dtype)
    rec_ref[0, :, columns] = jnp.where(first, upper, lower).astype(rec_ref.dtype)


def attention_fwd_kernel(group_size, tp_ref, own_ref, rec_ref, cos_ref, sin_ref, out_own_ref, out_rec_ref):
    half = own_ref.shape[1]
    first = tp_ref[0] == 0
    lower, upper = pick_halves(first, own_ref[0], rec_ref[0])
    q_lo, k_lo, v_lo = heads_of(group_size, lower, cos_ref[:half], sin_ref[:half])
    q_up, k_up, v_up = heads_of(group_size, upper, cos_ref[half:], sin_ref[half:])
    rows = lax.broadcasted_iota(jnp.int32, (group_size, half, half), 1).reshape(group_size * half, half)
    cols = lax.broadcasted_iota(jnp.int32, (group_size * half, half), 1)
    causal = rows >= cols

    s_lo = jnp.where(causal, dot(q_lo, k_lo, NT), MASK_VALUE)
    p_lo = jnp.exp((s_lo - jnp.max(s_lo, axis=1, keepdims=True)) * SCORE_SCALE)
    p_lo = (p_lo * (1.0 / jnp.sum(p_lo, axis=1, keepdims=True))).astype(BF16)
    a_lo = dot(p_lo, v_lo, NN)

    s_a = dot(q_up, k_lo, NT)
    s_b = jnp.where(causal, dot(q_up, k_up, NT), MASK_VALUE)
    top = jnp.maximum(jnp.max(s_a, axis=1, keepdims=True), jnp.max(s_b, axis=1, keepdims=True))
    p_a = jnp.exp((s_a - top) * SCORE_SCALE)
    p_b = jnp.exp((s_b - top) * SCORE_SCALE)
    inv = 1.0 / (jnp.sum(p_a, axis=1, keepdims=True) + jnp.sum(p_b, axis=1, keepdims=True))
    a_up = dot((p_a * inv).astype(BF16), v_lo, NN) + dot((p_b * inv).astype(BF16), v_up, NN)
    for i in range(group_size):
        part = slice(i * half, (i + 1) * half)
        store_halves(first, out_own_ref, out_rec_ref, slice(i * HEAD_DIM, (i + 1) * HEAD_DIM), a_lo[part], a_up[part])


def attention_bwd_kernel(group_size, tp_ref, own_ref, rec_ref, cos_ref, sin_ref, ga_own_ref, ga_rec_ref, *rest):
    out_own_ref, out_rec_ref = rest[-2:]
    half = own_ref.shape[1]
    first = tp_ref[0] == 0
    lower, upper = pick_halves(first, own_ref[0], rec_ref[0])
    cos_lo, sin_lo, cos_up, sin_up = cos_ref[:half], sin_ref[:half], cos_ref[half:], sin_ref[half:]
    q_lo, k_lo, v_lo = heads_of(group_size, lower, cos_lo, sin_lo)
    q_up, k_up, v_up = heads_of(group_size, upper, cos_up, sin_up)
    ga_lower, ga_upper = pick_halves(first, ga_own_ref[0], ga_rec_ref[0])

    def stacked(block):
        return jnp.concatenate([block[:, i * HEAD_DIM:(i + 1) * HEAD_DIM].astype(BF16) for i in range(group_size)], axis=0)

    ga_lo, ga_up = stacked(ga_lower), stacked(ga_upper)
    keys = lax.broadcasted_iota(jnp.int32, (half, half), 0)
    spots = lax.broadcasted_iota(jnp.int32, (half, half), 1)
    causal = jnp.concatenate([spots >= keys] * group_size, axis=1)

    s_lo = jnp.where(causal, dot(k_lo, q_lo, NT), MASK_VALUE)
    p_lo = jnp.exp((s_lo - jnp.max(s_lo, axis=0, keepdims=True)) * SCORE_SCALE)
    p_lo = p_lo * (1.0 / jnp.sum(p_lo, axis=0, keepdims=True))
    gp_lo = dot(v_lo, ga_lo, NT).astype(BF16).astype(F32)
    gs_lo = (p_lo * (gp_lo - jnp.sum(gp_lo * p_lo, axis=0, keepdims=True)) * SCORE_SCALE).astype(BF16)

    s_a = dot(k_lo, q_up, NT)
    s_b = jnp.where(causal, dot(k_up, q_up, NT), MASK_VALUE)
    top = jnp.maximum(jnp.max(s_a, axis=0, keepdims=True), jnp.max(s_b, axis=0, keepdims=True))
    p_a = jnp.exp((s_a - top) * SCORE_SCALE)
    p_b = jnp.exp((s_b - top) * SCORE_SCALE)
    inv = 1.0 / (jnp.sum(p_a, axis=0, keepdims=True) + jnp.sum(p_b, axis=0, keepdims=True))
    p_a = p_a * inv
    p_b = p_b * inv
    gp_a = dot(v_lo, ga_up, NT).astype(BF16).astype(F32)
    gp_b = dot(v_up, ga_up, NT).astype(BF16).astype(F32)
    mean_up = jnp.sum(gp_a * p_a, axis=0, keepdims=True) + jnp.sum(gp_b * p_b, axis=0, keepdims=True)
    gs_a = (p_a * (gp_a - mean_up) * SCORE_SCALE).astype(BF16)
    gs_b = (p_b * (gp_b - mean_up) * SCORE_SCALE).astype(BF16)

    gv_lo = dot(p_lo.astype(BF16), ga_lo, NN) + dot(p_a.astype(BF16), ga_up, NN)
    gv_up = dot(p_b.astype(BF16), ga_up, NN)
    gk_lo = (dot(gs_lo, q_lo, NN) + dot(gs_a, q_up, NN)).astype(BF16).astype(F32)
    gk_up = dot(gs_b, q_up, NN).astype(BF16).astype(F32)
    gq_lo = dot(gs_lo, k_lo, TN).astype(BF16).astype(F32)
    gq_up = (dot(gs_a, k_lo, TN) + dot(gs_b, k_up, TN)).astype(BF16).astype(F32)

    def store(index, lower_part, upper_part):
        store_halves(first, out_own_ref, out_rec_ref, slice(index * HEAD_DIM, (index + 1) * HEAD_DIM), lower_part, upper_part)

    for i in range(group_size):
        part = slice(i * half, (i + 1) * half)
        store(i, turn(gq_lo[part], cos_lo, -sin_lo), turn(gq_up[part], cos_up, -sin_up))
    store(group_size, turn(gk_lo, cos_lo, -sin_lo), turn(gk_up, cos_up, -sin_up))
    store(group_size + 1, gv_lo, gv_up)


def cost(flops, transcendentals, *arrays):
    return pl.CostEstimate(flops=int(flops), transcendentals=int(transcendentals), bytes_accessed=int(sum(a.size * a.dtype.itemsize for a in arrays)))


def attention_fwd(tp_index, qkv_own, qkv_rec, tables, groups, group_size):
    batch, half, width = qkv_own.shape
    block = width // groups
    out_block = group_size * HEAD_DIM
    shape = jax.ShapeDtypeStruct((batch, half, groups * out_block), BF16)
    spec = lambda columns: pl.BlockSpec((1, half, columns), lambda b, g, tp: (b, 0, g))
    table = pl.BlockSpec((2 * half, HEAD_DIM), lambda b, g, tp: (0, 0))
    return pl.pallas_call(
        functools.partial(attention_fwd_kernel, group_size),
        out_shape=(shape, shape),
        grid_spec=pltpu.PrefetchScalarGridSpec(
            num_scalar_prefetch=1,
            grid=(batch, groups),
            in_specs=[spec(block), spec(block), table, table],
            out_specs=(spec(out_block), spec(out_block)),
        ),
        compiler_params=pltpu.CompilerParams(vmem_limit_bytes=48 * 2**20),
        cost_estimate=cost(batch * groups * group_size * half * half * HEAD_DIM * 12, batch * groups * group_size * half * half * 3, qkv_own, qkv_rec, shape, shape),
        name="attention_fwd",
    )(tp_index, qkv_own, qkv_rec, *tables)


def attention_bwd(tp_index, qkv_own, qkv_rec, tables, ga_own, ga_rec, start, held, groups, group_size):
    batch, half, width = qkv_own.shape
    count = ga_rec.shape[0]
    block = width // groups
    ga_block = group_size * HEAD_DIM
    shape = jax.ShapeDtypeStruct((batch, half, width), BF16)
    spec = lambda columns, offset: pl.BlockSpec((1, half, columns), lambda b, g, tp: (b + offset, 0, g))
    table = pl.BlockSpec((2 * half, HEAD_DIM), lambda b, g, tp: (0, 0))
    in_specs = [spec(block, start), spec(block, start), table, table, spec(ga_block, start), spec(ga_block, 0)]
    args = [tp_index, qkv_own, qkv_rec, *tables, ga_own, ga_rec]
    aliases = {}
    if held is not None:
        in_specs += [pl.BlockSpec(memory_space=pl.ANY)] * 2
        aliases = {len(args): 0, len(args) + 1: 1}
        args += list(held)
    work = count * groups * group_size * half * half
    return pl.pallas_call(
        functools.partial(attention_bwd_kernel, group_size),
        out_shape=(shape, shape),
        grid_spec=pltpu.PrefetchScalarGridSpec(
            num_scalar_prefetch=1,
            grid=(count, groups),
            in_specs=in_specs,
            out_specs=(spec(block, start), spec(block, start)),
        ),
        input_output_aliases=aliases,
        compiler_params=pltpu.CompilerParams(vmem_limit_bytes=48 * 2**20),
        cost_estimate=cost(work * HEAD_DIM * 30, work * 3, ga_rec, ga_rec, ga_rec, ga_rec),
        name="attention_bwd",
    )(*args)


def finish_out_kernel(x_ref, near_ref, far_ref, *rest):
    out_sum = (near_ref[0].astype(F32) + far_ref[0].astype(F32)).astype(BF16).astype(F32)
    rest[-1][0] = (x_ref[0].astype(F32) + out_sum).astype(BF16)


def finish_grad_kernel(x_ref, dy_ref, near_ref, gain_ref, far_ref, *rest):
    out_ref, gain_out_ref = rest[-2:]
    values = x_ref[0].astype(F32)
    inv_rms = lax.rsqrt(jnp.mean(values * values, axis=-1, keepdims=True) + NORM_EPS)
    x_hat = values * inv_rms
    grad_normed = (near_ref[0].astype(F32) + far_ref[0].astype(F32)).astype(BF16).astype(F32)
    scaled = grad_normed * gain_ref[...]
    mean = jnp.mean(scaled * x_hat, axis=-1, keepdims=True)
    out_ref[0] = (dy_ref[0].astype(F32) + inv_rms * (scaled - x_hat * mean)).astype(BF16)

    @pl.when((pl.program_id(0) == 0) & (pl.program_id(1) == 0))
    def _():
        gain_out_ref[...] = jnp.zeros_like(gain_out_ref)

    gain_out_ref[...] += jnp.sum((grad_normed * x_hat).reshape(-1, 8, x_hat.shape[-1]), axis=0)


def finish(kernel, full, chunk, start, held, gain=None, row_block=64):
    batch, half, width = full[0].shape
    count = chunk[0].shape[0]
    row_block = min(row_block, half)
    spec = lambda offset: pl.BlockSpec((1, row_block, width), lambda b, r: (b + offset, r, 0))
    in_specs = [spec(start)] * len(full)
    args = list(full)
    out_shape = [jax.ShapeDtypeStruct((batch, half, width), BF16)]
    out_specs = [spec(start)]
    if gain is not None:
        in_specs.append(pl.BlockSpec((1, width), lambda b, r: (0, 0)))
        args.append(gain.reshape(1, width))
        out_shape.append(jax.ShapeDtypeStruct((8, width), F32))
        out_specs.append(pl.BlockSpec((8, width), lambda b, r: (0, 0)))
    in_specs += [spec(0)] * len(chunk)
    args += list(chunk)
    aliases = {}
    if held is not None:
        aliases = {len(args): 0}
        in_specs.append(pl.BlockSpec(memory_space=pl.ANY))
        args.append(held)
    result = pl.pallas_call(
        kernel,
        out_shape=out_shape,
        grid=(count, half // row_block),
        in_specs=in_specs,
        out_specs=out_specs,
        input_output_aliases=aliases,
        compiler_params=pltpu.CompilerParams(vmem_limit_bytes=32 * 2**20),
        cost_estimate=cost(count * half * width * 400, 0, *([chunk[0]] * (len(full) + len(chunk) + 1))),
    )(*args)
    return result if gain is not None else result[0]


DY_CHUNKS = 2
OUT_CHUNKS = 2
DN_CHUNKS = 4


def after(value, *others):
    return lax.optimization_barrier((value, *others))[0]


def solution(mesh):
    swap = [(0, 1), (1, 0)]

    def exchange(values):
        return lax.ppermute(values, "tp", swap)

    def mm(eq, a, b):
        return jnp.einsum(eq, a, b, preferred_element_type=F32)

    def local_block(hidden, norm_gain, w_query, w_key, w_value, w_out, grad_out):
        batch, half, _ = hidden.shape
        rows_loc = w_query.shape[0]
        groups = w_key.shape[1] // HEAD_DIM
        group_size = w_query.shape[1] // w_key.shape[1]
        block = (group_size + 2) * HEAD_DIM
        tp_index = lax.axis_index("tp").astype(jnp.int32).reshape(1)
        tables = rope_tables(2 * half)

        hidden_rec = exchange(hidden)
        step = batch // DY_CHUNKS
        grad_rec = []
        for i in range(DY_CHUNKS):
            grad_rec.append(exchange(grad_out[i * step:(i + 1) * step]))

        w_qkv = jnp.concatenate(
            [w_query.reshape(rows_loc, groups, -1), w_key.reshape(rows_loc, groups, -1), w_value.reshape(rows_loc, groups, -1)], axis=2
        ).reshape(rows_loc, groups * block)
        w_qkv = lax.all_gather(w_qkv, "dp", axis=0, tiled=True)
        w_o = lax.all_gather(w_out, "dp", axis=1, tiled=True)
        gain = lax.all_gather(norm_gain, "dp", axis=0, tiled=True).astype(F32)

        def norm(values):
            values = values.astype(F32)
            inv_rms = lax.rsqrt(jnp.mean(values * values, axis=-1, keepdims=True) + NORM_EPS)
            return (values * inv_rms * gain).astype(BF16)

        normed_own = norm(hidden)
        qkv_own = mm("bsd,de->bse", normed_own, w_qkv).astype(BF16)
        normed_rec = norm(after(hidden_rec, qkv_own))
        qkv_rec = mm("bsd,de->bse", normed_rec, w_qkv).astype(BF16)
        attn_own, attn_rec = attention_fwd(tp_index, qkv_own, qkv_rec, tables, groups, group_size)

        step = batch // OUT_CHUNKS
        out_send = []
        for i in range(OUT_CHUNKS):
            out_send.append(mm("bse,ed->bsd", attn_rec[i * step:(i + 1) * step], w_o).astype(BF16))
        out_far = []
        for i in range(OUT_CHUNKS):
            out_far.append(exchange(out_send[i]))

        ga_own = mm("bsd,ed->bse", after(grad_out, *out_send), w_o).astype(BF16)
        held = None
        step = batch // DY_CHUNKS
        for i in range(DY_CHUNKS):
            if i == DY_CHUNKS - 1:
                grad_wo = mm("bse,bsd->ed", attn_own, after(grad_out, *held)) + mm("bse,bsd->ed", attn_rec, jnp.concatenate(grad_rec, axis=0))
                ga_rec = mm("bsd,ed->bse", after(grad_rec[i], grad_wo), w_o).astype(BF16)
            else:
                ga_rec = mm("bsd,ed->bse", after(grad_rec[i], ga_own), w_o).astype(BF16)
            held = attention_bwd(tp_index, qkv_own, qkv_rec, tables, ga_own, ga_rec, i * step, held, groups, group_size)
        gqkv_own, gqkv_rec = held

        grad_wo = lax.psum_scatter(grad_wo, "dp", scatter_dimension=1, tiled=True)
        grad_wqkv = mm("bsd,bse->de", normed_own, gqkv_own) + mm("bsd,bse->de", normed_rec, gqkv_rec)
        gqkv_own, gqkv_rec = after((gqkv_own, gqkv_rec), grad_wqkv)
        grad_wqkv = lax.psum_scatter(grad_wqkv, "dp", scatter_dimension=0, tiled=True)

        step = batch // DN_CHUNKS
        dn_send = []
        for i in range(DN_CHUNKS):
            dn_send.append(mm("bse,de->bsd", gqkv_rec[i * step:(i + 1) * step], w_qkv).astype(BF16))
        dn_far = []
        for i in range(DN_CHUNKS):
            dn_far.append(exchange(dn_send[i]))

        attn_own, gqkv_own = after((attn_own, gqkv_own), *dn_send)
        out_near = lax.optimization_barrier(mm("bse,ed->bsd", attn_own, w_o).astype(BF16))
        dn_near = lax.optimization_barrier(mm("bse,de->bsd", gqkv_own, w_qkv).astype(BF16))
        hidden_out = None
        step = batch // OUT_CHUNKS
        for i in range(OUT_CHUNKS):
            hidden_out = finish(finish_out_kernel, [hidden, out_near], [out_far[i]], i * step, hidden_out)
        dn_near = after(dn_near, hidden_out)
        grad_hidden = None
        gain_parts = []
        step = batch // DN_CHUNKS
        for i in range(DN_CHUNKS):
            grad_hidden, part = finish(
                finish_grad_kernel, [hidden, grad_out, dn_near], [dn_far[i]], i * step, grad_hidden, gain
            )
            gain_parts.append(part)
        gain_sum = lax.psum(jnp.sum(sum(gain_parts), axis=0), ("dp", "tp"))
        grad_gain = lax.dynamic_slice(gain_sum, (lax.axis_index("dp") * rows_loc,), (rows_loc,))

        grad_wqkv = grad_wqkv.reshape(rows_loc, groups, block)
        split = group_size * HEAD_DIM
        grad_wq = grad_wqkv[:, :, :split].reshape(rows_loc, -1)
        grad_wk = grad_wqkv[:, :, split:split + HEAD_DIM].reshape(rows_loc, -1)
        grad_wv = grad_wqkv[:, :, split + HEAD_DIM:].reshape(rows_loc, -1)
        return hidden_out, grad_hidden, grad_gain, grad_wq, grad_wk, grad_wv, grad_wo

    act_spec = P("dp", "tp", None)
    col_spec = P("dp", "tp")
    row_spec = P("tp", "dp")
    return jax.shard_map(
        local_block,
        mesh=mesh,
        in_specs=(act_spec, P("dp"), col_spec, col_spec, col_spec, row_spec, act_spec),
        out_specs=(act_spec, act_spec, P("dp"), col_spec, col_spec, col_spec, row_spec),
        check_vma=False,
    )
```

time: 1510 us -> 739 us (0.49)
  waiting for transfers between devices: 857 us -> 236 us
  matrix products: 427 us -> 275 us
  Pallas kernels: 0 us -> 114 us
  other arithmetic: 83.5 us -> 10.6 us
  local copies, waits for them, and re-layouts: 83.3 us -> 28.6 us
    reduce_scatter x6 -> x2, waiting for transfers between devices: 473 us -> 0.01 us  [the longest x1 0.01 us: local_block(): lax.psum_scatter(grad_wqkv, 'dp', scatter_dimension=0, tiled=True)]
    all_gather x6 -> x2, waiting for transfers between devices: 382 us -> 57.2 us  [the longest x1 57.2 us: local_block(): w_qkv = lax.all_gather(w_qkv, 'dp', axis=0, tiled=True)]
    ppermute x0 -> x9, waiting for transfers between devices: none -> 178 us  [exchange(): return lax.ppermute(values, 'tp', swap)]
    dot_general x17, matrix products: 398 us -> 275 us  [mm(): return jnp.einsum(eq, a, b, preferred_element_type=F32)]
    pallas_call x0 -> x9, Pallas kernels: none -> 114 us  [the longest x2 51.6 us: attention_bwd(): pl.pallas_call(functools.partial(attention_bwd_kernel, group_size), out_s...]
    another operation x4 -> x0, other arithmetic: 38 us -> none
    sub x1 -> x0, matrix products: 28.9 us -> none  [local_block(): attn_prob = jax.nn.softmax(jnp.where(causal, scores, MASK_VALUE), axis=-1)]
    psum x1, blocking collectives: 5.57 us -> 33.8 us  [local_block(): gain_sum = lax.psum(jnp.sum(sum(gain_parts), axis=0), ('dp', 'tp'))]
  transfers between devices with their start and end apart: 12 -> 13, of which waited for: 12 -> 7; matrix products, arithmetic and copies ran while one was open for 15% -> 29% of each run, Pallas kernels for 0% -> 12%
where the time goes in v1:
time: 739 us; the launch traced here: 734 us
  matrix products  275 us (37%)
  waiting for transfers between devices  236 us (32%)
  Pallas kernels  114 us (15%)
  blocking collectives  43.1 us (6%)
  local copies, waits for them, and re-layouts  28.6 us (4%)
  between operations  14.2 us (2%)
  starting transfers between devices  12.1 us (2%)
  other arithmetic  10.6 us (1%)
    dot_general x17, matrix products, mm(): return jnp.einsum(eq, a, b, preferred_element_type=F32)  275 us
    ppermute x9, waiting for transfers between devices, exchange(): return lax.ppermute(values, 'tp', swap)  178 us
    all_gather x1, waiting for transfers between devices, local_block(): w_qkv = lax.all_gather(w_qkv, 'dp', axis=0, tiled=True)  57.2 us
    pallas_call x2, Pallas kernels, attention_bwd(): pl.pallas_call(functools.partial(attention_bwd_kernel, group_size), out_s...  51.6 us
    psum x1, blocking collectives, local_block(): gain_sum = lax.psum(jnp.sum(sum(gain_parts), axis=0), ('dp', 'tp'))  33.8 us
    pallas_call x1, Pallas kernels, attention_fwd(): pl.pallas_call(functools.partial(attention_fwd_kernel, group_size), out_s...  31.7 us
    pallas_call x6, Pallas kernels, finish(): pl.pallas_call(kernel, out_shape=out_shape, grid=(count, half // row_bloc...  30.7 us
  transfers between devices with their start and end apart: 13, of which 7 were waited for; matrix products, arithmetic and copies ran while one was open for 29% of the time, Pallas kernels for 12%

profile of v1, /device:TPU:0, one launch (start us, length us, event | category | flops | bytes accessed | tf_op | source)
XLA Modules:
  0.0 733.7 jit_solution(15361979744579735573)
XLA Ops:
  41.9 57.2 %all-gather.4.cloned.1.call-done = bf16[3072,2560]{1,0:T(8,128)(2,1)} async-done(((bf16[384,2560]{1,0:T(8,128)(2,1)}), bf16[3072,2560]{1,0:T(8,128)(2,1)}) %all-gather.4.cloned.1.call-update) | async-done | bytes 15728656 | tf_op jit(solution)/shard_map/all_gather | solution.py:287
  99.2 23.3 %fusion.33.own_ref = bf16[4,256,2560]{2,1,0:T(8,128)(2,1)} fusion(bf16[3072,2560]{1,0:T(8,128)(2,1)} %all-gather.4.cloned.1.call-done, bf16[4,256,3072]{2,1,0:T(8,128)(2,1)} %x_ref.11, f32[3072]{0:T(1024)S(1)} %bitcast.103, f32[4,256]{1,0:T(4,128)S(1)} %add_rsqrt_fusion.1), kind=kOutput, calls=%fused_computation.35 | convolution fusion | flops 16121331712 | bytes 27279360 | tf_op jit(solution)/shard_map/bsd,de->bse/dot_general | solution.py:267
  122.5 32.9 %collective-permute-done = bf16[4,256,3072]{2,1,0:T(8,128)(2,1)} collective-permute-done((bf16[4,256,3072]{2,1,0:T(8,128)(2,1)}, bf16[4,256,3072]{2,1,0:T(8,128)(2,1)}, u32[]{:S(2)}, u32[]{:S(2)}) %collective-permute-start) | collective-permute-done | bytes 6291488 | tf_op jit(solution)/shard_map/ppermute | solution.py:264
  159.5 23.2 %fusion.36.rec_ref = bf16[4,256,2560]{2,1,0:T(8,128)(2,1)} fusion(bf16[3072,2560]{1,0:T(8,128)(2,1)} %all-gather.4.cloned.1.call-done, bf16[4,256,3072]{2,1,0:T(8,128)(2,1)} %collective-permute-done, f32[4,256]{1,0:T(4,128)S(1)} %add_rsqrt_fusion, f32[3072]{0:T(1024)S(1)} %bitcast.104), kind=kOutput, calls=%fused_computation.36 | convolution fusion | flops 16121331712 | bytes 27279360 | tf_op jit(solution)/shard_map/bsd,de->bse/dot_general | solution.py:267
  182.7 31.7 %attention_fwd.1 = (bf16[4,256,1536]{2,1,0:T(8,128)(2,1)S(1)}, bf16[4,256,1536]{2,1,0:T(8,128)(2,1)}) custom-call(s32[1]{0:T(128)} %bitcast.tp_ref, bf16[4,256,2560]{2,1,0:T(8,128)(2,1)} %fusion.33.own_ref, bf16[4,256,2560]{2,1,0:T(8,128)(2,1)} %fusion.36.rec_ref, f32[512,128]{1,0:T(8,128)S(1)} %get-tuple-element.62.cos_ref, ...), custom_call_target="tpu_custom_call" | custom-call | flops 4831838208 | bytes 16777216 | tf_op jit(solution)/shard_map/attention_fwd/pallas_call | solution.py:148
  232.1 10.2 %fusion.50.ga_own_ref = bf16[4,256,1536]{2,1,0:T(8,128)(2,1)S(1)} fusion(bf16[4,256,3072]{2,1,0:T(8,128)(2,1)S(1)} %bitcast.100, bf16[1536,3072]{1,0:T(8,128)(2,1)S(1)} %copy-done.8), kind=kOutput, calls=%fused_computation.44 | convolution fusion | flops 9665249280 | bytes 18874368 | tf_op jit(solution)/shard_map/bsd,ed->bse/dot_general | solution.py:267
  251.9 26.1 %attention_bwd.2 = (bf16[4,256,2560]{2,1,0:T(8,128)(2,1)}, bf16[4,256,2560]{2,1,0:T(8,128)(2,1)}) custom-call(s32[1]{0:T(128)} %bitcast.tp_ref, bf16[4,256,2560]{2,1,0:T(8,128)(2,1)} %fusion.33.own_ref, bf16[4,256,2560]{2,1,0:T(8,128)(2,1)} %fusion.36.rec_ref, f32[512,128]{1,0:T(8,128)S(1)} %get-tuple-element.62.cos_ref, f32[512,128]{1,0:T(8,128)S(1)} %copy-done.2, ...), custom_call_target="tpu_custom_call" | custom-call | flops 6039797760 | bytes 6291456 | tf_op jit(solution)/shard_map/attention_bwd/pallas_call | solution.py:179
  278.1 13.3 %fusion.77 = f32[1536,3072,1]{1,0,2:T(8,128)} fusion(bf16[4,256,1536]{2,1,0:T(8,128)(2,1)S(1)} %copy-done.5, bf16[4,256,3072]{2,1,0:T(8,128)(2,1)S(1)} %bitcast.100), kind=kOutput, calls=%fused_computation.75 | convolution fusion | flops 9663676416 | bytes 28311552 | tf_op jit(solution)/shard_map/bse,bsd->ed/dot_general | solution.py:267
  291.3 19.8 %bitcast_add_fusion.1 = f32[1536,3072]{1,0:T(8,128)} fusion(f32[1536,3072,1]{1,0,2:T(8,128)} %fusion.77, bf16[4,256,1536]{2,1,0:T(8,128)(2,1)} %get-tuple-element.33, bf16[2,256,3072]{2,1,0:T(8,128)(2,1)} %collective-permute-done.1, bf16[2,256,3072]{2,1,0:T(8,128)(2,1)} %collective-permute-done.2), kind=kOutput, calls=%fused_computation.1 | convolution fusion | flops 9671540736 | bytes 47185920 | tf_op jit(solution)/shard_map/bse,bsd->ed/dot_general | solution.py:267
  320.8 25.5 %attention_bwd.3 = (bf16[4,256,2560]{2,1,0:T(8,128)(2,1)}, bf16[4,256,2560]{2,1,0:T(8,128)(2,1)}) custom-call(s32[1]{0:T(128)} %bitcast.tp_ref, bf16[4,256,2560]{2,1,0:T(8,128)(2,1)} %fusion.33.own_ref, bf16[4,256,2560]{2,1,0:T(8,128)(2,1)} %fusion.36.rec_ref, ...), custom_call_target="tpu_custom_call", output_to_operand_aliasing={{0}: (7, {}), {1}: (8, {})} | custom-call | flops 6039797760 | bytes 6291456 | tf_op jit(solution)/shard_map/attention_bwd/pallas_call | solution.py:179
  346.3 24.5 %fusion.41 = f32[3072,2560,1]{1,0,2:T(8,128)} fusion(bf16[4,256,2560]{2,1,0:T(8,128)(2,1)} %get-tuple-element.45, bf16[4,256,3072]{2,1,0:T(8,128)(2,1)} %x_ref.11, f32[3072]{0:T(1024)S(1)} %bitcast.105, f32[4,256]{1,0:T(4,128)S(1)} %add_rsqrt_fusion.1), kind=kOutput, calls=%fused_computation.37 | convolution fusion | flops 16118710272 | bytes 43008000 | tf_op jit(solution)/shard_map/bsd,bse->de/dot_general | solution.py:267
  370.8 33.9 %bitcast_add_fusion = f32[3072,2560]{1,0:T(8,128)} fusion(f32[3072,2560,1]{1,0,2:T(8,128)} %fusion.41, bf16[4,256,2560]{2,1,0:T(8,128)(2,1)} %get-tuple-element.43, bf16[4,256,3072]{2,1,0:T(8,128)(2,1)} %collective-permute-done, f32[4,256]{1,0:T(4,128)S(1)} %add_rsqrt_fusion, f32[3072]{0:T(1024)S(1)} %bitcast.106), kind=kOutput, calls=%fused_computation | convolution fusion | flops 16126574592 | bytes 74465280 | tf_op jit(solution)/shard_map/bsd,bse->de/dot_general | solution.py:267
  407.4 13.2 %fusion.53 = bf16[1,256,3072]{2,1,0:T(8,128)(2,1)} fusion(bf16[3072,2560]{1,0:T(8,128)(2,1)} %all-gather.4.cloned.1.call-done, bf16[4,256,2560]{2,1,0:T(8,128)(2,1)} %get-tuple-element.43), kind=kOutput, calls=%fused_computation.45 | convolution fusion | flops 4027318272 | bytes 18612224 | tf_op jit(solution)/shard_map/bse,de->bsd/dot_general | solution.py:267
  422.7 14.8 %fusion.54 = bf16[1,256,3072]{2,1,0:T(8,128)(2,1)} fusion(bf16[3072,2560]{1,0:T(8,128)(2,1)} %all-gather.4.cloned.1.call-done, bf16[4,256,2560]{2,1,0:T(8,128)(2,1)} %get-tuple-element.43), kind=kOutput, calls=%fused_computation.46 | convolution fusion | flops 4027318272 | bytes 18612224 | tf_op jit(solution)/shard_map/bse,de->bsd/dot_general | solution.py:267
  437.5 14.5 %fusion.55 = bf16[1,256,3072]{2,1,0:T(8,128)(2,1)} fusion(bf16[3072,2560]{1,0:T(8,128)(2,1)} %all-gather.4.cloned.1.call-done, bf16[4,256,2560]{2,1,0:T(8,128)(2,1)} %get-tuple-element.43), kind=kOutput, calls=%fused_computation.47 | convolution fusion | flops 4027318272 | bytes 18612224 | tf_op jit(solution)/shard_map/bse,de->bsd/dot_general | solution.py:267
  453.9 12.3 %fusion.56 = bf16[1,256,3072]{2,1,0:T(8,128)(2,1)} fusion(bf16[3072,2560]{1,0:T(8,128)(2,1)} %all-gather.4.cloned.1.call-done, bf16[4,256,2560]{2,1,0:T(8,128)(2,1)} %get-tuple-element.43), kind=kOutput, calls=%fused_computation.48 | convolution fusion | flops 4027318272 | bytes 18612224 | tf_op jit(solution)/shard_map/bse,de->bsd/dot_general | solution.py:267
  466.2 15.7 %fusion.27.near_ref = bf16[4,256,3072]{2,1,0:T(8,128)(2,1)} fusion(bf16[4,256,1536]{2,1,0:T(8,128)(2,1)} %copy-done.4, bf16[1536,3072]{1,0:T(8,128)(2,1)} %all-gather.6.cloned.1.call-done), kind=kOutput, calls=%fused_computation.33 | convolution fusion | flops 9666822144 | bytes 18874368 | tf_op jit(solution)/shard_map/bse,ed->bsd/dot_general | solution.py:267
  482.0 21.3 %fusion.30.near_ref = bf16[4,256,3072]{2,1,0:T(8,128)(2,1)S(1)} fusion(bf16[4,256,2560]{2,1,0:T(8,128)(2,1)} %get-tuple-element.45, bf16[3072,2560]{1,0:T(8,128)(2,1)} %all-gather.4.cloned.1.call-done), kind=kOutput, calls=%fused_computation.34 | convolution fusion | flops 16109273088 | bytes 27262976 | tf_op jit(solution)/shard_map/bse,de->bsd/dot_general | solution.py:267
  510.0 34.0 %collective-permute-done.3.far_ref = bf16[2,256,3072]{2,1,0:T(8,128)(2,1)} collective-permute-done((bf16[2,256,3072]{2,1,0:T(8,128)(2,1)}, bf16[2,256,3072]{2,1,0:T(8,128)(2,1)}, u32[]{:S(2)}, u32[]{:S(2)}) %collective-permute-start.3) | collective-permute-done | bytes 3145760 | tf_op jit(solution)/shard_map/ppermute | solution.py:264
  550.8 26.9 %collective-permute-done.8.far_ref = bf16[1,256,3072]{2,1,0:T(8,128)(2,1)} collective-permute-done((bf16[1,256,3072]{2,1,0:T(8,128)(2,1)}, bf16[1,256,3072]{2,1,0:T(8,128)(2,1)}, u32[]{:S(2)}, u32[]{:S(2)}) %collective-permute-start.8) | collective-permute-done | bytes 1572896 | tf_op jit(solution)/shard_map/ppermute | solution.py:264
  582.7 28.7 %collective-permute-done.7.far_ref = bf16[1,256,3072]{2,1,0:T(8,128)(2,1)} collective-permute-done((bf16[1,256,3072]{2,1,0:T(8,128)(2,1)}, bf16[1,256,3072]{2,1,0:T(8,128)(2,1)}, u32[]{:S(2)}, u32[]{:S(2)}) %collective-permute-start.7) | collective-permute-done | bytes 1572896 | tf_op jit(solution)/shard_map/ppermute | solution.py:264
  616.6 28.6 %collective-permute-done.6.far_ref = bf16[1,256,3072]{2,1,0:T(8,128)(2,1)} collective-permute-done((bf16[1,256,3072]{2,1,0:T(8,128)(2,1)}, bf16[1,256,3072]{2,1,0:T(8,128)(2,1)}, u32[]{:S(2)}, u32[]{:S(2)}) %collective-permute-start.6) | collective-permute-done | bytes 1572896 | tf_op jit(solution)/shard_map/ppermute | solution.py:264
  650.1 26.7 %collective-permute-done.5.far_ref = bf16[1,256,3072]{2,1,0:T(8,128)(2,1)} collective-permute-done((bf16[1,256,3072]{2,1,0:T(8,128)(2,1)}, bf16[1,256,3072]{2,1,0:T(8,128)(2,1)}, u32[]{:S(2)}, u32[]{:S(2)}) %collective-permute-start.5) | collective-permute-done | bytes 1572896 | tf_op jit(solution)/shard_map/ppermute | solution.py:264
  681.8 33.8 %psum.7 = f32[3072]{0:T(1024)S(1)} all-reduce(f32[3072]{0:T(1024)S(1)} %add_reduce_fusion), channel_id=1, replica_groups=mesh['tp'=2,'dp'=8] {'dp','tp'}, use_global_device_ids=true, to_apply=%region_3.0 | all-reduce | flops 3072 | bytes 24576 | tf_op jit(solution)/shard_map/psum | solution.py:351
  (93 shorter events, 127.2 us)
Async XLA Ops:
  7.2 92.0 %all-gather.4.cloned.1.call-start = ((), (), s32[]{:S(2)}) async-start(), calls=%async_computation.2 | async-start | bytes 17694720 | tf_op jit(solution)/shard_map/all_gather | solution.py:287
  14.6 201.6 %all-gather.6.cloned.1.call-start = ((), (), s32[]{:S(2)}) async-start(), calls=%async_computation.3 | async-start | bytes 10616832 | tf_op jit(solution)/shard_map/all_gather | solution.py:288
  15.4 11.8 %copy-start.7 = (bf16[384]{0:T(512)(128)(2,1)S(1)}, bf16[384]{0:T(512)(128)(2,1)}, u32[]{:S(2)}) copy-start(bf16[384]{0:T(512)(128)(2,1)} %param.8) | copy-start | bytes 2308
  15.4 700.9 %reduce-scatter.3.cloned.1.call-start = ((), (), s32[]{:S(2)}) async-start(), calls=%async_computation.4 | async-start | bytes 35389440 | tf_op jit(solution)/shard_map/reduce_scatter | solution.py:325
  15.4 140.0 %collective-permute-start = (bf16[4,256,3072]{2,1,0:T(8,128)(2,1)}, bf16[4,256,3072]{2,1,0:T(8,128)(2,1)}, u32[]{:S(2)}, u32[]{:S(2)}) collective-permute-start(bf16[4,256,3072]{2,1,0:T(8,128)(2,1)} %x_ref.11), channel_id=1, source_target_pairs={{0,8},{8,0},{1,9},{9,1},{2,10},{10,2},{3,11},{11,3},{4,12},{12,4},... | collective-permute-start | bytes 18874376 | tf_op jit(solution)/shard_map/ppermute | solution.py:264
  25.2 217.2 %collective-permute-start.2 = (bf16[2,256,3072]{2,1,0:T(8,128)(2,1)}, bf16[2,256,3072]{2,1,0:T(8,128)(2,1)}, u32[]{:S(2)}, u32[]{:S(2)}) collective-permute-start(bf16[2,256,3072]{2,1,0:T(8,128)(2,1)} %get-tuple-element.55), channel_id=1, source_target_pairs={{0,8},{8,0},{1,9},{9,1},{2,10},{10,2},{3,11},{11,3},{4,12},{12,4},... | collective-permute-start | bytes 9437192 | tf_op jit(solution)/shard_map/ppermute | solution.py:264
  25.2 266.1 %collective-permute-start.1 = (bf16[2,256,3072]{2,1,0:T(8,128)(2,1)}, bf16[2,256,3072]{2,1,0:T(8,128)(2,1)}, u32[]{:S(2)}, u32[]{:S(2)}) collective-permute-start(bf16[2,256,3072]{2,1,0:T(8,128)(2,1)} %get-tuple-element.56), channel_id=1, source_target_pairs={{0,8},{8,0},{1,9},{9,1},{2,10},{10,2},{3,11},{11,3},{4,12},{12,4},... | collective-permute-start | bytes 9437192 | tf_op jit(solution)/shard_map/ppermute | solution.py:264
  37.7 145.0 %copy-start.1 = (f32[512,128]{1,0:T(8,128)}, f32[512,128]{1,0:T(8,128)S(1)}, u32[]{:S(2)}) copy-start(f32[512,128]{1,0:T(8,128)S(1)} %get-tuple-element.63.sin_ref) | copy-start | bytes 786436
  216.2 9.4 %copy-start.9 = (bf16[4,256,1536]{2,1,0:T(8,128)(2,1)S(1)}, bf16[4,256,1536]{2,1,0:T(8,128)(2,1)}, u32[]{:S(2)}) copy-start(bf16[4,256,1536]{2,1,0:T(8,128)(2,1)} %get-tuple-element.33) | copy-start | bytes 9437188
  216.2 15.9 %slice-start.2 = ((s8[6291456]{0:T(1024)(128)(4,1)}), s8[4194304]{0:T(1024)(128)(4,1)S(1)}, s32[]{:S(2)}) async-start(s8[6291456]{0:T(1024)(128)(4,1)} %bitcast.99), calls=%async_computation.8 | async-start | bytes 8388608
  242.3 9.5 %copy-start.2 = (f32[512,128]{1,0:T(8,128)S(1)}, f32[512,128]{1,0:T(8,128)}, u32[]{:S(2)}) copy-start(f32[512,128]{1,0:T(8,128)} %copy-done.1) | copy-start | bytes 786436
  251.9 26.2 %copy-start.5 = (bf16[4,256,1536]{2,1,0:T(8,128)(2,1)S(1)}, bf16[4,256,1536]{2,1,0:T(8,128)(2,1)}, u32[]{:S(2)}) copy-start(bf16[4,256,1536]{2,1,0:T(8,128)(2,1)} %copy-done.4) | copy-start | bytes 9437188
  311.1 9.7 %copy-start.3 = (f32[512,128]{1,0:T(8,128)S(1)}, f32[512,128]{1,0:T(8,128)}, u32[]{:S(2)}) copy-start(f32[512,128]{1,0:T(8,128)} %copy-done.1) | copy-start | bytes 786436
  404.7 322.3 %reduce-scatter.5.cloned.1.call-start = ((), (), s32[]{:S(2)}) async-start(), calls=%async_computation.5 | async-start | bytes 21233664 | tf_op jit(solution)/shard_map/reduce_scatter | solution.py:322
  405.3 76.7 %collective-permute-start.4 = (bf16[2,256,3072]{2,1,0:T(8,128)(2,1)}, bf16[2,256,3072]{2,1,0:T(8,128)(2,1)S(1)}, u32[]{:S(2)}, u32[]{:S(2)}) collective-permute-start(bf16[2,256,3072]{2,1,0:T(8,128)(2,1)} %fusion.44), channel_id=1, source_target_pairs={{0,8},{8,0},{1,9},{9,1},{2,10},{10,2},{3,11},{11,3},{4,12},{12,4},... | collective-permute-start | bytes 9437192 | tf_op jit(solution)/shard_map/ppermute | solution.py:264
  407.3 136.7 %collective-permute-start.3 = (bf16[2,256,3072]{2,1,0:T(8,128)(2,1)}, bf16[2,256,3072]{2,1,0:T(8,128)(2,1)}, u32[]{:S(2)}, u32[]{:S(2)}) collective-permute-start(bf16[2,256,3072]{2,1,0:T(8,128)(2,1)} %fusion.47), channel_id=1, source_target_pairs={{0,8},{8,0},{1,9},{9,1},{2,10},{10,2},{3,11},{11,3},{4,12},{12,4},... | collective-permute-start | bytes 9437192 | tf_op jit(solution)/shard_map/ppermute | solution.py:264
  420.6 157.1 %collective-permute-start.8 = (bf16[1,256,3072]{2,1,0:T(8,128)(2,1)}, bf16[1,256,3072]{2,1,0:T(8,128)(2,1)}, u32[]{:S(2)}, u32[]{:S(2)}) collective-permute-start(bf16[1,256,3072]{2,1,0:T(8,128)(2,1)} %fusion.53), channel_id=1, source_target_pairs={{0,8},{8,0},{1,9},{9,1},{2,10},{10,2},{3,11},{11,3},{4,12},{12,4},... | collective-permute-start | bytes 4718600 | tf_op jit(solution)/shard_map/ppermute | solution.py:264
  437.5 174.0 %collective-permute-start.7 = (bf16[1,256,3072]{2,1,0:T(8,128)(2,1)}, bf16[1,256,3072]{2,1,0:T(8,128)(2,1)}, u32[]{:S(2)}, u32[]{:S(2)}) collective-permute-start(bf16[1,256,3072]{2,1,0:T(8,128)(2,1)} %fusion.54), channel_id=1, source_target_pairs={{0,8},{8,0},{1,9},{9,1},{2,10},{10,2},{3,11},{11,3},{4,12},{12,4},... | collective-permute-start | bytes 4718600 | tf_op jit(solution)/shard_map/ppermute | solution.py:264
  452.0 193.2 %collective-permute-start.6 = (bf16[1,256,3072]{2,1,0:T(8,128)(2,1)}, bf16[1,256,3072]{2,1,0:T(8,128)(2,1)}, u32[]{:S(2)}, u32[]{:S(2)}) collective-permute-start(bf16[1,256,3072]{2,1,0:T(8,128)(2,1)} %fusion.55), channel_id=1, source_target_pairs={{0,8},{8,0},{1,9},{9,1},{2,10},{10,2},{3,11},{11,3},{4,12},{12,4},... | collective-permute-start | bytes 4718600 | tf_op jit(solution)/shard_map/ppermute | solution.py:264
  466.2 37.1 %slice-start = ((s8[6291456]{0:T(1024)(128)(4,1)}), s8[4194304]{0:T(1024)(128)(4,1)S(1)}, s32[]{:S(2)}) async-start(s8[6291456]{0:T(1024)(128)(4,1)} %bitcast.97), calls=%async_computation.6 | async-start | bytes 8388608
  481.9 21.3 %slice-start.1 = ((s8[6291456]{0:T(1024)(128)(4,1)}), s8[2097152]{0:T(1024)(128)(4,1)S(1)}, s32[]{:S(2)}) async-start(s8[6291456]{0:T(1024)(128)(4,1)} %bitcast.97), calls=%async_computation.7 | async-start | bytes 4194304
  482.0 194.9 %collective-permute-start.5 = (bf16[1,256,3072]{2,1,0:T(8,128)(2,1)}, bf16[1,256,3072]{2,1,0:T(8,128)(2,1)}, u32[]{:S(2)}, u32[]{:S(2)}) collective-permute-start(bf16[1,256,3072]{2,1,0:T(8,128)(2,1)} %fusion.56), channel_id=1, source_target_pairs={{0,8},{8,0},{1,9},{9,1},{2,10},{10,2},{3,11},{11,3},{4,12},{12,4},... | collective-permute-start | bytes 4718600 | tf_op jit(solution)/shard_map/ppermute | solution.py:264
  506.1 71.6 %slice-start.4 = ((s8[6291456]{0:T(1024)(128)(4,1)}), s8[4194304]{0:T(1024)(128)(4,1)S(1)}, s32[]{:S(2)}) async-start(s8[6291456]{0:T(1024)(128)(4,1)} %bitcast.101), calls=%async_computation.10 | async-start | bytes 8388608
  510.0 67.7 %slice-start.5 = ((s8[6291456]{0:T(1024)(128)(4,1)}), s8[2097152]{0:T(1024)(128)(4,1)S(1)}, s32[]{:S(2)}) async-start(s8[6291456]{0:T(1024)(128)(4,1)} %bitcast.101), calls=%async_computation.11 | async-start | bytes 4194304
  (6 other events, 25.4 us)
Sparse Core Ops, SparseCore 0:
  14.7 84.3 all-gather.3
  101.0 56.7 all-gather.5
  404.8 187.6 reduce-scatter.2
  596.5 121.7 reduce-scatter.4

commit v2 on v1

--- a/solution.py
+++ b/solution.py
@@ -52,7 +52,8 @@
     rec_ref[0, :, columns] = jnp.where(first, upper, lower).astype(rec_ref.dtype)
 
 
-def attention_fwd_kernel(group_size, tp_ref, own_ref, rec_ref, cos_ref, sin_ref, out_own_ref, out_rec_ref):
+def attention_fwd_kernel(group_size, tp_ref, own_ref, rec_ref, cos_ref, sin_ref, *rest):
+    out_own_ref, out_rec_ref = rest[-2:]
     half = own_ref.shape[1]
     first = tp_ref[0] == 0
     lower, upper = pick_halves(first, own_ref[0], rec_ref[0])
@@ -138,26 +139,36 @@
     return pl.CostEstimate(flops=int(flops), transcendentals=int(transcendentals), bytes_accessed=int(sum(a.size * a.dtype.itemsize for a in arrays)))
 
 
-def attention_fwd(tp_index, qkv_own, qkv_rec, tables, groups, group_size):
+def attention_fwd(tp_index, qkv_own, qkv_rec, tables, start, held, groups, group_size):
     batch, half, width = qkv_own.shape
+    count = qkv_rec.shape[0]
     block = width // groups
     out_block = group_size * HEAD_DIM
     shape = jax.ShapeDtypeStruct((batch, half, groups * out_block), BF16)
-    spec = lambda columns: pl.BlockSpec((1, half, columns), lambda b, g, tp: (b, 0, g))
+    spec = lambda columns, offset: pl.BlockSpec((1, half, columns), lambda b, g, tp: (b + offset, 0, g))
     table = pl.BlockSpec((2 * half, HEAD_DIM), lambda b, g, tp: (0, 0))
+    in_specs = [spec(block, start), spec(block, 0), table, table]
+    args = [tp_index, qkv_own, qkv_rec, *tables]
+    aliases = {}
+    if held is not None:
+        in_specs += [pl.BlockSpec(memory_space=pl.ANY)] * 2
+        aliases = {len(args): 0, len(args) + 1: 1}
+        args += list(held)
+    work = count * groups * group_size * half * half
     return pl.pallas_call(
         functools.partial(attention_fwd_kernel, group_size),
         out_shape=(shape, shape),
         grid_spec=pltpu.PrefetchScalarGridSpec(
             num_scalar_prefetch=1,
-            grid=(batch, groups),
-            in_specs=[spec(block), spec(block), table, table],
-            out_specs=(spec(out_block), spec(out_block)),
+            grid=(count, groups),
+            in_specs=in_specs,
+            out_specs=(spec(out_block, start), spec(out_block, start)),
         ),
+        input_output_aliases=aliases,
         compiler_params=pltpu.CompilerParams(vmem_limit_bytes=48 * 2**20),
-        cost_estimate=cost(batch * groups * group_size * half * half * HEAD_DIM * 12, batch * groups * group_size * half * half * 3, qkv_own, qkv_rec, shape, shape),
+        cost_estimate=cost(work * HEAD_DIM * 12, work * 3, qkv_rec, qkv_rec),
         name="attention_fwd",
-    )(tp_index, qkv_own, qkv_rec, *tables)
+    )(*args)
 
 
 def attention_bwd(tp_index, qkv_own, qkv_rec, tables, ga_own, ga_rec, start, held, groups, group_size):
@@ -168,7 +179,7 @@
     shape = jax.ShapeDtypeStruct((batch, half, width), BF16)
     spec = lambda columns, offset: pl.BlockSpec((1, half, columns), lambda b, g, tp: (b + offset, 0, g))
     table = pl.BlockSpec((2 * half, HEAD_DIM), lambda b, g, tp: (0, 0))
-    in_specs = [spec(block, start), spec(block, start), table, table, spec(ga_block, start), spec(ga_block, 0)]
+    in_specs = [spec(block, start), spec(block, 0), table, table, spec(ga_block, start), spec(ga_block, 0)]
     args = [tp_index, qkv_own, qkv_rec, *tables, ga_own, ga_rec]
     aliases = {}
     if held is not None:
@@ -248,9 +259,72 @@
     return result if gain is not None else result[0]
 
 
-DY_CHUNKS = 2
-OUT_CHUNKS = 2
-DN_CHUNKS = 4
+def regroup_kernel(q_ref, k_ref, v_ref, out_ref):
+    split = q_ref.shape[1]
+    out_ref[:, :split] = q_ref[...]
+    out_ref[:, split:split + HEAD_DIM] = k_ref[...]
+    out_ref[:, split + HEAD_DIM:] = v_ref[...]
+
+
+def regroup(w_query, w_key, w_value):
+    rows = w_query.shape[0]
+    groups = w_key.shape[1] // HEAD_DIM
+    split = w_query.shape[1] // groups
+    spec = lambda columns: pl.BlockSpec((rows, columns), lambda g: (0, g))
+    out = jax.ShapeDtypeStruct((rows, groups * (split + 2 * HEAD_DIM)), w_query.dtype)
+    return pl.pallas_call(
+        regroup_kernel,
+        out_shape=out,
+        grid=(groups,),
+        in_specs=[spec(split), spec(HEAD_DIM), spec(HEAD_DIM)],
+        out_specs=spec(split + 2 * HEAD_DIM),
+        cost_estimate=cost(rows * out.shape[1] * 400, 0, out, out),
+        name="regroup",
+    )(w_query, w_key, w_value)
+
+
+def ungroup_kernel(first_ref, near_a_ref, far_a_ref, near_b_ref, far_b_ref, q_ref, k_ref, v_ref):
+    split = q_ref.shape[1]
+    group, last = pl.program_id(0), pl.num_programs(0) - 1
+
+    def put(block):
+        q_ref[...] = block[:, :split]
+        k_ref[...] = block[:, split:split + HEAD_DIM]
+        v_ref[...] = block[:, split + HEAD_DIM:]
+
+    @pl.when(group < last - 1)
+    def _():
+        put(first_ref[...])
+
+    @pl.when(group == last - 1)
+    def _():
+        put(near_a_ref[...] + far_a_ref[...])
+
+    @pl.when(group == last)
+    def _():
+        put(near_b_ref[...] + far_b_ref[...])
+
+
+def ungroup(first, terms_a, terms_b, groups):
+    rows, block = terms_a[0].shape
+    split = block - 2 * HEAD_DIM
+    row_block = rows // 2
+    spec = lambda columns: pl.BlockSpec((row_block, columns), lambda g, r: (r, g))
+    late = pl.BlockSpec((row_block, block), lambda g, r: (r, 0))
+    shape = lambda columns: jax.ShapeDtypeStruct((rows, groups * columns), F32)
+    return pl.pallas_call(
+        ungroup_kernel,
+        out_shape=(shape(split), shape(HEAD_DIM), shape(HEAD_DIM)),
+        grid=(groups, rows // row_block),
+        in_specs=[pl.BlockSpec((row_block, block), lambda g, r: (r, jnp.minimum(g, groups - 3))), late, late, late, late],
+        out_specs=(spec(split), spec(HEAD_DIM), spec(HEAD_DIM)),
+        compiler_params=pltpu.CompilerParams(vmem_limit_bytes=32 * 2**20),
+        cost_estimate=cost(rows * block * groups * 400, 0, first, *terms_a, *terms_b, first, first),
+        name="ungroup",
+    )(first, *terms_a, *terms_b)
+
+
+CHUNKS = 2
 
 
 def after(value, *others):
@@ -275,15 +349,17 @@
         tp_index = lax.axis_index("tp").astype(jnp.int32).reshape(1)
         tables = rope_tables(2 * half)
 
-        hidden_rec = exchange(hidden)
-        step = batch // DY_CHUNKS
-        grad_rec = []
-        for i in range(DY_CHUNKS):
+        step = batch // CHUNKS
+        hidden_rec, grad_rec = [], []
+        source = hidden
+        for i in range(CHUNKS):
+            piece = lax.optimization_barrier(source[i * step:(i + 1) * step])
+            source = after(hidden, piece)
+            hidden_rec.append(exchange(piece))
+        for i in range(CHUNKS):
             grad_rec.append(exchange(grad_out[i * step:(i + 1) * step]))
 
-        w_qkv = jnp.concatenate(
-            [w_query.reshape(rows_loc, groups, -1), w_key.reshape(rows_loc, groups, -1), w_value.reshape(rows_loc, groups, -1)], axis=2
-        ).reshape(rows_loc, groups * block)
+        w_qkv = regroup(w_query, w_key, w_value)
         w_qkv = lax.all_gather(w_qkv, "dp", axis=0, tiled=True)
         w_o = lax.all_gather(w_out, "dp", axis=1, tiled=True)
         gain = lax.all_gather(norm_gain, "dp", axis=0, tiled=True).astype(F32)
@@ -295,67 +371,84 @@
 
         normed_own = norm(hidden)
         qkv_own = mm("bsd,de->bse", normed_own, w_qkv).astype(BF16)
-        normed_rec = norm(after(hidden_rec, qkv_own))
-        qkv_rec = mm("bsd,de->bse", normed_rec, w_qkv).astype(BF16)
-        attn_own, attn_rec = attention_fwd(tp_index, qkv_own, qkv_rec, tables, groups, group_size)
-
-        step = batch // OUT_CHUNKS
+        qkv_rec = []
+        attn = None
+        before = qkv_own
+        for i in range(CHUNKS):
+            rec = norm(after(hidden_rec[i], before))
+            qkv_rec.append(mm("bsd,de->bse", rec, w_qkv).astype(BF16))
+            attn = attention_fwd(tp_index, qkv_own, qkv_rec[i], tables, i * step, attn, groups, group_size)
+            before = attn[0]
+        attn_own, attn_rec = attn
+
         out_send = []
-        for i in range(OUT_CHUNKS):
-            out_send.append(mm("bse,ed->bsd", attn_rec[i * step:(i + 1) * step], w_o).astype(BF16))
-        out_far = []
-        for i in range(OUT_CHUNKS):
-            out_far.append(exchange(out_send[i]))
+        for i in range(CHUNKS):
+            out_send.append(lax.optimization_barrier(mm("bse,ed->bsd", attn_rec[i * step:(i + 1) * step], w_o).astype(BF16)))
 
         ga_own = mm("bsd,ed->bse", after(grad_out, *out_send), w_o).astype(BF16)
+        normed_rec = norm(jnp.concatenate([after(piece, ga_own) for piece in hidden_rec], axis=0))
         held = None
-        step = batch // DY_CHUNKS
-        for i in range(DY_CHUNKS):
-            if i == DY_CHUNKS - 1:
+        before = ga_own
+        for i in range(CHUNKS):
+            if i == CHUNKS - 1:
                 grad_wo = mm("bse,bsd->ed", attn_own, after(grad_out, *held)) + mm("bse,bsd->ed", attn_rec, jnp.concatenate(grad_rec, axis=0))
-                ga_rec = mm("bsd,ed->bse", after(grad_rec[i], grad_wo), w_o).astype(BF16)
-            else:
-                ga_rec = mm("bsd,ed->bse", after(grad_rec[i], ga_own), w_o).astype(BF16)
-            held = attention_bwd(tp_index, qkv_own, qkv_rec, tables, ga_own, ga_rec, i * step, held, groups, group_size)
+                before = grad_wo
+            ga_rec = mm("bsd,ed->bse", after(grad_rec[i], before), w_o).astype(BF16)
+            held = attention_bwd(tp_index, qkv_own, qkv_rec[i], tables, ga_own, ga_rec, i * step, held, groups, group_size)
         gqkv_own, gqkv_rec = held
-
         grad_wo = lax.psum_scatter(grad_wo, "dp", scatter_dimension=1, tiled=True)
-        grad_wqkv = mm("bsd,bse->de", normed_own, gqkv_own) + mm("bsd,bse->de", normed_rec, gqkv_rec)
-        gqkv_own, gqkv_rec = after((gqkv_own, gqkv_rec), grad_wqkv)
-        grad_wqkv = lax.psum_scatter(grad_wqkv, "dp", scatter_dimension=0, tiled=True)
-
-        step = batch // DN_CHUNKS
+
         dn_send = []
-        for i in range(DN_CHUNKS):
-            dn_send.append(mm("bse,de->bsd", gqkv_rec[i * step:(i + 1) * step], w_qkv).astype(BF16))
-        dn_far = []
-        for i in range(DN_CHUNKS):
-            dn_far.append(exchange(dn_send[i]))
-
-        attn_own, gqkv_own = after((attn_own, gqkv_own), *dn_send)
+        for i in range(CHUNKS):
+            dn_send.append(lax.optimization_barrier(mm("bse,de->bsd", gqkv_rec[i * step:(i + 1) * step], w_qkv).astype(BF16)))
+
+        out_far, dn_far = [], []
+        out_far.append(exchange(out_send[0]))
+        for i in range(batch):
+            dn_far.append(exchange(dn_send[i // step][i % step:i % step + 1]))
+        for i in range(step, batch):
+            out_far.append(exchange(out_send[1][i - step:i - step + 1]))
+
+        cut = groups // 2 * block
+        gqkv_own, gqkv_rec = after((gqkv_own, gqkv_rec), *dn_send)
+        late = mm("bsd,bse->de", normed_own, gqkv_own[:, :, cut:]) + mm("bsd,bse->de", normed_rec, gqkv_rec[:, :, cut:])
+        place = lax.axis_index("dp").astype(jnp.uint32)
+        core, along_x, along_y = place & 1, (place >> 1) & 1, place >> 2
+
+        def halve(values, axis, coordinate, bit):
+            theirs = lax.dynamic_index_in_dim(values, coordinate ^ 1, axis, keepdims=False)
+            theirs, values = lax.optimization_barrier((theirs, values))
+            mine = lax.dynamic_index_in_dim(values, coordinate, axis, keepdims=False)
+            return theirs, mine, lax.ppermute(theirs, "dp", [(i, i ^ bit) for i in range(8)])
+
+        late = late.reshape(2, 2, 2, rows_loc, cut)
+        sent, mine, far = halve(late, 2, core, 1)
+        gqkv_own, gqkv_rec = after((gqkv_own, gqkv_rec), sent)
+        early = mm("bsd,bse->de", normed_own, gqkv_own[:, :, :cut]) + mm("bsd,bse->de", normed_rec, gqkv_rec[:, :, :cut])
+        early_sum = lax.psum_scatter(early, "dp", scatter_dimension=0, tiled=True)
+        late = mine + after(far, early)
+        sent_x, mine_x, far_x = halve(late[..., :block], 1, along_x, 2)
+        sent_y, mine_y, far_y = halve(late[..., block:], 0, along_y, 4)
+
+        attn_own, gqkv_own = after((attn_own, gqkv_own), sent_x, sent_y)
         out_near = lax.optimization_barrier(mm("bse,ed->bsd", attn_own, w_o).astype(BF16))
         dn_near = lax.optimization_barrier(mm("bse,de->bsd", gqkv_own, w_qkv).astype(BF16))
-        hidden_out = None
-        step = batch // OUT_CHUNKS
-        for i in range(OUT_CHUNKS):
-            hidden_out = finish(finish_out_kernel, [hidden, out_near], [out_far[i]], i * step, hidden_out)
-        dn_near = after(dn_near, hidden_out)
+        hidden_out = finish(finish_out_kernel, [hidden, out_near], [out_far[0]], 0, None)
+        sent_xy, mine_xy, far_xy = halve(mine_x + after(far_x, hidden_out), 0, along_y, 4)
+        sent_yx, mine_yx, far_yx = halve(mine_y + after(far_y, hidden_out), 0, along_x, 2)
+        dn_near = after(dn_near, sent_xy, sent_yx)
         grad_hidden = None
         gain_parts = []
-        step = batch // DN_CHUNKS
-        for i in range(DN_CHUNKS):
+        for i in range(batch):
             grad_hidden, part = finish(
-                finish_grad_kernel, [hidden, grad_out, dn_near], [dn_far[i]], i * step, grad_hidden, gain
+                finish_grad_kernel, [hidden, grad_out, dn_near], [dn_far[i]], i, grad_hidden, gain
             )
             gain_parts.append(part)
         gain_sum = lax.psum(jnp.sum(sum(gain_parts), axis=0), ("dp", "tp"))
         grad_gain = lax.dynamic_slice(gain_sum, (lax.axis_index("dp") * rows_loc,), (rows_loc,))
-
-        grad_wqkv = grad_wqkv.reshape(rows_loc, groups, block)
-        split = group_size * HEAD_DIM
-        grad_wq = grad_wqkv[:, :, :split].reshape(rows_loc, -1)
-        grad_wk = grad_wqkv[:, :, split:split + HEAD_DIM].reshape(rows_loc, -1)
-        grad_wv = grad_wqkv[:, :, split + HEAD_DIM:].reshape(rows_loc, -1)
+        for i in range(step, batch):
+            hidden_out = finish(finish_out_kernel, [hidden, out_near], [after(out_far[i - step + 1], gain_sum, hidden_out)], i, hidden_out)
+        grad_wq, grad_wk, grad_wv = ungroup(early_sum, (mine_xy, far_xy), (mine_yx, far_yx), groups)
         return hidden_out, grad_hidden, grad_gain, grad_wq, grad_wk, grad_wv, grad_wo
 
     act_spec = P("dp", "tp", None)

time: 739 us -> 786 us (1.064)
  matrix products: 275 us -> 252 us
  other arithmetic: 10.6 us -> 29.5 us
  local copies, waits for them, and re-layouts: 28.6 us -> 44 us
  waiting for transfers between devices: 236 us -> 250 us
  Pallas kernels: 114 us -> 126 us
  starting transfers between devices: 12.1 us -> 22.3 us
    ppermute x0 -> x5, waiting for transfers between devices: none -> 36.9 us  [halve(): lax.ppermute(theirs, 'dp', [(i, i ^ bit) for i in range(8)])]
    dot_general x17 -> x18, matrix products: 275 us -> 252 us  [mm(): return jnp.einsum(eq, a, b, preferred_element_type=F32)]
    ppermute x9 -> x11, waiting for transfers between devices: 178 us -> 158 us  [exchange(): return lax.ppermute(values, 'tp', swap)]
    slice x3 -> x6, local copies, waits for them, and re-layouts: 1.93 us -> 18.1 us  [the longest x2 5.76 us: local_block(): dn_far.append(exchange(dn_send[i // step][i % step:i % step + 1]))]
    add x0 -> x3, other arithmetic: none -> 14.7 us  [the longest x1 11.1 us: local_block(): late = mine + after(far, early)]
    squeeze x0 -> x7, local copies, waits for them, and re-layouts: none -> 12.1 us  [the longest x5 11.9 us: halve(): lax.dynamic_index_in_dim(values, coordinate ^ 1, axis, keepdims=False)]
    pallas_call x0 -> x2, Pallas kernels: none -> 11.1 us  [the longest x1 7.33 us: ungroup(): pl.pallas_call(ungroup_kernel, out_shape=(shape(split), shape(HEAD_DIM),...]
    reshape x4 -> x0, local copies, waits for them, and re-layouts: 10 us -> none  [the longest x1 5.31 us: local_block(): grad_wqkv = grad_wqkv.reshape(rows_loc, groups, block)]
  transfers between devices with their start and end apart: 13 -> 20, of which waited for: 7 -> 10; matrix products, arithmetic and copies ran while one was open for 29% -> 25% of each run, Pallas kernels for 12% -> 12%
where the time goes in v2:
time: 786 us; the launch traced here: 781 us
  matrix products  252 us (32%)
  waiting for transfers between devices  250 us (32%)
  Pallas kernels  126 us (16%)
  local copies, waits for them, and re-layouts  44 us (6%)
  blocking collectives  42.6 us (5%)
  other arithmetic  29.5 us (4%)
  starting transfers between devices  22.3 us (3%)
  between operations  14.7 us (2%)
    dot_general x18, matrix products, mm(): return jnp.einsum(eq, a, b, preferred_element_type=F32)  252 us
    ppermute x11, waiting for transfers between devices, exchange(): return lax.ppermute(values, 'tp', swap)  158 us
    all_gather x1, waiting for transfers between devices, local_block(): w_qkv = lax.all_gather(w_qkv, 'dp', axis=0, tiled=True)  53.7 us
    pallas_call x2, Pallas kernels, attention_bwd(): pl.pallas_call(functools.partial(attention_bwd_kernel, group_size), out_s...  50.7 us
    ppermute x5, waiting for transfers between devices, halve(): lax.ppermute(theirs, 'dp', [(i, i ^ bit) for i in range(8)])  36.9 us
    pallas_call x2, Pallas kernels, attention_fwd(): pl.pallas_call(functools.partial(attention_fwd_kernel, group_size), out_s...  33.7 us
    psum x1, blocking collectives, local_block(): gain_sum = lax.psum(jnp.sum(sum(gain_parts), axis=0), ('dp', 'tp'))  33.3 us
    pallas_call x7, Pallas kernels, finish(): pl.pallas_call(kernel, out_shape=out_shape, grid=(count, half // row_bloc...  30 us
  transfers between devices with their start and end apart: 20, of which 10 were waited for; matrix products, arithmetic and copies ran while one was open for 25% of the time, Pallas kernels for 12%

profile of v2, /device:TPU:0, one launch (start us, length us, event | category | flops | bytes accessed | tf_op | source)
XLA Modules:
  0.0 781.3 jit_solution(1938920727836073038)
XLA Ops:
  41.8 53.7 %all-gather.4.cloned.1.call-done = bf16[3072,2560]{1,0:T(8,128)(2,1)} async-done(((bf16[384,2560]{1,0:T(8,128)(2,1)}), bf16[3072,2560]{1,0:T(8,128)(2,1)}) %all-gather.4.cloned.1.call-update) | async-done | bytes 15728656 | tf_op jit(solution)/shard_map/all_gather | solution.py:363
  95.6 23.7 %fusion.45.own_ref = bf16[4,256,2560]{2,1,0:T(8,128)(2,1)} fusion(bf16[3072,2560]{1,0:T(8,128)(2,1)} %all-gather.4.cloned.1.call-done, bf16[4,256,3072]{2,1,0:T(8,128)(2,1)} %x_ref.13, f32[3072]{0:T(1024)S(1)} %bitcast.106, f32[4,256]{1,0:T(4,128)S(1)} %add_rsqrt_fusion.1), kind=kOutput, calls=%fused_computation.55 | convolution fusion | flops 16121331712 | bytes 27279360 | tf_op jit(solution)/shard_map/bsd,de->bse/dot_general | solution.py:341
  121.8 14.0 %fusion.50.rec_ref = bf16[2,256,2560]{2,1,0:T(8,128)(2,1)S(1)} fusion(bf16[3072,2560]{1,0:T(8,128)(2,1)} %all-gather.4.cloned.1.call-done, bf16[2,256,3072]{2,1,0:T(8,128)(2,1)} %collective-permute-done.1, f32[3072]{0:T(1024)S(1)} %bitcast.107, f32[2,256]{1,0:T(2,128)S(1)} %add_rsqrt_fusion.3), kind=kOutput, calls=%fused_computation.56 | convolution fusion | flops 8060665856 | bytes 21510144 | tf_op jit(solution)/shard_map/bsd,de->bse/dot_general | solution.py:341
  135.9 17.0 %attention_fwd.2 = (bf16[4,256,1536]{2,1,0:T(8,128)(2,1)}, bf16[4,256,1536]{2,1,0:T(8,128)(2,1)}) custom-call(s32[1]{0:T(128)} %bitcast.tp_ref, bf16[4,256,2560]{2,1,0:T(8,128)(2,1)} %fusion.45.own_ref, bf16[2,256,2560]{2,1,0:T(8,128)(2,1)S(1)} %fusion.50.rec_ref, f32[512,128]{1,0:T(8,128)S(1)} %get-tuple-element.120.cos_ref, ...), custom_call_target="tpu_custom_call" | custom-call | flops 2415919104 | bytes 5242880 | tf_op jit(solution)/shard_map/attention_fwd/pallas_call | solution.py:158
  158.3 13.0 %fusion.53.rec_ref = bf16[2,256,2560]{2,1,0:T(8,128)(2,1)S(1)} fusion(bf16[3072,2560]{1,0:T(8,128)(2,1)} %all-gather.4.cloned.1.call-done, bf16[2,256,3072]{2,1,0:T(8,128)(2,1)} %collective-permute-done, f32[2,256]{1,0:T(2,128)S(1)} %add_rsqrt_fusion.2, f32[3072]{0:T(1024)S(1)} %bitcast.108), kind=kOutput, calls=%fused_computation.57 | convolution fusion | flops 8060665856 | bytes 21510144 | tf_op jit(solution)/shard_map/bsd,de->bse/dot_general | solution.py:341
  171.2 16.7 %attention_fwd.3 = (bf16[4,256,1536]{2,1,0:T(8,128)(2,1)}, bf16[4,256,1536]{2,1,0:T(8,128)(2,1)}) custom-call(s32[1]{0:T(128)} %bitcast.tp_ref, bf16[4,256,2560]{2,1,0:T(8,128)(2,1)} %fusion.45.own_ref, bf16[2,256,2560]{2,1,0:T(8,128)(2,1)S(1)} %fusion.53.rec_ref, ...), custom_call_target="tpu_custom_call", output_to_operand_aliasing={{0}: (5, {}), {1}: (6, {})} | custom-call | flops 2415919104 | bytes 5242880 | tf_op jit(solution)/shard_map/attention_fwd/pallas_call | solution.py:158
  232.8 25.3 %attention_bwd.2 = (bf16[4,256,2560]{2,1,0:T(8,128)(2,1)}, bf16[4,256,2560]{2,1,0:T(8,128)(2,1)}) custom-call(s32[1]{0:T(128)} %bitcast.tp_ref, bf16[4,256,2560]{2,1,0:T(8,128)(2,1)} %fusion.45.own_ref, bf16[2,256,2560]{2,1,0:T(8,128)(2,1)S(1)} %copy-done.11, f32[512,128]{1,0:T(8,128)S(1)} %get-tuple-element.120.cos_ref, ...), custom_call_target="tpu_custom_call" | custom-call | flops 6039797760 | bytes 6291456 | tf_op jit(solution)/shard_map/attention_bwd/pallas_call | solution.py:190
  262.4 13.2 %fusion.103 = f32[1536,3072,1]{1,0,2:T(8,128)} fusion(bf16[4,256,1536]{2,1,0:T(8,128)(2,1)S(1)} %copy-done.18, bf16[4,256,3072]{2,1,0:T(8,128)(2,1)S(1)} %bitcast.103), kind=kOutput, calls=%fused_computation.103 | convolution fusion | flops 9663676416 | bytes 28311552 | tf_op jit(solution)/shard_map/bse,bsd->ed/dot_general | solution.py:341
  275.7 14.0 %collective-permute-done.2 = bf16[2,256,3072]{2,1,0:T(8,128)(2,1)} collective-permute-done((bf16[2,256,3072]{2,1,0:T(8,128)(2,1)}, bf16[2,256,3072]{2,1,0:T(8,128)(2,1)}, u32[]{:S(2)}, u32[]{:S(2)}) %collective-permute-start.2) | collective-permute-done | bytes 3145760 | tf_op jit(solution)/shard_map/ppermute | solution.py:338
  289.7 20.3 %bitcast_add_fusion = f32[1536,3072]{1,0:T(8,128)} fusion(f32[1536,3072,1]{1,0,2:T(8,128)} %fusion.103, bf16[4,256,1536]{2,1,0:T(8,128)(2,1)} %get-tuple-element.63, bf16[2,256,3072]{2,1,0:T(8,128)(2,1)} %collective-permute-done.2, bf16[2,256,3072]{2,1,0:T(8,128)(2,1)} %collective-permute-done.3), kind=kOutput, calls=%fused_computation | convolution fusion | flops 9671540736 | bytes 47185920 | tf_op jit(solution)/shard_map/bse,bsd->ed/dot_general | solution.py:341
  319.5 25.4 %attention_bwd.3 = (bf16[4,256,2560]{2,1,0:T(8,128)(2,1)}, bf16[4,256,2560]{2,1,0:T(8,128)(2,1)}) custom-call(s32[1]{0:T(128)} %bitcast.tp_ref, bf16[4,256,2560]{2,1,0:T(8,128)(2,1)} %fusion.45.own_ref, bf16[2,256,2560]{2,1,0:T(8,128)(2,1)S(1)} %fusion.53.rec_ref, ...), custom_call_target="tpu_custom_call", output_to_operand_aliasing={{0}: (7, {}), {1}: (8, {})} | custom-call | flops 6039797760 | bytes 6291456 | tf_op jit(solution)/shard_map/attention_bwd/pallas_call | solution.py:190
  344.9 14.0 %fusion.59 = bf16[2,256,3072]{2,1,0:T(8,128)(2,1)} fusion(bf16[4,256,2560]{2,1,0:T(8,128)(2,1)} %get-tuple-element.79, bf16[3072,2560]{1,0:T(8,128)(2,1)} %all-gather.4.cloned.1.call-done), kind=kOutput, calls=%fused_computation.59 | convolution fusion | flops 8054636544 | bytes 24117248 | tf_op jit(solution)/shard_map/bse,de->bsd/dot_general | solution.py:341
  358.8 13.8 %fusion.56 = bf16[2,256,3072]{2,1,0:T(8,128)(2,1)} fusion(bf16[4,256,2560]{2,1,0:T(8,128)(2,1)} %get-tuple-element.79, bf16[3072,2560]{1,0:T(8,128)(2,1)} %all-gather.4.cloned.1.call-done), kind=kOutput, calls=%fused_computation.58 | convolution fusion | flops 8054636544 | bytes 24117248 | tf_op jit(solution)/shard_map/bse,de->bsd/dot_general | solution.py:341
  372.7 11.8 %fusion.73 = f32[3072,1280,1]{1,0,2:T(8,128)} fusion(bf16[4,256,3072]{2,1,0:T(8,128)(2,1)S(1)} %bitcast.99, f32[3072]{0:T(1024)S(1)} %bitcast.109, f32[4,256]{1,0:T(4,128)S(1)} %copy-done.21, bf16[4,256,2560]{2,1,0:T(8,128)(2,1)S(1)} %bitcast.120), kind=kOutput, calls=%fused_computation.64 | convolution fusion | flops 8065646592 | bytes 24657920 | tf_op jit(solution)/shard_map/bsd,bse->de/dot_general | solution.py:341
  384.5 17.1 %bitcast_add_fusion.2 = f32[3072,1280]{1,0:T(8,128)} fusion(f32[3072,1280,1]{1,0,2:T(8,128)} %fusion.73, f32[4,256]{1,0:T(4,128)S(1)} %add_rsqrt_fusion, f32[3072]{0:T(1024)S(1)} %bitcast.110, bf16[4,256,2560]{2,1,0:T(8,128)(2,1)} %get-tuple-element.79, bf16[2,256,3072]{2,1,0:T(8,128)(2,1)} %collective-permute-done, ...), kind=kOutput, calls=%fused_computation.2 | convolution fusion | flops 8072724480 | bytes 40386560 | tf_op jit(solution)/shard_map/bsd,bse->de/dot_general | solution.py:341
  408.5 13.3 %fusion.71 = f32[3072,1280,1]{1,0,2:T(8,128)} fusion(bf16[4,256,3072]{2,1,0:T(8,128)(2,1)S(1)} %bitcast.99, f32[3072]{0:T(1024)S(1)} %bitcast.111, f32[4,256]{1,0:T(4,128)S(1)} %copy-done.21, bf16[4,256,2560]{2,1,0:T(8,128)(2,1)} %get-tuple-element.84), kind=kOutput, calls=%fused_computation.63 | convolution fusion | flops 8065646592 | bytes 24657920 | tf_op jit(solution)/shard_map/bsd,bse->de/dot_general | solution.py:341
  421.8 17.3 %bitcast_add_fusion.1 = f32[3072,1280]{1,0:T(8,128)} fusion(f32[3072,1280,1]{1,0,2:T(8,128)} %fusion.71, f32[4,256]{1,0:T(4,128)S(1)} %add_rsqrt_fusion, f32[3072]{0:T(1024)S(1)} %bitcast.112, bf16[4,256,2560]{2,1,0:T(8,128)(2,1)} %get-tuple-element.79, bf16[2,256,3072]{2,1,0:T(8,128)(2,1)} %collective-permute-done, ...), kind=kOutput, calls=%fused_computation.1 | convolution fusion | flops 8072724480 | bytes 40386560 | tf_op jit(solution)/shard_map/bsd,bse->de/dot_general | solution.py:341
  481.2 29.7 %collective-permute-done.7.far_ref = bf16[2,256,3072]{2,1,0:T(8,128)(2,1)S(1)} collective-permute-done((bf16[2,256,3072]{2,1,0:T(8,128)(2,1)}, bf16[2,256,3072]{2,1,0:T(8,128)(2,1)S(1)}, u32[]{:S(2)}, u32[]{:S(2)}) %collective-permute-start.7) | collective-permute-done | bytes 3145760 | tf_op jit(solution)/shard_map/ppermute | solution.py:338
  512.6 13.7 %fusion.39.near_ref = bf16[4,256,3072]{2,1,0:T(8,128)(2,1)S(1)} fusion(bf16[4,256,1536]{2,1,0:T(8,128)(2,1)} %get-tuple-element.83, bf16[1536,3072]{1,0:T(8,128)(2,1)} %all-gather.6.cloned.1.call-done), kind=kOutput, calls=%fused_computation.53 | convolution fusion | flops 9666822144 | bytes 18874368 | tf_op jit(solution)/shard_map/bse,ed->bsd/dot_general | solution.py:341
  531.4 28.9 %collective-permute-done.8 = f32[2,384,640]{2,1,0:T(8,128)} collective-permute-done((f32[2,384,640]{2,1,0:T(8,128)}, f32[2,384,640]{2,1,0:T(8,128)}, u32[]{:S(2)}, u32[]{:S(2)}) %collective-permute-start.8) | collective-permute-done | bytes 1966112 | tf_op jit(solution)/shard_map/ppermute | solution.py:422
  581.1 31.0 %collective-permute-done.11.far_ref = bf16[1,256,3072]{2,1,0:T(8,128)(2,1)} collective-permute-done((bf16[1,256,3072]{2,1,0:T(8,128)(2,1)}, bf16[1,256,3072]{2,1,0:T(8,128)(2,1)}, u32[]{:S(2)}, u32[]{:S(2)}) %collective-permute-start.11) | collective-permute-done | bytes 1572896 | tf_op jit(solution)/shard_map/ppermute | solution.py:338
  613.9 20.7 %fusion.42.near_ref = bf16[4,256,3072]{2,1,0:T(8,128)(2,1)S(1)} fusion(bf16[4,256,2560]{2,1,0:T(8,128)(2,1)} %get-tuple-element.84, bf16[3072,2560]{1,0:T(8,128)(2,1)} %all-gather.4.cloned.1.call-done), kind=kOutput, calls=%fused_computation.54 | convolution fusion | flops 16109273088 | bytes 27262976 | tf_op jit(solution)/shard_map/bse,de->bsd/dot_general | solution.py:341
  646.8 66.0 %collective-permute-done.12.far_ref = bf16[1,256,3072]{2,1,0:T(8,128)(2,1)} collective-permute-done((bf16[1,256,3072]{2,1,0:T(8,128)(2,1)}, bf16[1,256,3072]{2,1,0:T(8,128)(2,1)}, u32[]{:S(2)}, u32[]{:S(2)}) %collective-permute-start.12) | collective-permute-done | bytes 1572896 | tf_op jit(solution)/shard_map/ppermute | solution.py:338
  717.7 33.3 %psum.7 = f32[3072]{0:T(1024)S(1)} all-reduce(f32[3072]{0:T(1024)S(1)} %add_reduce_fusion), channel_id=1, replica_groups=mesh['tp'=2,'dp'=8] {'dp','tp'}, use_global_device_ids=true, to_apply=%region_5.6 | all-reduce | flops 3072 | bytes 24576 | tf_op jit(solution)/shard_map/psum | solution.py:447
  (158 shorter events, 219.7 us)
Async XLA Ops:
  7.2 88.4 %all-gather.4.cloned.1.call-start = ((), (), s32[]{:S(2)}) async-start(), calls=%async_computation.2 | async-start | bytes 17694720 | tf_op jit(solution)/shard_map/all_gather | solution.py:363
  11.0 177.0 %all-gather.6.cloned.1.call-start = ((), (), s32[]{:S(2)}) async-start(), calls=%async_computation.3 | async-start | bytes 10616832 | tf_op jit(solution)/shard_map/all_gather | solution.py:364
  11.8 753.6 %reduce-scatter.3.cloned.1.call-start = ((), (), s32[]{:S(2)}) async-start(), calls=%async_computation.4 | async-start | bytes 17694720 | tf_op jit(solution)/shard_map/reduce_scatter | solution.py:428
  15.7 103.5 %collective-permute-start.1 = (bf16[2,256,3072]{2,1,0:T(8,128)(2,1)}, bf16[2,256,3072]{2,1,0:T(8,128)(2,1)}, u32[]{:S(2)}, u32[]{:S(2)}) collective-permute-start(bf16[2,256,3072]{2,1,0:T(8,128)(2,1)} %slice.60), channel_id=1, source_target_pairs={{0,8},{8,0},{1,9},{9,1},{2,10},{10,2},{3,11},{11,3},{4,12},{12,4},... | collective-permute-start | bytes 9437192 | tf_op jit(solution)/shard_map/ppermute | solution.py:338
  20.9 134.8 %collective-permute-start = (bf16[2,256,3072]{2,1,0:T(8,128)(2,1)}, bf16[2,256,3072]{2,1,0:T(8,128)(2,1)}, u32[]{:S(2)}, u32[]{:S(2)}) collective-permute-start(bf16[2,256,3072]{2,1,0:T(8,128)(2,1)} %slice.61), channel_id=1, source_target_pairs={{0,8},{8,0},{1,9},{9,1},{2,10},{10,2},{3,11},{11,3},{4,12},{12,4},... | collective-permute-start | bytes 9437192 | tf_op jit(solution)/shard_map/ppermute | solution.py:338
  25.1 198.0 %collective-permute-start.3 = (bf16[2,256,3072]{2,1,0:T(8,128)(2,1)}, bf16[2,256,3072]{2,1,0:T(8,128)(2,1)}, u32[]{:S(2)}, u32[]{:S(2)}) collective-permute-start(bf16[2,256,3072]{2,1,0:T(8,128)(2,1)} %get-tuple-element.109), channel_id=1, source_target_pairs={{0,8},{8,0},{1,9},{9,1},{2,10},{10,2},{3,11},{11,3},{4,12},{12,4},... | collective-permute-start | bytes 9437192 | tf_op jit(solution)/shard_map/ppermute | solution.py:338
  26.8 262.8 %collective-permute-start.2 = (bf16[2,256,3072]{2,1,0:T(8,128)(2,1)}, bf16[2,256,3072]{2,1,0:T(8,128)(2,1)}, u32[]{:S(2)}, u32[]{:S(2)}) collective-permute-start(bf16[2,256,3072]{2,1,0:T(8,128)(2,1)} %get-tuple-element.110), channel_id=1, source_target_pairs={{0,8},{8,0},{1,9},{9,1},{2,10},{10,2},{3,11},{11,3},{4,12},{12,4},... | collective-permute-start | bytes 9437192 | tf_op jit(solution)/shard_map/ppermute | solution.py:338
  41.8 77.4 %copy-start.20 = (f32[4,256]{1,0:T(4,128)}, f32[4,256]{1,0:T(4,128)S(1)}, u32[]{:S(2)}) copy-start(f32[4,256]{1,0:T(4,128)S(1)} %add_rsqrt_fusion.1) | copy-start | bytes 12292
  439.1 335.2 %reduce-scatter.5.cloned.1.call-start = ((), (), s32[]{:S(2)}) async-start(), calls=%async_computation.5 | async-start | bytes 21233664 | tf_op jit(solution)/shard_map/reduce_scatter | solution.py:399
  439.7 21.0 %collective-permute-start.4 = (f32[2,2,384,1280]{3,2,1,0:T(8,128)}, f32[2,2,384,1280]{3,2,1,0:T(8,128)}, u32[]{:S(2)}, u32[]{:S(2)}) collective-permute-start(f32[2,2,384,1280]{3,2,1,0:T(8,128)} %dynamic-slice_bitcast_fusion), channel_id=1, source_target_pairs={{0,1},{1,0},{2,3},{3,2},{4,5},{5,4},{6,7},{7,6},{8,9},{9,8},{10,11... | collective-permute-start | bytes 23592968 | tf_op jit(solution)/shard_map/ppermute | solution.py:422
  439.7 71.2 %collective-permute-start.7 = (bf16[2,256,3072]{2,1,0:T(8,128)(2,1)}, bf16[2,256,3072]{2,1,0:T(8,128)(2,1)S(1)}, u32[]{:S(2)}, u32[]{:S(2)}) collective-permute-start(bf16[2,256,3072]{2,1,0:T(8,128)(2,1)} %fusion.62), channel_id=1, source_target_pairs={{0,8},{8,0},{1,9},{9,1},{2,10},{10,2},{3,11},{11,3},{4,12},{12,4},... | collective-permute-start | bytes 9437192 | tf_op jit(solution)/shard_map/ppermute | solution.py:338
  443.4 125.3 %collective-permute-start.9 = (bf16[1,256,3072]{2,1,0:T(8,128)(2,1)}, bf16[1,256,3072]{2,1,0:T(8,128)(2,1)S(1)}, u32[]{:S(2)}, u32[]{:S(2)}) collective-permute-start(bf16[1,256,3072]{2,1,0:T(8,128)(2,1)} %get-tuple-element.113), channel_id=1, source_target_pairs={{0,8},{8,0},{1,9},{9,1},{2,10},{10,2},{3,11},{11,3},{4,12},{12,4},... | collective-permute-start | bytes 4718600 | tf_op jit(solution)/shard_map/ppermute | solution.py:338
  444.6 133.8 %collective-permute-start.10 = (bf16[1,256,3072]{2,1,0:T(8,128)(2,1)}, bf16[1,256,3072]{2,1,0:T(8,128)(2,1)S(1)}, u32[]{:S(2)}, u32[]{:S(2)}) collective-permute-start(bf16[1,256,3072]{2,1,0:T(8,128)(2,1)} %get-tuple-element.114), channel_id=1, source_target_pairs={{0,8},{8,0},{1,9},{9,1},{2,10},{10,2},{3,11},{11,3},{4,12},{12,4},... | collective-permute-start | bytes 4718600 | tf_op jit(solution)/shard_map/ppermute | solution.py:338
  449.3 162.9 %collective-permute-start.11 = (bf16[1,256,3072]{2,1,0:T(8,128)(2,1)}, bf16[1,256,3072]{2,1,0:T(8,128)(2,1)}, u32[]{:S(2)}, u32[]{:S(2)}) collective-permute-start(bf16[1,256,3072]{2,1,0:T(8,128)(2,1)} %get-tuple-element.115), channel_id=1, source_target_pairs={{0,8},{8,0},{1,9},{9,1},{2,10},{10,2},{3,11},{11,3},{4,12},{12,4},... | collective-permute-start | bytes 4718600 | tf_op jit(solution)/shard_map/ppermute | solution.py:338
  479.3 82.4 %collective-permute-start.6 = (f32[2,384,640]{2,1,0:T(8,128)}, f32[2,384,640]{2,1,0:T(8,128)}, u32[]{:S(2)}, u32[]{:S(2)}) collective-permute-start(f32[2,384,640]{2,1,0:T(8,128)} %dynamic-slice_bitcast_fusion.2), channel_id=1, source_target_pairs={{0,2},{1,3},{2,0},{3,1},{4,6},{5,7},{6,4},{7,5},{8,10},{9,11},{10,... | collective-permute-start | bytes 5898248 | tf_op jit(solution)/shard_map/ppermute | solution.py:422
  510.9 49.3 %collective-permute-start.8 = (f32[2,384,640]{2,1,0:T(8,128)}, f32[2,384,640]{2,1,0:T(8,128)}, u32[]{:S(2)}, u32[]{:S(2)}) collective-permute-start(f32[2,384,640]{2,1,0:T(8,128)} %dynamic-slice_bitcast_fusion.1), channel_id=1, source_target_pairs={{0,4},{1,5},{2,6},{3,7},{4,0},{5,1},{6,2},{7,3},{8,12},{9,13},{10,... | collective-permute-start | bytes 5898248 | tf_op jit(solution)/shard_map/ppermute | solution.py:422
  560.3 190.8 %collective-permute-start.13 = (bf16[1,256,3072]{2,1,0:T(8,128)(2,1)}, bf16[1,256,3072]{2,1,0:T(8,128)(2,1)}, u32[]{:S(2)}, u32[]{:S(2)}) collective-permute-start(bf16[1,256,3072]{2,1,0:T(8,128)(2,1)} %get-tuple-element.111), channel_id=1, source_target_pairs={{0,8},{8,0},{1,9},{9,1},{2,10},{10,2},{3,11},{11,3},{4,12},{12,4},... | collective-permute-start | bytes 4718600 | tf_op jit(solution)/shard_map/ppermute | solution.py:338
  561.7 198.8 %collective-permute-start.5 = (bf16[1,256,3072]{2,1,0:T(8,128)(2,1)}, bf16[1,256,3072]{2,1,0:T(8,128)(2,1)}, u32[]{:S(2)}, u32[]{:S(2)}) collective-permute-start(bf16[1,256,3072]{2,1,0:T(8,128)(2,1)} %get-tuple-element.112), channel_id=1, source_target_pairs={{0,8},{8,0},{1,9},{9,1},{2,10},{10,2},{3,11},{11,3},{4,12},{12,4},... | collective-permute-start | bytes 4718600 | tf_op jit(solution)/shard_map/ppermute | solution.py:338
  569.8 64.8 %slice-start.6 = ((s8[6291456]{0:T(1024)(128)(4,1)}), s8[4194304]{0:T(1024)(128)(4,1)S(1)}, s32[]{:S(2)}) async-start(s8[6291456]{0:T(1024)(128)(4,1)} %bitcast.104), calls=%async_computation.12 | async-start | bytes 8388608
  569.8 64.8 %slice-start.7 = ((s8[6291456]{0:T(1024)(128)(4,1)}), s8[2097152]{0:T(1024)(128)(4,1)S(1)}, s32[]{:S(2)}) async-start(s8[6291456]{0:T(1024)(128)(4,1)} %bitcast.104), calls=%async_computation.13 | async-start | bytes 4194304
  569.8 64.8 %copy-start.7 = (bf16[1,256,3072]{2,1,0:T(8,128)(2,1)S(1)}, bf16[1,256,3072]{2,1,0:T(8,128)(2,1)}, u32[]{:S(2)}) copy-start(bf16[1,256,3072]{2,1,0:T(8,128)(2,1)} %copy-done.6) | copy-start | bytes 4718596
  569.8 143.0 %collective-permute-start.12 = (bf16[1,256,3072]{2,1,0:T(8,128)(2,1)}, bf16[1,256,3072]{2,1,0:T(8,128)(2,1)}, u32[]{:S(2)}, u32[]{:S(2)}) collective-permute-start(bf16[1,256,3072]{2,1,0:T(8,128)(2,1)} %get-tuple-element.116), channel_id=1, source_target_pairs={{0,8},{8,0},{1,9},{9,1},{2,10},{10,2},{3,11},{11,3},{4,12},{12,4},... | collective-permute-start | bytes 4718600 | tf_op jit(solution)/shard_map/ppermute | solution.py:338
  579.5 185.9 %collective-permute-start.15 = (f32[384,640]{1,0:T(8,128)}, f32[384,640]{1,0:T(8,128)}, u32[]{:S(2)}, u32[]{:S(2)}) collective-permute-start(f32[384,640]{1,0:T(8,128)} %dynamic-slice_bitcast_fusion.5), channel_id=1, source_target_pairs={{0,2},{1,3},{2,0},{3,1},{4,6},{5,7},{6,4},{7,5},{8,10},{9,11},{10,... | collective-permute-start | bytes 2949128 | tf_op jit(solution)/shard_map/ppermute | solution.py:422
  612.2 153.2 %collective-permute-start.14 = (f32[384,640]{1,0:T(8,128)}, f32[384,640]{1,0:T(8,128)}, u32[]{:S(2)}, u32[]{:S(2)}) collective-permute-start(f32[384,640]{1,0:T(8,128)} %dynamic-slice_bitcast_fusion.6), channel_id=1, source_target_pairs={{0,4},{1,5},{2,6},{3,7},{4,0},{5,1},{6,2},{7,3},{8,12},{9,13},{10,... | collective-permute-start | bytes 2949128 | tf_op jit(solution)/shard_map/ppermute | solution.py:422
  (30 other events, 404.1 us)
Sparse Core Ops, SparseCore 0:
  11.2 84.3 all-gather.3
  97.4 56.7 all-gather.5
  439.2 142.4 reduce-scatter.2
  585.6 135.1 reduce-scatter.4

commit v3 on v2

--- a/solution.py
+++ b/solution.py
@@ -81,7 +81,7 @@
 
 
 def attention_bwd_kernel(group_size, tp_ref, own_ref, rec_ref, cos_ref, sin_ref, ga_own_ref, ga_rec_ref, *rest):
-    out_own_ref, out_rec_ref = rest[-2:]
+    out_ref = rest[-1]
     half = own_ref.shape[1]
     first = tp_ref[0] == 0
     lower, upper = pick_halves(first, own_ref[0], rec_ref[0])
@@ -126,7 +126,7 @@
     gq_up = (dot(gs_a, k_lo, TN) + dot(gs_b, k_up, TN)).astype(BF16).astype(F32)
 
     def store(index, lower_part, upper_part):
-        store_halves(first, out_own_ref, out_rec_ref, slice(index * HEAD_DIM, (index + 1) * HEAD_DIM), lower_part, upper_part)
+        store_halves(first, out_ref.at[0], out_ref.at[1], slice(index * HEAD_DIM, (index + 1) * HEAD_DIM), lower_part, upper_part)
 
     for i in range(group_size):
         part = slice(i * half, (i + 1) * half)
@@ -171,36 +171,91 @@
     )(*args)
 
 
-def attention_bwd(tp_index, qkv_own, qkv_rec, tables, ga_own, ga_rec, start, held, groups, group_size):
+def attention_bwd(tp_index, qkv_own, qkv_rec, tables, ga_own, ga_rec, start, rec_start, held, groups, group_size):
     batch, half, width = qkv_own.shape
     count = ga_rec.shape[0]
     block = width // groups
     ga_block = group_size * HEAD_DIM
-    shape = jax.ShapeDtypeStruct((batch, half, width), BF16)
+    shape = jax.ShapeDtypeStruct((2, batch, half, width), BF16)
     spec = lambda columns, offset: pl.BlockSpec((1, half, columns), lambda b, g, tp: (b + offset, 0, g))
     table = pl.BlockSpec((2 * half, HEAD_DIM), lambda b, g, tp: (0, 0))
-    in_specs = [spec(block, start), spec(block, 0), table, table, spec(ga_block, start), spec(ga_block, 0)]
+    in_specs = [spec(block, start), spec(block, rec_start), table, table, spec(ga_block, start), spec(ga_block, 0)]
     args = [tp_index, qkv_own, qkv_rec, *tables, ga_own, ga_rec]
     aliases = {}
     if held is not None:
-        in_specs += [pl.BlockSpec(memory_space=pl.ANY)] * 2
-        aliases = {len(args): 0, len(args) + 1: 1}
-        args += list(held)
+        in_specs.append(pl.BlockSpec(memory_space=pl.ANY))
+        aliases = {len(args): 0}
+        args.append(held)
     work = count * groups * group_size * half * half
     return pl.pallas_call(
         functools.partial(attention_bwd_kernel, group_size),
-        out_shape=(shape, shape),
+        out_shape=shape,
         grid_spec=pltpu.PrefetchScalarGridSpec(
             num_scalar_prefetch=1,
             grid=(count, groups),
             in_specs=in_specs,
-            out_specs=(spec(block, start), spec(block, start)),
+            out_specs=pl.BlockSpec((2, 1, half, block), lambda b, g, tp: (0, b + start, 0, g)),
         ),
         input_output_aliases=aliases,
         compiler_params=pltpu.CompilerParams(vmem_limit_bytes=48 * 2**20),
         cost_estimate=cost(work * HEAD_DIM * 30, work * 3, ga_rec, ga_rec, ga_rec, ga_rec),
         name="attention_bwd",
     )(*args)
+
+
+def split_norm_kernel(core_ref, gain_ref, own_ref, rec_a_ref, rec_b_ref, mine_ref, sent_ref):
+    kind, batch_index = pl.program_id(0), pl.program_id(1)
+    half_batch = pl.num_programs(1) // 2
+    first = core_ref[0] == 0
+
+    def put(source):
+        values = source[0].astype(F32)
+        inv_rms = lax.rsqrt(jnp.mean(values * values, axis=-1, keepdims=True) + NORM_EPS)
+        normed = values * inv_rms * gain_ref[...]
+        rows = normed.shape[1] // 8
+        for i in range(4):
+            even = normed[:, 2 * i * rows:(2 * i + 1) * rows]
+            odd = normed[:, (2 * i + 1) * rows:(2 * i + 2) * rows]
+            mine_ref[0, 0, :, i * rows:(i + 1) * rows] = jnp.where(first, even, odd).astype(BF16)
+            sent_ref[0, 0, :, i * rows:(i + 1) * rows] = jnp.where(first, odd, even).astype(BF16)
+
+    @pl.when(kind == 0)
+    def _():
+        put(own_ref)
+
+    @pl.when((kind == 1) & (batch_index < half_batch))
+    def _():
+        put(rec_a_ref)
+
+    @pl.when((kind == 1) & (batch_index >= half_batch))
+    def _():
+        put(rec_b_ref)
+
+
+def split_norm(core_index, gain, own, rec_a, rec_b, row_block=128):
+    batch, half, width = own.shape
+    part = batch // 2
+    row_block = min(row_block, half)
+    last = half // row_block - 1
+    out = jax.ShapeDtypeStruct((2, batch, half, width // 2), BF16)
+    block = (1, row_block, width)
+    own_spec = pl.BlockSpec(block, lambda k, b, r, c: (jnp.where(k == 0, b, batch - 1), jnp.where(k == 0, r, last), 0))
+    a_spec = pl.BlockSpec(block, lambda k, b, r, c: (jnp.where(k == 0, 0, jnp.minimum(b, part - 1)), jnp.where(k == 0, 0, jnp.where(b < part, r, last)), 0))
+    b_spec = pl.BlockSpec(block, lambda k, b, r, c: (jnp.where(k == 0, 0, jnp.maximum(b - part, 0)), jnp.where(k == 0, 0, jnp.where(b < part, 0, r)), 0))
+    out_spec = pl.BlockSpec((1, 1, row_block, width // 2), lambda k, b, r, c: (k, b, r, 0))
+    return pl.pallas_call(
+        split_norm_kernel,
+        out_shape=(out, out),
+        grid_spec=pltpu.PrefetchScalarGridSpec(
+            num_scalar_prefetch=1,
+            grid=(2, batch, half // row_block),
+            in_specs=[pl.BlockSpec((1, width), lambda k, b, r, c: (0, 0)), own_spec, a_spec, b_spec],
+            out_specs=(out_spec, out_spec),
+        ),
+        compiler_params=pltpu.CompilerParams(vmem_limit_bytes=40 * 2**20),
+        cost_estimate=cost(2 * batch * half * width * 400, 0, own, own, own, own),
+        name="split_norm",
+    )(core_index, gain.reshape(1, width), own, rec_a, rec_b)
 
 
 def finish_out_kernel(x_ref, near_ref, far_ref, *rest):
@@ -283,45 +338,37 @@
     )(w_query, w_key, w_value)
 
 
-def ungroup_kernel(first_ref, near_a_ref, far_a_ref, near_b_ref, far_b_ref, q_ref, k_ref, v_ref):
+def ungroup_kernel(*refs):
+    q_ref, k_ref, v_ref = refs[-3:]
     split = q_ref.shape[1]
-    group, last = pl.program_id(0), pl.num_programs(0) - 1
-
-    def put(block):
-        q_ref[...] = block[:, :split]
-        k_ref[...] = block[:, split:split + HEAD_DIM]
-        v_ref[...] = block[:, split + HEAD_DIM:]
-
-    @pl.when(group < last - 1)
-    def _():
-        put(first_ref[...])
-
-    @pl.when(group == last - 1)
-    def _():
-        put(near_a_ref[...] + far_a_ref[...])
-
-    @pl.when(group == last)
-    def _():
-        put(near_b_ref[...] + far_b_ref[...])
-
-
-def ungroup(first, terms_a, terms_b, groups):
-    rows, block = terms_a[0].shape
+    for group in range(len(refs) // 2 - 1):
+
+        @pl.when(pl.program_id(1) == group)
+        def _(group=group):
+            block = refs[2 * group][...] + refs[2 * group + 1][...]
+            q_ref[...] = block[:, :split]
+            k_ref[...] = block[:, split:split + HEAD_DIM]
+            v_ref[...] = block[:, split + HEAD_DIM:]
+
+
+def ungroup(terms, row_block=96):
+    groups = len(terms)
+    rows, block = terms[0][0].shape
     split = block - 2 * HEAD_DIM
-    row_block = rows // 2
-    spec = lambda columns: pl.BlockSpec((row_block, columns), lambda g, r: (r, g))
-    late = pl.BlockSpec((row_block, block), lambda g, r: (r, 0))
+    row_block = min(row_block, rows)
+    spec = lambda columns: pl.BlockSpec((row_block, columns), lambda r, g: (r, g))
     shape = lambda columns: jax.ShapeDtypeStruct((rows, groups * columns), F32)
+    flat = [term for pair in terms for term in pair]
     return pl.pallas_call(
         ungroup_kernel,
         out_shape=(shape(split), shape(HEAD_DIM), shape(HEAD_DIM)),
-        grid=(groups, rows // row_block),
-        in_specs=[pl.BlockSpec((row_block, block), lambda g, r: (r, jnp.minimum(g, groups - 3))), late, late, late, late],
+        grid=(rows // row_block, groups),
+        in_specs=[pl.BlockSpec((row_block, block), lambda r, g: (r, 0))] * len(flat),
         out_specs=(spec(split), spec(HEAD_DIM), spec(HEAD_DIM)),
         compiler_params=pltpu.CompilerParams(vmem_limit_bytes=32 * 2**20),
-        cost_estimate=cost(rows * block * groups * 400, 0, first, *terms_a, *terms_b, first, first),
+        cost_estimate=cost(rows * block * groups * 400, 0, *flat, *flat[:groups]),
         name="ungroup",
-    )(first, *terms_a, *terms_b)
+    )(*flat)
 
 
 CHUNKS = 2
@@ -356,8 +403,9 @@
             piece = lax.optimization_barrier(source[i * step:(i + 1) * step])
             source = after(hidden, piece)
             hidden_rec.append(exchange(piece))
-        for i in range(CHUNKS):
-            grad_rec.append(exchange(grad_out[i * step:(i + 1) * step]))
+        pieces = [(0, 2), (2, 1), (3, 1)]
+        for start, count in pieces:
+            grad_rec.append(exchange(grad_out[start:start + count]))
 
         w_qkv = regroup(w_query, w_key, w_value)
         w_qkv = lax.all_gather(w_qkv, "dp", axis=0, tiled=True)
@@ -386,69 +434,93 @@
             out_send.append(lax.optimization_barrier(mm("bse,ed->bsd", attn_rec[i * step:(i + 1) * step], w_o).astype(BF16)))
 
         ga_own = mm("bsd,ed->bse", after(grad_out, *out_send), w_o).astype(BF16)
-        normed_rec = norm(jnp.concatenate([after(piece, ga_own) for piece in hidden_rec], axis=0))
-        held = None
+        place = lax.axis_index("dp").astype(jnp.uint32)
+        core, along_x, along_y = place & 1, (place >> 1) & 1, place >> 2
+        core_index = core.astype(jnp.int32).reshape(1)
+        normed_mine, normed_sent = split_norm(core_index, gain, hidden, hidden_rec[0], after(hidden_rec[1], ga_own))
+
+        gqkv = None
         before = ga_own
-        for i in range(CHUNKS):
-            if i == CHUNKS - 1:
-                grad_wo = mm("bse,bsd->ed", attn_own, after(grad_out, *held)) + mm("bse,bsd->ed", attn_rec, jnp.concatenate(grad_rec, axis=0))
+        for i, (start, count) in enumerate(pieces):
+            if i == len(pieces) - 1:
+                grad_wo = mm("bse,bsd->ed", attn_own, after(grad_out, gqkv)) + mm("bse,bsd->ed", attn_rec, jnp.concatenate(grad_rec, axis=0))
                 before = grad_wo
             ga_rec = mm("bsd,ed->bse", after(grad_rec[i], before), w_o).astype(BF16)
-            held = attention_bwd(tp_index, qkv_own, qkv_rec[i], tables, ga_own, ga_rec, i * step, held, groups, group_size)
-        gqkv_own, gqkv_rec = held
+            gqkv = attention_bwd(tp_index, qkv_own, qkv_rec[start // step], tables, ga_own, ga_rec, start, start % step, gqkv, groups, group_size)
+            before = gqkv
         grad_wo = lax.psum_scatter(grad_wo, "dp", scatter_dimension=1, tiled=True)
 
+        cut = groups // 2 * block
+
+        def pick(values, axis, coordinate, columns=0):
+            at = [jnp.uint32(0)] * values.ndim
+            at[axis], at[-1] = coordinate, jnp.uint32(columns)
+            size = [*values.shape[:-1], block]
+            size[axis] = 1
+            return lax.squeeze(lax.dynamic_slice(values, at, size), [axis])
+
+        def pass_on(values, bit):
+            return lax.ppermute(values, "dp", [(i, i ^ bit) for i in range(8)])
+
+        def weight_grad(normed, columns, before):
+            return mm("hbsd,hbse->de", normed, after(gqkv, *before)[..., columns])
+
+        late, early = slice(cut, 2 * cut), slice(0, cut)
+        late_sent = weight_grad(normed_sent, late, [])
+        late_far = pass_on(late_sent, 1)
+        early_sent = weight_grad(normed_sent, early, [late_sent])
+        early_far = pass_on(early_sent, 1)
+
+        def first_stage(mine, far):
+            total = (mine + far).reshape(2, 2, rows_loc, cut)
+            sent = pick(total, 1, along_x ^ 1), pick(total, 0, along_y ^ 1, block)
+            sent, total = lax.optimization_barrier((sent, total))
+            mine = pick(total, 1, along_x), pick(total, 0, along_y, block)
+            return sent, mine, (pass_on(sent[0], 2), pass_on(sent[1], 4))
+
+        def second_stage(mine, far, before):
+            far = after(far, *before)
+            total = mine[0] + far[0], mine[1] + far[1]
+            sent = pick(total[0], 0, along_y ^ 1), pick(total[1], 0, along_x ^ 1)
+            sent, total = lax.optimization_barrier((sent, total))
+            mine = pick(total[0], 0, along_y), pick(total[1], 0, along_x)
+            return sent, [(mine[0], pass_on(sent[0], 4)), (mine[1], pass_on(sent[1], 2))]
+
+        late_sent, late_mine, late_far = first_stage(weight_grad(normed_mine, late, [early_sent]), late_far)
+        early_sent, early_mine, early_far = first_stage(weight_grad(normed_mine, early, late_sent), early_far)
+
+        gqkv_rec = after(gqkv, *early_sent)[1]
         dn_send = []
         for i in range(CHUNKS):
             dn_send.append(lax.optimization_barrier(mm("bse,de->bsd", gqkv_rec[i * step:(i + 1) * step], w_qkv).astype(BF16)))
 
         out_far, dn_far = [], []
         out_far.append(exchange(out_send[0]))
-        for i in range(batch):
-            dn_far.append(exchange(dn_send[i // step][i % step:i % step + 1]))
-        for i in range(step, batch):
-            out_far.append(exchange(out_send[1][i - step:i - step + 1]))
-
-        cut = groups // 2 * block
-        gqkv_own, gqkv_rec = after((gqkv_own, gqkv_rec), *dn_send)
-        late = mm("bsd,bse->de", normed_own, gqkv_own[:, :, cut:]) + mm("bsd,bse->de", normed_rec, gqkv_rec[:, :, cut:])
-        place = lax.axis_index("dp").astype(jnp.uint32)
-        core, along_x, along_y = place & 1, (place >> 1) & 1, place >> 2
-
-        def halve(values, axis, coordinate, bit):
-            theirs = lax.dynamic_index_in_dim(values, coordinate ^ 1, axis, keepdims=False)
-            theirs, values = lax.optimization_barrier((theirs, values))
-            mine = lax.dynamic_index_in_dim(values, coordinate, axis, keepdims=False)
-            return theirs, mine, lax.ppermute(theirs, "dp", [(i, i ^ bit) for i in range(8)])
-
-        late = late.reshape(2, 2, 2, rows_loc, cut)
-        sent, mine, far = halve(late, 2, core, 1)
-        gqkv_own, gqkv_rec = after((gqkv_own, gqkv_rec), sent)
-        early = mm("bsd,bse->de", normed_own, gqkv_own[:, :, :cut]) + mm("bsd,bse->de", normed_rec, gqkv_rec[:, :, :cut])
-        early_sum = lax.psum_scatter(early, "dp", scatter_dimension=0, tiled=True)
-        late = mine + after(far, early)
-        sent_x, mine_x, far_x = halve(late[..., :block], 1, along_x, 2)
-        sent_y, mine_y, far_y = halve(late[..., block:], 0, along_y, 4)
-
-        attn_own, gqkv_own = after((attn_own, gqkv_own), sent_x, sent_y)
+        out_far.append(exchange(out_send[1][:1]))
+        out_far.append(exchange(out_send[1][1:]))
+        dn_sent = [dn_send[0], dn_send[1][:1], dn_send[1][1:]]
+        for i in range(3):
+            dn_far.append(exchange(dn_sent[i]))
+
+        attn_own, gqkv = after((attn_own, gqkv), *dn_send)
         out_near = lax.optimization_barrier(mm("bse,ed->bsd", attn_own, w_o).astype(BF16))
-        dn_near = lax.optimization_barrier(mm("bse,de->bsd", gqkv_own, w_qkv).astype(BF16))
-        hidden_out = finish(finish_out_kernel, [hidden, out_near], [out_far[0]], 0, None)
-        sent_xy, mine_xy, far_xy = halve(mine_x + after(far_x, hidden_out), 0, along_y, 4)
-        sent_yx, mine_yx, far_yx = halve(mine_y + after(far_y, hidden_out), 0, along_x, 2)
-        dn_near = after(dn_near, sent_xy, sent_yx)
+        dn_near = lax.optimization_barrier(mm("bse,de->bsd", gqkv[0], w_qkv).astype(BF16))
+        late_sent, late_terms = second_stage(late_mine, late_far, [out_near, dn_near])
+        hidden_out = finish(finish_out_kernel, [hidden, after(out_near, *late_sent)], [out_far[0]], 0, None)
+        hidden_out = finish(finish_out_kernel, [hidden, out_near], [after(out_far[1], hidden_out)], 2, hidden_out)
+        early_sent, early_terms = second_stage(early_mine, early_far, [hidden_out])
+        dn_near = after(dn_near, *early_sent)
         grad_hidden = None
         gain_parts = []
-        for i in range(batch):
+        for i, (start, count) in enumerate(pieces):
             grad_hidden, part = finish(
-                finish_grad_kernel, [hidden, grad_out, dn_near], [dn_far[i]], i, grad_hidden, gain
+                finish_grad_kernel, [hidden, grad_out, dn_near], [dn_far[i]], start, grad_hidden, gain
             )
             gain_parts.append(part)
         gain_sum = lax.psum(jnp.sum(sum(gain_parts), axis=0), ("dp", "tp"))
         grad_gain = lax.dynamic_slice(gain_sum, (lax.axis_index("dp") * rows_loc,), (rows_loc,))
-        for i in range(step, batch):
-            hidden_out = finish(finish_out_kernel, [hidden, out_near], [after(out_far[i - step + 1], gain_sum, hidden_out)], i, hidden_out)
-        grad_wq, grad_wk, grad_wv = ungroup(early_sum, (mine_xy, far_xy), (mine_yx, far_yx), groups)
+        grad_wq, grad_wk, grad_wv = w_grads = ungroup([(mine, after(far, gain_sum)) for mine, far in early_terms + late_terms])
+        hidden_out = finish(finish_out_kernel, [hidden, out_near], [after(out_far[2], *w_grads)], 3, hidden_out)
         return hidden_out, grad_hidden, grad_gain, grad_wq, grad_wk, grad_wv, grad_wo
 
     act_spec = P("dp", "tp", None)

time: 786 us -> 790 us (level)
  Pallas kernels: 126 us -> 142 us
  waiting for transfers between devices: 250 us -> 239 us
  other arithmetic: 29.5 us -> 19 us
  local copies, waits for them, and re-layouts: 44 us -> 54.1 us
    ppermute x5 -> x10, waiting for transfers between devices: 36.9 us -> 10.6 us  [pass_on(): return lax.ppermute(values, 'dp', [(i, i ^ bit) for i in range(8)])]
    ppermute x11, waiting for transfers between devices: 158 us -> 176 us  [exchange(): return lax.ppermute(values, 'tp', swap)]
    pallas_call x0 -> x1, Pallas kernels: none -> 16.1 us  [split_norm(): pl.pallas_call(split_norm_kernel, out_shape=(out, out), grid_spec=pltpu.P...]
    unnamed x69 -> x99, local copies, waits for them, and re-layouts: 9.99 us -> 20.2 us
    squeeze x7 -> x12, local copies, waits for them, and re-layouts: 12.1 us -> 19.9 us  [pick(): return lax.squeeze(lax.dynamic_slice(values, at, size), [axis])]
    pallas_call x7 -> x6, Pallas kernels: 30 us -> 23.6 us  [finish(): pl.pallas_call(kernel, out_shape=out_shape, grid=(count, half // row_bloc...]
    pallas_call x2 -> x3, Pallas kernels: 50.7 us -> 54.2 us  [attention_bwd(): pl.pallas_call(functools.partial(attention_bwd_kernel, group_size), out_s...]
    dot_general x18 -> x19, matrix products: 252 us -> 252 us  [mm(): return jnp.einsum(eq, a, b, preferred_element_type=F32)]
  transfers between devices with their start and end apart: 20 -> 24, of which waited for: 10 -> 8; matrix products, arithmetic and copies ran while one was open for 25% -> 36% of each run, Pallas kernels for 12% -> 18%
where the time goes in v3:
time: 790 us; the launch traced here: 785 us
  matrix products  252 us (32%)
  waiting for transfers between devices  239 us (30%)
  Pallas kernels  142 us (18%)
  local copies, waits for them, and re-layouts  54.1 us (7%)
  blocking collectives  41.5 us (5%)
  starting transfers between devices  23.1 us (3%)
  other arithmetic  19 us (2%)
  between operations  14.4 us (2%)
    dot_general x19, matrix products, mm(): return jnp.einsum(eq, a, b, preferred_element_type=F32)  252 us
    ppermute x11, waiting for transfers between devices, exchange(): return lax.ppermute(values, 'tp', swap)  176 us
    pallas_call x3, Pallas kernels, attention_bwd(): pl.pallas_call(functools.partial(attention_bwd_kernel, group_size), out_s...  54.2 us
    all_gather x1, waiting for transfers between devices, local_block(): w_qkv = lax.all_gather(w_qkv, 'dp', axis=0, tiled=True)  51.5 us
    pallas_call x2, Pallas kernels, attention_fwd(): pl.pallas_call(functools.partial(attention_fwd_kernel, group_size), out_s...  34 us
    psum x1, blocking collectives, local_block(): gain_sum = lax.psum(jnp.sum(sum(gain_parts), axis=0), ('dp', 'tp'))  32.2 us
    pallas_call x6, Pallas kernels, finish(): pl.pallas_call(kernel, out_shape=out_shape, grid=(count, half // row_bloc...  23.6 us
    unnamed x99, local copies, waits for them, and re-layouts  20.2 us
  transfers between devices with their start and end apart: 24, of which 8 were waited for; matrix products, arithmetic and copies ran while one was open for 36% of the time, Pallas kernels for 18%

profile of v3, /device:TPU:0, one launch (start us, length us, event | category | flops | bytes accessed | tf_op | source)
XLA Modules:
  0.0 784.8 jit_solution(10929055001888370793)
XLA Ops:
  44.0 51.5 %all-gather.4.cloned.1.call-done = bf16[3072,2560]{1,0:T(8,128)(2,1)} async-done(((bf16[384,2560]{1,0:T(8,128)(2,1)}), bf16[3072,2560]{1,0:T(8,128)(2,1)}) %all-gather.4.cloned.1.call-update) | async-done | bytes 15728656 | tf_op jit(solution)/shard_map/all_gather | solution.py:411
  95.6 23.3 %fusion.47.own_ref = bf16[4,256,2560]{2,1,0:T(8,128)(2,1)} fusion(bf16[3072,2560]{1,0:T(8,128)(2,1)} %all-gather.4.cloned.1.call-done, bf16[4,256,3072]{2,1,0:T(8,128)(2,1)} %x_ref.11, f32[3072]{0:T(1024)S(1)} %bitcast.145, f32[4,256]{1,0:T(4,128)S(1)} %add_rsqrt_fusion), kind=kOutput, calls=%fused_computation.53 | convolution fusion | flops 16121331712 | bytes 27279360 | tf_op jit(solution)/shard_map/bsd,de->bse/dot_general | solution.py:388
  118.9 36.7 %collective-permute-done.1.rec_a_ref = bf16[2,256,3072]{2,1,0:T(8,128)(2,1)S(1)} collective-permute-done((bf16[2,256,3072]{2,1,0:T(8,128)(2,1)}, bf16[2,256,3072]{2,1,0:T(8,128)(2,1)S(1)}, u32[]{:S(2)}, u32[]{:S(2)}) %collective-permute-start.1) | collective-permute-done | bytes 3145760 | tf_op jit(solution)/shard_map/ppermute | solution.py:385
  168.6 17.1 %attention_fwd.2 = (bf16[4,256,1536]{2,1,0:T(8,128)(2,1)}, bf16[4,256,1536]{2,1,0:T(8,128)(2,1)}) custom-call(s32[1]{0:T(128)} %bitcast.tp_ref, bf16[4,256,2560]{2,1,0:T(8,128)(2,1)} %fusion.47.own_ref, bf16[2,256,2560]{2,1,0:T(8,128)(2,1)S(1)} %fusion.62.rec_ref, f32[512,128]{1,0:T(8,128)S(1)} %get-tuple-element.132.cos_ref, f32[512,128]{1,0:T(8,128)S(1)} %copy-done.8), custom_call_target="tpu_custom_call" | custom-call | flops 2415919104 | bytes 5242880 | tf_op jit(solution)/shard_map/attention_fwd/pallas_call | solution.py:158
  185.7 37.4 %collective-permute-done.rec_b_ref = bf16[2,256,3072]{2,1,0:T(8,128)(2,1)} collective-permute-done((bf16[2,256,3072]{2,1,0:T(8,128)(2,1)}, bf16[2,256,3072]{2,1,0:T(8,128)(2,1)}, u32[]{:S(2)}, u32[]{:S(2)}) %collective-permute-start) | collective-permute-done | bytes 3145760 | tf_op jit(solution)/shard_map/ppermute | solution.py:385
  225.7 13.0 %fusion.65.rec_ref = bf16[2,256,2560]{2,1,0:T(8,128)(2,1)S(1)} fusion(bf16[3072,2560]{1,0:T(8,128)(2,1)} %all-gather.4.cloned.1.call-done, bf16[2,256,3072]{2,1,0:T(8,128)(2,1)} %collective-permute-done.rec_b_ref, f32[2,256]{1,0:T(2,128)S(1)} %add_rsqrt_fusion.1, f32[3072]{0:T(1024)S(1)} %bitcast.147), kind=kOutput, calls=%fused_computation.65 | convolution fusion | flops 8060665856 | bytes 21510144 | tf_op jit(solution)/shard_map/bsd,de->bse/dot_general | solution.py:388
  238.7 16.9 %attention_fwd.3 = (bf16[4,256,1536]{2,1,0:T(8,128)(2,1)}, bf16[4,256,1536]{2,1,0:T(8,128)(2,1)}) custom-call(s32[1]{0:T(128)} %bitcast.tp_ref, bf16[4,256,2560]{2,1,0:T(8,128)(2,1)} %fusion.47.own_ref, bf16[2,256,2560]{2,1,0:T(8,128)(2,1)S(1)} %fusion.65.rec_ref, ...), custom_call_target="tpu_custom_call", output_to_operand_aliasing={{0}: (5, {}), {1}: (6, {})} | custom-call | flops 2415919104 | bytes 5242880 | tf_op jit(solution)/shard_map/attention_fwd/pallas_call | solution.py:158
  271.6 13.6 %fusion.80.ga_own_ref = bf16[4,256,1536]{2,1,0:T(8,128)(2,1)} fusion(bf16[4,256,3072]{2,1,0:T(8,128)(2,1)S(1)} %bitcast.144, bf16[1536,3072]{1,0:T(8,128)(2,1)} %all-gather.6.cloned.1.call-done), kind=kOutput, calls=%fused_computation.70 | convolution fusion | flops 9665249280 | bytes 18874368 | tf_op jit(solution)/shard_map/bsd,ed->bse/dot_general | solution.py:388
  299.6 25.8 %attention_bwd.3.rest_0_ = bf16[2,4,256,2560]{3,2,1,0:T(8,128)(2,1)} custom-call(s32[1]{0:T(128)} %bitcast.tp_ref, bf16[4,256,2560]{2,1,0:T(8,128)(2,1)} %fusion.47.own_ref, bf16[2,256,2560]{2,1,0:T(8,128)(2,1)S(1)} %copy-done.16, f32[512,128]{1,0:T(8,128)S(1)} %get-tuple-element.132.cos_ref, f32[512,128]{1,0:T(8,128)S(1)} %copy-done.9, ...), custom_call_target="tpu_custom_call" | custom-call | flops 6039797760 | bytes 6291456 | tf_op jit(solution)/shard_map/attention_bwd/pallas_call | solution.py:190
  332.2 13.9 %attention_bwd.4.rest_0_ = bf16[2,4,256,2560]{3,2,1,0:T(8,128)(2,1)} custom-call(s32[1]{0:T(128)} %bitcast.tp_ref, bf16[4,256,2560]{2,1,0:T(8,128)(2,1)} %fusion.47.own_ref, bf16[2,256,2560]{2,1,0:T(8,128)(2,1)S(1)} %fusion.65.rec_ref, f32[512,128]{1,0:T(8,128)S(1)} %get-tuple-element.132.cos_ref, ...), custom_call_target="tpu_custom_call", output_to_operand_aliasing={{}: (7, {})} | custom-call | flops 3019898880 | bytes 3145728 | tf_op jit(solution)/shard_map/attention_bwd/pallas_call | solution.py:190
  346.1 13.5 %fusion.107 = f32[1536,3072,1]{1,0,2:T(8,128)} fusion(bf16[4,256,1536]{2,1,0:T(8,128)(2,1)S(1)} %copy-done.32, bf16[4,256,3072]{2,1,0:T(8,128)(2,1)S(1)} %bitcast.144), kind=kOutput, calls=%fused_computation.117 | convolution fusion | flops 9663676416 | bytes 28311552 | tf_op jit(solution)/shard_map/bse,bsd->ed/dot_general | solution.py:388
  359.7 19.6 %bitcast_add_fusion = f32[1536,3072]{1,0:T(8,128)} fusion(f32[1536,3072,1]{1,0,2:T(8,128)} %fusion.107, bf16[4,256,1536]{2,1,0:T(8,128)(2,1)} %get-tuple-element.69, bf16[1,256,3072]{2,1,0:T(8,128)(2,1)} %collective-permute-done.2, bf16[1,256,3072]{2,1,0:T(8,128)(2,1)} %collective-permute-done.3, bf16[2,256,3072]{2,1,0:T(8,128)(2,1)} %collective-permute-done.4), kind=kOutput, calls=%fused_computation | convolution fusion | flops 9674686464 | bytes 47185920 | tf_op jit(solution)/shard_map/bse,bsd->ed/dot_general | solution.py:388
  386.2 14.5 %attention_bwd.5 = bf16[2,4,256,2560]{3,2,1,0:T(8,128)(2,1)} custom-call(s32[1]{0:T(128)} %bitcast.tp_ref, bf16[4,256,2560]{2,1,0:T(8,128)(2,1)} %fusion.47.own_ref, bf16[2,256,2560]{2,1,0:T(8,128)(2,1)S(1)} %fusion.65.rec_ref, f32[512,128]{1,0:T(8,128)S(1)} %get-tuple-element.132.cos_ref, f32[512,128]{1,0:T(8,128)S(1)} %copy-done.9, ...), custom_call_target="tpu_custom_call", output_to_operand_aliasing={{}: (7, {})} | custom-call | flops 3019898880 | bytes 3145728 | tf_op jit(solution)/shard_map/attention_bwd/pallas_call | solution.py:190
  400.7 16.1 %split_norm.1 = (bf16[2,4,256,1536]{3,2,1,0:T(8,128)(2,1)S(1)}, bf16[2,4,256,1536]{3,2,1,0:T(8,128)(2,1)}) custom-call(s32[1]{0:T(128)} %bitcast.10.core_ref, f32[1,3072]{1,0:T(1,128)S(1)} %bitcast.148, bf16[4,256,3072]{2,1,0:T(8,128)(2,1)} %x_ref.11, bf16[2,256,3072]{2,1,0:T(8,128)(2,1)S(1)} %copy-done.7, bf16[2,256,3072]{2,1,0:T(8,128)(2,1)} %collective-permute-done.rec_b_ref), custom_call_target="tpu_custom_call" | custom-call | flops 2516582400 | bytes 25165824 | tf_op jit(solution)/shard_map/split_norm/pallas_call | solution.py:246
  416.8 16.5 %convolution_bitcast_fusion.3 = f32[1536,1280]{1,0:T(8,128)} fusion(bf16[2,4,256,1536]{3,2,1,0:T(8,128)(2,1)} %get-tuple-element.77, bf16[2,4,256,2560]{3,2,1,0:T(8,128)(2,1)} %attention_bwd.5), kind=kOutput, calls=%fused_computation.33 | convolution fusion | flops 8053063680 | bytes 19398656 | tf_op jit(solution)/shard_map/hbsd,hbse->de/dot_general | solution.py:388
  448.9 13.3 %fusion.26 = f32[1536,1280]{1,0:T(8,128)S(1)} fusion(f32[1536,1280]{1,0:T(8,128)} %collective-permute-done.5, bf16[2,4,256,1536]{3,2,1,0:T(8,128)(2,1)S(1)} %copy-done.22, bf16[2,4,256,2560]{3,2,1,0:T(8,128)(2,1)} %attention_bwd.5), kind=kOutput, calls=%fused_computation.31 | convolution fusion | flops 8055029760 | bytes 27262976 | tf_op jit(solution)/shard_map/hbsd,hbse->de/dot_general | solution.py:388
  468.8 13.3 %fusion.25 = f32[1536,1280]{1,0:T(8,128)S(1)} fusion(f32[1536,1280]{1,0:T(8,128)} %collective-permute-done.6, bf16[2,4,256,1536]{3,2,1,0:T(8,128)(2,1)S(1)} %copy-done.22, bf16[2,4,256,2560]{3,2,1,0:T(8,128)(2,1)} %attention_bwd.5), kind=kOutput, calls=%fused_computation.29 | convolution fusion | flops 8055029760 | bytes 27262976 | tf_op jit(solution)/shard_map/hbsd,hbse->de/dot_general | solution.py:388
  486.1 13.9 %fusion.71 = bf16[2,256,3072]{2,1,0:T(8,128)(2,1)} fusion(bf16[3072,2560]{1,0:T(8,128)(2,1)} %all-gather.4.cloned.1.call-done, bf16[2,4,256,2560]{3,2,1,0:T(8,128)(2,1)} %attention_bwd.5), kind=kOutput, calls=%fused_computation.67 | convolution fusion | flops 8054636544 | bytes 21495808 | tf_op jit(solution)/shard_map/bse,de->bsd/dot_general | solution.py:388
  500.1 14.0 %fusion.68 = bf16[2,256,3072]{2,1,0:T(8,128)(2,1)} fusion(bf16[3072,2560]{1,0:T(8,128)(2,1)} %all-gather.4.cloned.1.call-done, bf16[2,4,256,2560]{3,2,1,0:T(8,128)(2,1)} %attention_bwd.5), kind=kOutput, calls=%fused_computation.66 | convolution fusion | flops 8054636544 | bytes 21495808 | tf_op jit(solution)/shard_map/bse,de->bsd/dot_general | solution.py:388
  514.1 22.5 %fusion.44.near_ref = bf16[4,256,3072]{2,1,0:T(8,128)(2,1)} fusion(bf16[3072,2560]{1,0:T(8,128)(2,1)} %all-gather.4.cloned.1.call-done, bf16[2,4,256,2560]{3,2,1,0:T(8,128)(2,1)} %attention_bwd.5), kind=kOutput, calls=%fused_computation.52 | convolution fusion | flops 16109273088 | bytes 27262976 | tf_op jit(solution)/shard_map/bse,de->bsd/dot_general | solution.py:388
  554.3 12.7 %fusion.41.near_ref = bf16[4,256,3072]{2,1,0:T(8,128)(2,1)S(1)} fusion(bf16[4,256,1536]{2,1,0:T(8,128)(2,1)S(1)} %copy-done.33, bf16[1536,3072]{1,0:T(8,128)(2,1)} %all-gather.6.cloned.1.call-done), kind=kOutput, calls=%fused_computation.51 | convolution fusion | flops 9666822144 | bytes 18874368 | tf_op jit(solution)/shard_map/bse,ed->bsd/dot_general | solution.py:388
  600.6 54.9 %collective-permute-done.16.far_ref = bf16[1,256,3072]{2,1,0:T(8,128)(2,1)S(1)} collective-permute-done((bf16[1,256,3072]{2,1,0:T(8,128)(2,1)}, bf16[1,256,3072]{2,1,0:T(8,128)(2,1)S(1)}, u32[]{:S(2)}, u32[]{:S(2)}) %collective-permute-start.16) | collective-permute-done | bytes 1572896 | tf_op jit(solution)/shard_map/ppermute | solution.py:385
  657.2 32.1 %collective-permute-done.17.far_ref = bf16[1,256,3072]{2,1,0:T(8,128)(2,1)S(1)} collective-permute-done((bf16[1,256,3072]{2,1,0:T(8,128)(2,1)}, bf16[1,256,3072]{2,1,0:T(8,128)(2,1)S(1)}, u32[]{:S(2)}, u32[]{:S(2)}) %collective-permute-start.17) | collective-permute-done | bytes 1572896 | tf_op jit(solution)/shard_map/ppermute | solution.py:385
  722.3 32.2 %psum.7 = f32[3072]{0:T(1024)S(1)} all-reduce(f32[3072]{0:T(1024)S(1)} %add_reduce_fusion), channel_id=1, replica_groups=mesh['tp'=2,'dp'=8] {'dp','tp'}, use_global_device_ids=true, to_apply=%region_4.0 | all-reduce | flops 3072 | bytes 24576 | tf_op jit(solution)/shard_map/psum | solution.py:520
  (198 shorter events, 231.7 us)
Async XLA Ops:
  7.2 88.4 %all-gather.4.cloned.1.call-start = ((), (), s32[]{:S(2)}) async-start(), calls=%async_computation.1 | async-start | bytes 17694720 | tf_op jit(solution)/shard_map/all_gather | solution.py:411
  11.0 244.6 %all-gather.6.cloned.1.call-start = ((), (), s32[]{:S(2)}) async-start(), calls=%async_computation.2 | async-start | bytes 10616832 | tf_op jit(solution)/shard_map/all_gather | solution.py:412
  11.8 766.2 %reduce-scatter.2.cloned.1.call-start = ((), (), s32[]{:S(2)}) async-start(), calls=%async_computation.3 | async-start | bytes 21233664 | tf_op jit(solution)/shard_map/reduce_scatter | solution.py:451
  15.8 309.6 %collective-permute-start.3 = (bf16[1,256,3072]{2,1,0:T(8,128)(2,1)}, bf16[1,256,3072]{2,1,0:T(8,128)(2,1)}, u32[]{:S(2)}, u32[]{:S(2)}) collective-permute-start(bf16[1,256,3072]{2,1,0:T(8,128)(2,1)} %get-tuple-element.123), channel_id=1, source_target_pairs={{0,8},{8,0},{1,9},{9,1},{2,10},{10,2},{3,11},{11,3},{4,12},{12,4},... | collective-permute-start | bytes 4718600 | tf_op jit(solution)/shard_map/ppermute | solution.py:385
  19.1 340.6 %collective-permute-start.2 = (bf16[1,256,3072]{2,1,0:T(8,128)(2,1)}, bf16[1,256,3072]{2,1,0:T(8,128)(2,1)}, u32[]{:S(2)}, u32[]{:S(2)}) collective-permute-start(bf16[1,256,3072]{2,1,0:T(8,128)(2,1)} %get-tuple-element.124), channel_id=1, source_target_pairs={{0,8},{8,0},{1,9},{9,1},{2,10},{10,2},{3,11},{11,3},{4,12},{12,4},... | collective-permute-start | bytes 4718600 | tf_op jit(solution)/shard_map/ppermute | solution.py:385
  21.0 134.6 %collective-permute-start.1 = (bf16[2,256,3072]{2,1,0:T(8,128)(2,1)}, bf16[2,256,3072]{2,1,0:T(8,128)(2,1)S(1)}, u32[]{:S(2)}, u32[]{:S(2)}) collective-permute-start(bf16[2,256,3072]{2,1,0:T(8,128)(2,1)} %slice.63), channel_id=1, source_target_pairs={{0,8},{8,0},{1,9},{9,1},{2,10},{10,2},{3,11},{11,3},{4,12},{12,4},... | collective-permute-start | bytes 9437192 | tf_op jit(solution)/shard_map/ppermute | solution.py:385
  24.8 198.3 %collective-permute-start = (bf16[2,256,3072]{2,1,0:T(8,128)(2,1)}, bf16[2,256,3072]{2,1,0:T(8,128)(2,1)}, u32[]{:S(2)}, u32[]{:S(2)}) collective-permute-start(bf16[2,256,3072]{2,1,0:T(8,128)(2,1)} %slice.64), channel_id=1, source_target_pairs={{0,8},{8,0},{1,9},{9,1},{2,10},{10,2},{3,11},{11,3},{4,12},{12,4},... | collective-permute-start | bytes 9437192 | tf_op jit(solution)/shard_map/ppermute | solution.py:385
  26.8 262.9 %collective-permute-start.4 = (bf16[2,256,3072]{2,1,0:T(8,128)(2,1)}, bf16[2,256,3072]{2,1,0:T(8,128)(2,1)}, u32[]{:S(2)}, u32[]{:S(2)}) collective-permute-start(bf16[2,256,3072]{2,1,0:T(8,128)(2,1)} %slice.69), channel_id=1, source_target_pairs={{0,8},{8,0},{1,9},{9,1},{2,10},{10,2},{3,11},{11,3},{4,12},{12,4},... | collective-permute-start | bytes 9437192 | tf_op jit(solution)/shard_map/ppermute | solution.py:385
  433.3 15.6 %collective-permute-start.5 = (f32[1536,1280]{1,0:T(8,128)}, f32[1536,1280]{1,0:T(8,128)}, u32[]{:S(2)}, u32[]{:S(2)}) collective-permute-start(f32[1536,1280]{1,0:T(8,128)} %convolution_bitcast_fusion.3), channel_id=1, source_target_pairs={{0,1},{1,0},{2,3},{3,2},{4,5},{5,4},{6,7},{7,6},{8,9},{9,8},{10,11... | collective-permute-start | bytes 23592968 | tf_op jit(solution)/shard_map/ppermute | solution.py:463
  444.5 24.4 %collective-permute-start.6 = (f32[1536,1280]{1,0:T(8,128)}, f32[1536,1280]{1,0:T(8,128)}, u32[]{:S(2)}, u32[]{:S(2)}) collective-permute-start(f32[1536,1280]{1,0:T(8,128)} %convolution_bitcast_fusion.2), channel_id=1, source_target_pairs={{0,1},{1,0},{2,3},{3,2},{4,5},{5,4},{6,7},{7,6},{8,9},{9,8},{10,11... | collective-permute-start | bytes 23592968 | tf_op jit(solution)/shard_map/ppermute | solution.py:463
  445.0 105.7 %collective-permute-start.13 = (bf16[2,256,3072]{2,1,0:T(8,128)(2,1)}, bf16[2,256,3072]{2,1,0:T(8,128)(2,1)S(1)}, u32[]{:S(2)}, u32[]{:S(2)}) collective-permute-start(bf16[2,256,3072]{2,1,0:T(8,128)(2,1)} %fusion.74), channel_id=1, source_target_pairs={{0,8},{8,0},{1,9},{9,1},{2,10},{10,2},{3,11},{11,3},{4,12},{12,4},... | collective-permute-start | bytes 9437192 | tf_op jit(solution)/shard_map/ppermute | solution.py:385
  448.8 100.3 %collective-permute-start.10 = (bf16[1,256,3072]{2,1,0:T(8,128)(2,1)}, bf16[1,256,3072]{2,1,0:T(8,128)(2,1)S(1)}, u32[]{:S(2)}, u32[]{:S(2)}) collective-permute-start(bf16[1,256,3072]{2,1,0:T(8,128)(2,1)} %get-tuple-element.127), channel_id=1, source_target_pairs={{0,8},{8,0},{1,9},{9,1},{2,10},{10,2},{3,11},{11,3},{4,12},{12,4},... | collective-permute-start | bytes 4718600 | tf_op jit(solution)/shard_map/ppermute | solution.py:385
  465.7 86.6 %collective-permute-start.11 = (f32[2,384,640]{2,1,0:T(8,128)}, f32[2,384,640]{2,1,0:T(8,128)}, u32[]{:S(2)}, u32[]{:S(2)}) collective-permute-start(f32[2,384,640]{2,1,0:T(8,128)} %dynamic-slice_bitcast_fusion.3), channel_id=1, source_target_pairs={{0,2},{1,3},{2,0},{3,1},{4,6},{5,7},{6,4},{7,5},{8,10},{9,11},{10,... | collective-permute-start | bytes 5898248 | tf_op jit(solution)/shard_map/ppermute | solution.py:463
  467.5 85.2 %collective-permute-start.12 = (f32[2,384,640]{2,1,0:T(8,128)}, f32[2,384,640]{2,1,0:T(8,128)}, u32[]{:S(2)}, u32[]{:S(2)}) collective-permute-start(f32[2,384,640]{2,1,0:T(8,128)} %dynamic-slice_bitcast_fusion.2), channel_id=1, source_target_pairs={{0,4},{1,5},{2,6},{3,7},{4,0},{5,1},{6,2},{7,3},{8,12},{9,13},{10,... | collective-permute-start | bytes 5898248 | tf_op jit(solution)/shard_map/ppermute | solution.py:463
  485.6 96.7 %collective-permute-start.8 = (f32[2,384,640]{2,1,0:T(8,128)}, f32[2,384,640]{2,1,0:T(8,128)}, u32[]{:S(2)}, u32[]{:S(2)}) collective-permute-start(f32[2,384,640]{2,1,0:T(8,128)} %dynamic-slice_bitcast_fusion.1), channel_id=1, source_target_pairs={{0,2},{1,3},{2,0},{3,1},{4,6},{5,7},{6,4},{7,5},{8,10},{9,11},{10,... | collective-permute-start | bytes 5898248 | tf_op jit(solution)/shard_map/ppermute | solution.py:463
  549.1 44.3 %collective-permute-start.9 = (f32[2,384,640]{2,1,0:T(8,128)S(1)}, f32[2,384,640]{2,1,0:T(8,128)}, u32[]{:S(2)}, u32[]{:S(2)}) collective-permute-start(f32[2,384,640]{2,1,0:T(8,128)S(1)} %copy-done.34), channel_id=1, source_target_pairs={{0,4},{1,5},{2,6},{3,7},{4,0},{5,1},{6,2},{7,3},{8,12},{9,13},{10,... | collective-permute-start | bytes 5898248 | tf_op jit(solution)/shard_map/ppermute | solution.py:463
  550.7 141.2 %collective-permute-start.15 = (bf16[2,256,3072]{2,1,0:T(8,128)(2,1)}, bf16[2,256,3072]{2,1,0:T(8,128)(2,1)S(1)}, u32[]{:S(2)}, u32[]{:S(2)}) collective-permute-start(bf16[2,256,3072]{2,1,0:T(8,128)(2,1)} %fusion.68), channel_id=1, source_target_pairs={{0,8},{8,0},{1,9},{9,1},{2,10},{10,2},{3,11},{11,3},{4,12},{12,4},... | collective-permute-start | bytes 9437192 | tf_op jit(solution)/shard_map/ppermute | solution.py:385
  552.3 103.3 %collective-permute-start.16 = (bf16[1,256,3072]{2,1,0:T(8,128)(2,1)}, bf16[1,256,3072]{2,1,0:T(8,128)(2,1)S(1)}, u32[]{:S(2)}, u32[]{:S(2)}) collective-permute-start(bf16[1,256,3072]{2,1,0:T(8,128)(2,1)} %get-tuple-element.125), channel_id=1, source_target_pairs={{0,8},{8,0},{1,9},{9,1},{2,10},{10,2},{3,11},{11,3},{4,12},{12,4},... | collective-permute-start | bytes 4718600 | tf_op jit(solution)/shard_map/ppermute | solution.py:385
  552.7 136.6 %collective-permute-start.17 = (bf16[1,256,3072]{2,1,0:T(8,128)(2,1)}, bf16[1,256,3072]{2,1,0:T(8,128)(2,1)S(1)}, u32[]{:S(2)}, u32[]{:S(2)}) collective-permute-start(bf16[1,256,3072]{2,1,0:T(8,128)(2,1)} %get-tuple-element.126), channel_id=1, source_target_pairs={{0,8},{8,0},{1,9},{9,1},{2,10},{10,2},{3,11},{11,3},{4,12},{12,4},... | collective-permute-start | bytes 4718600 | tf_op jit(solution)/shard_map/ppermute | solution.py:385
  582.4 185.5 %collective-permute-start.7 = (bf16[1,256,3072]{2,1,0:T(8,128)(2,1)}, bf16[1,256,3072]{2,1,0:T(8,128)(2,1)}, u32[]{:S(2)}, u32[]{:S(2)}) collective-permute-start(bf16[1,256,3072]{2,1,0:T(8,128)(2,1)} %get-tuple-element.128), channel_id=1, source_target_pairs={{0,8},{8,0},{1,9},{9,1},{2,10},{10,2},{3,11},{11,3},{4,12},{12,4},... | collective-permute-start | bytes 4718600 | tf_op jit(solution)/shard_map/ppermute | solution.py:385
  593.3 161.2 %collective-permute-start.20 = (f32[384,640]{1,0:T(8,128)}, f32[384,640]{1,0:T(8,128)}, u32[]{:S(2)}, u32[]{:S(2)}) collective-permute-start(f32[384,640]{1,0:T(8,128)} %dynamic-slice_bitcast_fusion.10), channel_id=1, source_target_pairs={{0,2},{1,3},{2,0},{3,1},{4,6},{5,7},{6,4},{7,5},{8,10},{9,11},{10,... | collective-permute-start | bytes 2949128 | tf_op jit(solution)/shard_map/ppermute | solution.py:463
  656.8 97.7 %collective-permute-start.19 = (f32[384,640]{1,0:T(8,128)}, f32[384,640]{1,0:T(8,128)}, u32[]{:S(2)}, u32[]{:S(2)}) collective-permute-start(f32[384,640]{1,0:T(8,128)} %dynamic-slice_bitcast_fusion.11), channel_id=1, source_target_pairs={{0,4},{1,5},{2,6},{3,7},{4,0},{5,1},{6,2},{7,3},{8,12},{9,13},{10,... | collective-permute-start | bytes 2949128 | tf_op jit(solution)/shard_map/ppermute | solution.py:463
  690.4 64.1 %collective-permute-start.18 = (f32[384,640]{1,0:T(8,128)}, f32[384,640]{1,0:T(8,128)}, u32[]{:S(2)}, u32[]{:S(2)}) collective-permute-start(f32[384,640]{1,0:T(8,128)} %dynamic-slice_bitcast_fusion.8), channel_id=1, source_target_pairs={{0,2},{1,3},{2,0},{3,1},{4,6},{5,7},{6,4},{7,5},{8,10},{9,11},{10,... | collective-permute-start | bytes 2949128 | tf_op jit(solution)/shard_map/ppermute | solution.py:463
  693.6 60.9 %collective-permute-start.14 = (f32[384,640]{1,0:T(8,128)}, f32[384,640]{1,0:T(8,128)}, u32[]{:S(2)}, u32[]{:S(2)}) collective-permute-start(f32[384,640]{1,0:T(8,128)} %dynamic-slice_bitcast_fusion.9), channel_id=1, source_target_pairs={{0,4},{1,5},{2,6},{3,7},{4,0},{5,1},{6,2},{7,3},{8,12},{9,13},{10,... | collective-permute-start | bytes 2949128 | tf_op jit(solution)/shard_map/ppermute | solution.py:463
  (49 other events, 821.3 us)
Sparse Core Ops, SparseCore 0:
  11.2 84.3 all-gather.3
  97.4 56.7 all-gather.5
  379.5 147.2 reduce-scatter.1

commit v4 on v3

--- a/solution.py
+++ b/solution.py
@@ -203,59 +203,100 @@
     )(*args)
 
 
-def split_norm_kernel(core_ref, gain_ref, own_ref, rec_a_ref, rec_b_ref, mine_ref, sent_ref):
-    kind, batch_index = pl.program_id(0), pl.program_id(1)
-    half_batch = pl.num_programs(1) // 2
+def split_norm_kernel(core_ref, gain_ref, source_ref, *rest):
+    mine_ref, sent_ref = rest[-2:]
     first = core_ref[0] == 0
-
-    def put(source):
-        values = source[0].astype(F32)
-        inv_rms = lax.rsqrt(jnp.mean(values * values, axis=-1, keepdims=True) + NORM_EPS)
-        normed = values * inv_rms * gain_ref[...]
-        rows = normed.shape[1] // 8
-        for i in range(4):
-            even = normed[:, 2 * i * rows:(2 * i + 1) * rows]
-            odd = normed[:, (2 * i + 1) * rows:(2 * i + 2) * rows]
-            mine_ref[0, 0, :, i * rows:(i + 1) * rows] = jnp.where(first, even, odd).astype(BF16)
-            sent_ref[0, 0, :, i * rows:(i + 1) * rows] = jnp.where(first, odd, even).astype(BF16)
-
-    @pl.when(kind == 0)
-    def _():
-        put(own_ref)
-
-    @pl.when((kind == 1) & (batch_index < half_batch))
-    def _():
-        put(rec_a_ref)
-
-    @pl.when((kind == 1) & (batch_index >= half_batch))
-    def _():
-        put(rec_b_ref)
-
-
-def split_norm(core_index, gain, own, rec_a, rec_b, row_block=128):
-    batch, half, width = own.shape
-    part = batch // 2
+    values = source_ref[0].astype(F32)
+    inv_rms = lax.rsqrt(jnp.mean(values * values, axis=-1, keepdims=True) + NORM_EPS)
+    normed = values * inv_rms * gain_ref[...]
+    rows = normed.shape[1] // 8
+    for i in range(4):
+        even = normed[:, 2 * i * rows:(2 * i + 1) * rows]
+        odd = normed[:, (2 * i + 1) * rows:(2 * i + 2) * rows]
+        mine_ref[0, 0, :, i * rows:(i + 1) * rows] = jnp.where(first, even, odd).astype(BF16)
+        sent_ref[0, 0, :, i * rows:(i + 1) * rows] = jnp.where(first, odd, even).astype(BF16)
+
+
+def split_norm(core_index, gain, source, kind, start, batch, held, row_block=128):
+    count, half, width = source.shape
     row_block = min(row_block, half)
-    last = half // row_block - 1
     out = jax.ShapeDtypeStruct((2, batch, half, width // 2), BF16)
-    block = (1, row_block, width)
-    own_spec = pl.BlockSpec(block, lambda k, b, r, c: (jnp.where(k == 0, b, batch - 1), jnp.where(k == 0, r, last), 0))
-    a_spec = pl.BlockSpec(block, lambda k, b, r, c: (jnp.where(k == 0, 0, jnp.minimum(b, part - 1)), jnp.where(k == 0, 0, jnp.where(b < part, r, last)), 0))
-    b_spec = pl.BlockSpec(block, lambda k, b, r, c: (jnp.where(k == 0, 0, jnp.maximum(b - part, 0)), jnp.where(k == 0, 0, jnp.where(b < part, 0, r)), 0))
-    out_spec = pl.BlockSpec((1, 1, row_block, width // 2), lambda k, b, r, c: (k, b, r, 0))
+    out_spec = pl.BlockSpec((1, 1, row_block, width // 2), lambda b, r, c: (kind, b + start, r, 0))
+    in_specs = [pl.BlockSpec((1, width), lambda b, r, c: (0, 0)), pl.BlockSpec((1, row_block, width), lambda b, r, c: (b, r, 0))]
+    args = [core_index, gain.reshape(1, width), source]
+    aliases = {}
+    if held is not None:
+        in_specs += [pl.BlockSpec(memory_space=pl.ANY)] * 2
+        aliases = {len(args): 0, len(args) + 1: 1}
+        args += list(held)
     return pl.pallas_call(
         split_norm_kernel,
         out_shape=(out, out),
         grid_spec=pltpu.PrefetchScalarGridSpec(
-            num_scalar_prefetch=1,
-            grid=(2, batch, half // row_block),
-            in_specs=[pl.BlockSpec((1, width), lambda k, b, r, c: (0, 0)), own_spec, a_spec, b_spec],
-            out_specs=(out_spec, out_spec),
+            num_scalar_prefetch=1, grid=(count, half // row_block), in_specs=in_specs, out_specs=(out_spec, out_spec)
         ),
-        compiler_params=pltpu.CompilerParams(vmem_limit_bytes=40 * 2**20),
-        cost_estimate=cost(2 * batch * half * width * 400, 0, own, own, own, own),
+        input_output_aliases=aliases,
+        compiler_params=pltpu.CompilerParams(vmem_limit_bytes=32 * 2**20),
+        cost_estimate=cost(count * half * width * 400, 0, source, source),
         name="split_norm",
-    )(core_index, gain.reshape(1, width), own, rec_a, rec_b)
+    )(*args)
+
+
+def gain_sum_kernel(tp_size, dp_size, part_ref, out_ref, slots, send_sem, recv_sem):
+    total = tp_size * dp_size
+    me_dp = lax.axis_index("dp")
+    me = lax.axis_index("tp") * dp_size + me_dp
+
+    def place(index):
+        return (index // dp_size, lax.rem(index, dp_size))
+
+    barrier = pltpu.get_barrier_semaphore()
+    for offset in range(1, total):
+        pl.semaphore_signal(barrier, inc=1, device_id=place(lax.rem(me + offset, total)), device_id_type=pl.DeviceIdType.MESH)
+    pl.semaphore_wait(barrier, total - 1)
+
+    def copy(offset, slot, target):
+        return pltpu.make_async_remote_copy(
+            src_ref=part_ref.at[place(target)[1]],
+            dst_ref=slots.at[slot],
+            send_sem=send_sem.at[offset],
+            recv_sem=recv_sem.at[slot],
+            device_id=place(target),
+            device_id_type=pl.DeviceIdType.MESH,
+        )
+
+    for offset in range(1, total):
+        copy(offset, me, lax.rem(me + offset, total)).start()
+    slots[me] = part_ref[me_dp]
+    for offset in range(1, total):
+        copy(offset, me, lax.rem(me + offset, total)).wait_send()
+        copy(offset, lax.rem(me + total - offset, total), me).wait_recv()
+    result = slots[0]
+    for i in range(1, total):
+        result = result + slots[i]
+    out_ref[...] = result
+
+
+def gain_sum(part, tp_size, dp_size):
+    rows = part.shape[0] // dp_size
+    tile = 8 * HEAD_DIM
+    padded = jnp.pad(part.reshape(dp_size, rows), ((0, 0), (0, -rows % tile))).reshape(dp_size, -1, HEAD_DIM)
+    sublanes = padded.shape[1]
+    total = tp_size * dp_size
+    result = pl.pallas_call(
+        functools.partial(gain_sum_kernel, tp_size, dp_size),
+        out_shape=jax.ShapeDtypeStruct((sublanes, HEAD_DIM), F32),
+        in_specs=[pl.BlockSpec(memory_space=pltpu.VMEM)],
+        out_specs=pl.BlockSpec(memory_space=pltpu.VMEM),
+        scratch_shapes=[
+            pltpu.VMEM((total, sublanes, HEAD_DIM), F32),
+            pltpu.SemaphoreType.DMA((total,)),
+            pltpu.SemaphoreType.DMA((total,)),
+        ],
+        compiler_params=pltpu.CompilerParams(collective_id=0, has_side_effects=True),
+        name="gain_sum",
+    )(padded)
+    return result.reshape(-1)[:rows]
 
 
 def finish_out_kernel(x_ref, near_ref, far_ref, *rest):
@@ -338,10 +379,10 @@
     )(w_query, w_key, w_value)
 
 
-def ungroup_kernel(*refs):
+def ungroup_kernel(count, *refs):
     q_ref, k_ref, v_ref = refs[-3:]
     split = q_ref.shape[1]
-    for group in range(len(refs) // 2 - 1):
+    for group in range(count):
 
         @pl.when(pl.program_id(1) == group)
         def _(group=group):
@@ -351,24 +392,31 @@
             v_ref[...] = block[:, split + HEAD_DIM:]
 
 
-def ungroup(terms, row_block=96):
-    groups = len(terms)
+def ungroup(terms, start, groups, held, row_block=192):
     rows, block = terms[0][0].shape
     split = block - 2 * HEAD_DIM
     row_block = min(row_block, rows)
-    spec = lambda columns: pl.BlockSpec((row_block, columns), lambda r, g: (r, g))
+    spec = lambda columns: pl.BlockSpec((row_block, columns), lambda r, g: (r, g + start))
     shape = lambda columns: jax.ShapeDtypeStruct((rows, groups * columns), F32)
-    flat = [term for pair in terms for term in pair]
+    args = [term for pair in terms for term in pair]
+    in_specs = [pl.BlockSpec((row_block, block), lambda r, g: (r, 0))] * len(args)
+    estimate = cost(rows * block * len(terms) * 400, 0, *args, *args[:len(terms)])
+    aliases = {}
+    if held is not None:
+        in_specs += [pl.BlockSpec(memory_space=pl.ANY)] * 3
+        aliases = {len(args) + i: i for i in range(3)}
+        args += list(held)
     return pl.pallas_call(
-        ungroup_kernel,
+        functools.partial(ungroup_kernel, len(terms)),
         out_shape=(shape(split), shape(HEAD_DIM), shape(HEAD_DIM)),
-        grid=(rows // row_block, groups),
-        in_specs=[pl.BlockSpec((row_block, block), lambda r, g: (r, 0))] * len(flat),
+        grid=(rows // row_block, len(terms)),
+        in_specs=in_specs,
         out_specs=(spec(split), spec(HEAD_DIM), spec(HEAD_DIM)),
+        input_output_aliases=aliases,
         compiler_params=pltpu.CompilerParams(vmem_limit_bytes=32 * 2**20),
-        cost_estimate=cost(rows * block * groups * 400, 0, *flat, *flat[:groups]),
+        cost_estimate=estimate,
         name="ungroup",
-    )(*flat)
+    )(*args)
 
 
 CHUNKS = 2
@@ -417,6 +465,14 @@
             inv_rms = lax.rsqrt(jnp.mean(values * values, axis=-1, keepdims=True) + NORM_EPS)
             return (values * inv_rms * gain).astype(BF16)
 
+        place = lax.axis_index("dp").astype(jnp.uint32)
+        core, along_x, along_y = place & 1, (place >> 1) & 1, place >> 2
+        core_index = core.astype(jnp.int32).reshape(1)
+        split = split_norm(core_index, gain, hidden, 0, 0, batch, None)
+        for i in range(CHUNKS):
+            split = split_norm(core_index, gain, hidden_rec[i], 1, i * step, batch, split)
+        normed_mine, normed_sent = split
+
         normed_own = norm(hidden)
         qkv_own = mm("bsd,de->bse", normed_own, w_qkv).astype(BF16)
         qkv_rec = []
@@ -434,11 +490,6 @@
             out_send.append(lax.optimization_barrier(mm("bse,ed->bsd", attn_rec[i * step:(i + 1) * step], w_o).astype(BF16)))
 
         ga_own = mm("bsd,ed->bse", after(grad_out, *out_send), w_o).astype(BF16)
-        place = lax.axis_index("dp").astype(jnp.uint32)
-        core, along_x, along_y = place & 1, (place >> 1) & 1, place >> 2
-        core_index = core.astype(jnp.int32).reshape(1)
-        normed_mine, normed_sent = split_norm(core_index, gain, hidden, hidden_rec[0], after(hidden_rec[1], ga_own))
-
         gqkv = None
         before = ga_own
         for i, (start, count) in enumerate(pieces):
@@ -486,41 +537,43 @@
             mine = pick(total[0], 0, along_y), pick(total[1], 0, along_x)
             return sent, [(mine[0], pass_on(sent[0], 4)), (mine[1], pass_on(sent[1], 2))]
 
-        late_sent, late_mine, late_far = first_stage(weight_grad(normed_mine, late, [early_sent]), late_far)
-        early_sent, early_mine, early_far = first_stage(weight_grad(normed_mine, early, late_sent), early_far)
-
-        gqkv_rec = after(gqkv, *early_sent)[1]
+        gqkv_rec = after(gqkv, early_sent)[1]
         dn_send = []
         for i in range(CHUNKS):
             dn_send.append(lax.optimization_barrier(mm("bse,de->bsd", gqkv_rec[i * step:(i + 1) * step], w_qkv).astype(BF16)))
 
         out_far, dn_far = [], []
-        out_far.append(exchange(out_send[0]))
-        out_far.append(exchange(out_send[1][:1]))
-        out_far.append(exchange(out_send[1][1:]))
+        for i in range(CHUNKS):
+            out_far.append(exchange(out_send[i]))
         dn_sent = [dn_send[0], dn_send[1][:1], dn_send[1][1:]]
         for i in range(3):
             dn_far.append(exchange(dn_sent[i]))
 
-        attn_own, gqkv = after((attn_own, gqkv), *dn_send)
+        late_sent, late_mine, late_far = first_stage(weight_grad(normed_mine, late, dn_send), late_far)
+        early_sent, early_mine, early_far = first_stage(weight_grad(normed_mine, early, late_sent), early_far)
+
+        attn_own, gqkv = after((attn_own, gqkv), *early_sent)
         out_near = lax.optimization_barrier(mm("bse,ed->bsd", attn_own, w_o).astype(BF16))
         dn_near = lax.optimization_barrier(mm("bse,de->bsd", gqkv[0], w_qkv).astype(BF16))
         late_sent, late_terms = second_stage(late_mine, late_far, [out_near, dn_near])
-        hidden_out = finish(finish_out_kernel, [hidden, after(out_near, *late_sent)], [out_far[0]], 0, None)
-        hidden_out = finish(finish_out_kernel, [hidden, out_near], [after(out_far[1], hidden_out)], 2, hidden_out)
+        hidden_out = None
+        for i in range(CHUNKS):
+            hidden_out = finish(finish_out_kernel, [hidden, after(out_near, *late_sent)], [out_far[i]], i * step, hidden_out)
         early_sent, early_terms = second_stage(early_mine, early_far, [hidden_out])
         dn_near = after(dn_near, *early_sent)
         grad_hidden = None
         gain_parts = []
+        w_grads = None
         for i, (start, count) in enumerate(pieces):
             grad_hidden, part = finish(
                 finish_grad_kernel, [hidden, grad_out, dn_near], [dn_far[i]], start, grad_hidden, gain
             )
             gain_parts.append(part)
-        gain_sum = lax.psum(jnp.sum(sum(gain_parts), axis=0), ("dp", "tp"))
-        grad_gain = lax.dynamic_slice(gain_sum, (lax.axis_index("dp") * rows_loc,), (rows_loc,))
-        grad_wq, grad_wk, grad_wv = w_grads = ungroup([(mine, after(far, gain_sum)) for mine, far in early_terms + late_terms])
-        hidden_out = finish(finish_out_kernel, [hidden, out_near], [after(out_far[2], *w_grads)], 3, hidden_out)
+            if i == 0:
+                w_grads = ungroup([(mine, after(far, grad_hidden)) for mine, far in late_terms], groups // 2, groups, None)
+                dn_near = after(dn_near, *w_grads)
+        grad_gain = gain_sum(jnp.sum(sum(gain_parts), axis=0), mesh.shape["tp"], mesh.shape["dp"])
+        grad_wq, grad_wk, grad_wv = ungroup([(mine, after(far, grad_gain)) for mine, far in early_terms], 0, groups, w_grads)
         return hidden_out, grad_hidden, grad_gain, grad_wq, grad_wk, grad_wv, grad_wo
 
     act_spec = P("dp", "tp", None)

time: 790 us -> 736 us (0.932)
  blocking collectives: 41.5 us -> 9.29 us
  waiting for transfers between devices: 239 us -> 215 us
  local copies, waits for them, and re-layouts: 54.1 us -> 46.1 us
    psum x1 -> x0, blocking collectives: 32.2 us -> none  [local_block(): gain_sum = lax.psum(jnp.sum(sum(gain_parts), axis=0), ('dp', 'tp'))]
    ppermute x11 -> x10, waiting for transfers between devices: 176 us -> 146 us  [exchange(): return lax.ppermute(values, 'tp', swap)]
    pallas_call x1 -> x3, Pallas kernels: 16.1 us -> 11.3 us  [split_norm(): pl.pallas_call(split_norm_kernel, out_shape=(out, out), grid_spec=pltpu.P...]
    pallas_call x6 -> x5, Pallas kernels: 23.6 us -> 27.9 us  [finish(): pl.pallas_call(kernel, out_shape=out_shape, grid=(count, half // row_bloc...]
    unnamed x99 -> x89, local copies, waits for them, and re-layouts: 20.2 us -> 17.6 us
  transfers between devices with their start and end apart: 24 -> 23, of which waited for: 8 -> 10; matrix products, arithmetic and copies ran while one was open for 36% -> 39% of each run, Pallas kernels for 18% -> 19%
where the time goes in v4:
time: 736 us; the launch traced here: 731 us
  matrix products  256 us (35%)
  waiting for transfers between devices  215 us (29%)
  Pallas kernels  145 us (20%)
  local copies, waits for them, and re-layouts  46.1 us (6%)
  starting transfers between devices  26.5 us (4%)
  other arithmetic  19.2 us (3%)
  between operations  14.5 us (2%)
  blocking collectives  9.29 us (1%)
    dot_general x19, matrix products, mm(): return jnp.einsum(eq, a, b, preferred_element_type=F32)  256 us
    ppermute x10, waiting for transfers between devices, exchange(): return lax.ppermute(values, 'tp', swap)  146 us
    pallas_call x3, Pallas kernels, attention_bwd(): pl.pallas_call(functools.partial(attention_bwd_kernel, group_size), out_s...  52.9 us
    all_gather x1, waiting for transfers between devices, local_block(): w_qkv = lax.all_gather(w_qkv, 'dp', axis=0, tiled=True)  51.5 us
    pallas_call x2, Pallas kernels, attention_fwd(): pl.pallas_call(functools.partial(attention_fwd_kernel, group_size), out_s...  33.8 us
    pallas_call x5, Pallas kernels, finish(): pl.pallas_call(kernel, out_shape=out_shape, grid=(count, half // row_bloc...  27.9 us
    unnamed x89, local copies, waits for them, and re-layouts  17.6 us
    ppermute x10, waiting for transfers between devices, pass_on(): return lax.ppermute(values, 'dp', [(i, i ^ bit) for i in range(8)])  16.6 us
  transfers between devices with their start and end apart: 23, of which 10 were waited for; matrix products, arithmetic and copies ran while one was open for 39% of the time, Pallas kernels for 19%

profile of v4, /device:TPU:0, one launch (start us, length us, event | category | flops | bytes accessed | tf_op | source)
XLA Modules:
  0.0 731.0 jit_solution(9281890152888207197)
XLA Ops:
  44.1 51.5 %all-gather.4.cloned.1.call-done = bf16[3072,2560]{1,0:T(8,128)(2,1)} async-done(((bf16[384,2560]{1,0:T(8,128)(2,1)}), bf16[3072,2560]{1,0:T(8,128)(2,1)}) %all-gather.4.cloned.1.call-update) | async-done | bytes 15728656 | tf_op jit(solution)/shard_map/all_gather | solution.py:459
  95.6 23.4 %fusion.47.own_ref = bf16[4,256,2560]{2,1,0:T(8,128)(2,1)} fusion(bf16[3072,2560]{1,0:T(8,128)(2,1)} %all-gather.4.cloned.1.call-done, bf16[4,256,3072]{2,1,0:T(8,128)(2,1)} %x_ref.9, f32[3072]{0:T(1024)S(1)} %bitcast.156, f32[4,256]{1,0:T(4,128)S(1)} %add_rsqrt_fusion), kind=kOutput, calls=%fused_computation.53 | convolution fusion | flops 16121331712 | bytes 27279360 | tf_op jit(solution)/shard_map/bsd,de->bse/dot_general | solution.py:436
  119.0 36.7 %collective-permute-done.1.source_ref = bf16[2,256,3072]{2,1,0:T(8,128)(2,1)} collective-permute-done((bf16[2,256,3072]{2,1,0:T(8,128)(2,1)}, bf16[2,256,3072]{2,1,0:T(8,128)(2,1)}, u32[]{:S(2)}, u32[]{:S(2)}) %collective-permute-start.1) | collective-permute-done | bytes 3145760 | tf_op jit(solution)/shard_map/ppermute | solution.py:433
  158.3 12.9 %fusion.62.rec_ref = bf16[2,256,2560]{2,1,0:T(8,128)(2,1)S(1)} fusion(bf16[3072,2560]{1,0:T(8,128)(2,1)} %all-gather.4.cloned.1.call-done, bf16[2,256,3072]{2,1,0:T(8,128)(2,1)} %collective-permute-done.1.source_ref, f32[3072]{0:T(1024)S(1)} %bitcast.157, f32[2,256]{1,0:T(2,128)S(1)} %add_rsqrt_fusion.2), kind=kOutput, calls=%fused_computation.64 | convolution fusion | flops 8060665856 | bytes 21510144 | tf_op jit(solution)/shard_map/bsd,de->bse/dot_general | solution.py:436
  171.2 16.9 %attention_fwd.2 = (bf16[4,256,1536]{2,1,0:T(8,128)(2,1)}, bf16[4,256,1536]{2,1,0:T(8,128)(2,1)}) custom-call(s32[1]{0:T(128)} %bitcast.tp_ref, bf16[4,256,2560]{2,1,0:T(8,128)(2,1)} %fusion.47.own_ref, bf16[2,256,2560]{2,1,0:T(8,128)(2,1)S(1)} %fusion.62.rec_ref, f32[512,128]{1,0:T(8,128)S(1)} %get-tuple-element.140.cos_ref, f32[512,128]{1,0:T(8,128)S(1)} %copy-done.11), custom_call_target="tpu_custom_call" | custom-call | flops 2415919104 | bytes 5242880 | tf_op jit(solution)/shard_map/attention_fwd/pallas_call | solution.py:158
  188.1 34.9 %collective-permute-done.source_ref = bf16[2,256,3072]{2,1,0:T(8,128)(2,1)S(1)} collective-permute-done((bf16[2,256,3072]{2,1,0:T(8,128)(2,1)}, bf16[2,256,3072]{2,1,0:T(8,128)(2,1)S(1)}, u32[]{:S(2)}, u32[]{:S(2)}) %collective-permute-start) | collective-permute-done | bytes 3145760 | tf_op jit(solution)/shard_map/ppermute | solution.py:433
  224.7 12.9 %fusion.65.rec_ref = bf16[2,256,2560]{2,1,0:T(8,128)(2,1)S(1)} fusion(bf16[3072,2560]{1,0:T(8,128)(2,1)} %all-gather.4.cloned.1.call-done, bf16[2,256,3072]{2,1,0:T(8,128)(2,1)} %copy-done.9, f32[2,256]{1,0:T(2,128)S(1)} %add_rsqrt_fusion.1, f32[3072]{0:T(1024)S(1)} %bitcast.158), kind=kOutput, calls=%fused_computation.65 | convolution fusion | flops 8060665856 | bytes 21510144 | tf_op jit(solution)/shard_map/bsd,de->bse/dot_general | solution.py:436
  237.6 16.9 %attention_fwd.3 = (bf16[4,256,1536]{2,1,0:T(8,128)(2,1)}, bf16[4,256,1536]{2,1,0:T(8,128)(2,1)}) custom-call(s32[1]{0:T(128)} %bitcast.tp_ref, bf16[4,256,2560]{2,1,0:T(8,128)(2,1)} %fusion.47.own_ref, bf16[2,256,2560]{2,1,0:T(8,128)(2,1)S(1)} %fusion.65.rec_ref, ...), custom_call_target="tpu_custom_call", output_to_operand_aliasing={{0}: (5, {}), {1}: (6, {})} | custom-call | flops 2415919104 | bytes 5242880 | tf_op jit(solution)/shard_map/attention_fwd/pallas_call | solution.py:158
  299.6 25.5 %attention_bwd.3.rest_0_ = bf16[2,4,256,2560]{3,2,1,0:T(8,128)(2,1)} custom-call(s32[1]{0:T(128)} %bitcast.tp_ref, bf16[4,256,2560]{2,1,0:T(8,128)(2,1)} %fusion.47.own_ref, bf16[2,256,2560]{2,1,0:T(8,128)(2,1)S(1)} %copy-done.14, f32[512,128]{1,0:T(8,128)S(1)} %get-tuple-element.140.cos_ref, f32[512,128]{1,0:T(8,128)S(1)} %copy-done.12, ...), custom_call_target="tpu_custom_call" | custom-call | flops 6039797760 | bytes 6291456 | tf_op jit(solution)/shard_map/attention_bwd/pallas_call | solution.py:190
  331.9 13.7 %attention_bwd.4.rest_0_ = bf16[2,4,256,2560]{3,2,1,0:T(8,128)(2,1)} custom-call(s32[1]{0:T(128)} %bitcast.tp_ref, bf16[4,256,2560]{2,1,0:T(8,128)(2,1)} %fusion.47.own_ref, bf16[2,256,2560]{2,1,0:T(8,128)(2,1)S(1)} %fusion.65.rec_ref, f32[512,128]{1,0:T(8,128)S(1)} %get-tuple-element.140.cos_ref, ...), custom_call_target="tpu_custom_call", output_to_operand_aliasing={{}: (7, {})} | custom-call | flops 3019898880 | bytes 3145728 | tf_op jit(solution)/shard_map/attention_bwd/pallas_call | solution.py:190
  345.7 13.4 %fusion.106 = f32[1536,3072,1]{1,0,2:T(8,128)} fusion(bf16[4,256,1536]{2,1,0:T(8,128)(2,1)S(1)} %copy-done.27, bf16[4,256,3072]{2,1,0:T(8,128)(2,1)S(1)} %bitcast.149), kind=kOutput, calls=%fused_computation.119 | convolution fusion | flops 9663676416 | bytes 28311552 | tf_op jit(solution)/shard_map/bse,bsd->ed/dot_general | solution.py:436
  359.0 19.4 %bitcast_add_fusion = f32[1536,3072]{1,0:T(8,128)} fusion(f32[1536,3072,1]{1,0,2:T(8,128)} %fusion.106, bf16[4,256,1536]{2,1,0:T(8,128)(2,1)S(1)} %copy-done.18, bf16[1,256,3072]{2,1,0:T(8,128)(2,1)} %collective-permute-done.2, bf16[1,256,3072]{2,1,0:T(8,128)(2,1)} %collective-permute-done.3, bf16[2,256,3072]{2,1,0:T(8,128)(2,1)} %collective-permute-done.4), kind=kOutput, calls=%fused_computation | convolution fusion | flops 9674686464 | bytes 47185920 | tf_op jit(solution)/shard_map/bse,bsd->ed/dot_general | solution.py:436
  407.3 13.7 %attention_bwd.5 = bf16[2,4,256,2560]{3,2,1,0:T(8,128)(2,1)} custom-call(s32[1]{0:T(128)} %bitcast.tp_ref, bf16[4,256,2560]{2,1,0:T(8,128)(2,1)} %fusion.47.own_ref, bf16[2,256,2560]{2,1,0:T(8,128)(2,1)S(1)} %copy-done.8, f32[512,128]{1,0:T(8,128)S(1)} %get-tuple-element.140.cos_ref, f32[512,128]{1,0:T(8,128)S(1)} %copy-done.12, ...), custom_call_target="tpu_custom_call", output_to_operand_aliasing={{}: (7, {})} | custom-call | flops 3019898880 | bytes 3145728 | tf_op jit(solution)/shard_map/attention_bwd/pallas_call | solution.py:190
  421.0 13.1 %convolution_bitcast_fusion.3 = f32[1536,1280]{1,0:T(8,128)} fusion(bf16[2,4,256,1536]{3,2,1,0:T(8,128)(2,1)S(1)} %get-tuple-element.85, bf16[2,4,256,2560]{3,2,1,0:T(8,128)(2,1)} %attention_bwd.5), kind=kOutput, calls=%fused_computation.33 | convolution fusion | flops 8053063680 | bytes 19398656 | tf_op jit(solution)/shard_map/hbsd,hbse->de/dot_general | solution.py:436
  436.2 14.4 %convolution_bitcast_fusion.2 = f32[1536,1280]{1,0:T(8,128)} fusion(bf16[2,4,256,1536]{3,2,1,0:T(8,128)(2,1)} %copy-done.6, bf16[2,4,256,2560]{3,2,1,0:T(8,128)(2,1)} %attention_bwd.5), kind=kOutput, calls=%fused_computation.32 | convolution fusion | flops 8053063680 | bytes 19398656 | tf_op jit(solution)/shard_map/hbsd,hbse->de/dot_general | solution.py:436
  450.7 14.1 %fusion.71 = bf16[2,256,3072]{2,1,0:T(8,128)(2,1)} fusion(bf16[3072,2560]{1,0:T(8,128)(2,1)} %all-gather.4.cloned.1.call-done, bf16[2,4,256,2560]{3,2,1,0:T(8,128)(2,1)} %attention_bwd.5), kind=kOutput, calls=%fused_computation.67 | convolution fusion | flops 8054636544 | bytes 21495808 | tf_op jit(solution)/shard_map/bse,de->bsd/dot_general | solution.py:436
  464.8 14.0 %fusion.68 = bf16[2,256,3072]{2,1,0:T(8,128)(2,1)} fusion(bf16[3072,2560]{1,0:T(8,128)(2,1)} %all-gather.4.cloned.1.call-done, bf16[2,4,256,2560]{3,2,1,0:T(8,128)(2,1)} %attention_bwd.5), kind=kOutput, calls=%fused_computation.66 | convolution fusion | flops 8054636544 | bytes 21495808 | tf_op jit(solution)/shard_map/bse,de->bsd/dot_general | solution.py:436
  484.7 13.3 %fusion.26 = f32[1536,1280]{1,0:T(8,128)S(1)} fusion(f32[1536,1280]{1,0:T(8,128)} %collective-permute-done.5, bf16[2,4,256,1536]{3,2,1,0:T(8,128)(2,1)S(1)} %bitcast.155, bf16[2,4,256,2560]{3,2,1,0:T(8,128)(2,1)} %attention_bwd.5), kind=kOutput, calls=%fused_computation.31 | convolution fusion | flops 8055029760 | bytes 27262976 | tf_op jit(solution)/shard_map/hbsd,hbse->de/dot_general | solution.py:436
  504.8 12.9 %fusion.25 = f32[1536,1280]{1,0:T(8,128)S(1)} fusion(f32[1536,1280]{1,0:T(8,128)} %collective-permute-done.6, bf16[2,4,256,1536]{3,2,1,0:T(8,128)(2,1)S(1)} %bitcast.155, bf16[2,4,256,2560]{3,2,1,0:T(8,128)(2,1)} %attention_bwd.5), kind=kOutput, calls=%fused_computation.29 | convolution fusion | flops 8055029760 | bytes 27262976 | tf_op jit(solution)/shard_map/hbsd,hbse->de/dot_general | solution.py:436
  522.8 23.0 %fusion.44.near_ref = bf16[4,256,3072]{2,1,0:T(8,128)(2,1)} fusion(bf16[3072,2560]{1,0:T(8,128)(2,1)} %all-gather.4.cloned.1.call-done, bf16[2,4,256,2560]{3,2,1,0:T(8,128)(2,1)} %attention_bwd.5), kind=kOutput, calls=%fused_computation.52 | convolution fusion | flops 16109273088 | bytes 27262976 | tf_op jit(solution)/shard_map/bse,de->bsd/dot_general | solution.py:436
  550.0 13.4 %fusion.41.near_ref = bf16[4,256,3072]{2,1,0:T(8,128)(2,1)S(1)} fusion(bf16[4,256,1536]{2,1,0:T(8,128)(2,1)} %get-tuple-element.94, bf16[1536,3072]{1,0:T(8,128)(2,1)} %all-gather.6.cloned.1.call-done), kind=kOutput, calls=%fused_computation.51 | convolution fusion | flops 9666822144 | bytes 18874368 | tf_op jit(solution)/shard_map/bse,ed->bsd/dot_general | solution.py:436
  575.5 15.6 %collective-permute-done.11 = f32[2,384,640]{2,1,0:T(8,128)S(1)} collective-permute-done((f32[2,384,640]{2,1,0:T(8,128)}, f32[2,384,640]{2,1,0:T(8,128)S(1)}, u32[]{:S(2)}, u32[]{:S(2)}) %collective-permute-start.11) | collective-permute-done | bytes 1966112 | tf_op jit(solution)/shard_map/ppermute | solution.py:514
  615.9 24.4 %collective-permute-done.14.far_ref = bf16[2,256,3072]{2,1,0:T(8,128)(2,1)} collective-permute-done((bf16[2,256,3072]{2,1,0:T(8,128)(2,1)}, bf16[2,256,3072]{2,1,0:T(8,128)(2,1)}, u32[]{:S(2)}, u32[]{:S(2)}) %collective-permute-start.14) | collective-permute-done | bytes 3145760 | tf_op jit(solution)/shard_map/ppermute | solution.py:433
  678.9 28.2 %collective-permute-done.16.far_ref = bf16[1,256,3072]{2,1,0:T(8,128)(2,1)S(1)} collective-permute-done((bf16[1,256,3072]{2,1,0:T(8,128)(2,1)}, bf16[1,256,3072]{2,1,0:T(8,128)(2,1)S(1)}, u32[]{:S(2)}, u32[]{:S(2)}) %collective-permute-start.16) | collective-permute-done | bytes 1572896 | tf_op jit(solution)/shard_map/ppermute | solution.py:433
  (189 shorter events, 238.3 us)
Async XLA Ops:
  7.2 88.4 %all-gather.4.cloned.1.call-start = ((), (), s32[]{:S(2)}) async-start(), calls=%async_computation.1 | async-start | bytes 17694720 | tf_op jit(solution)/shard_map/all_gather | solution.py:459
  11.0 243.5 %all-gather.6.cloned.1.call-start = ((), (), s32[]{:S(2)}) async-start(), calls=%async_computation.2 | async-start | bytes 10616832 | tf_op jit(solution)/shard_map/all_gather | solution.py:460
  11.8 712.5 %reduce-scatter.2.cloned.1.call-start = ((), (), s32[]{:S(2)}) async-start(), calls=%async_computation.3 | async-start | bytes 21233664 | tf_op jit(solution)/shard_map/reduce_scatter | solution.py:502
  15.8 309.3 %collective-permute-start.3 = (bf16[1,256,3072]{2,1,0:T(8,128)(2,1)}, bf16[1,256,3072]{2,1,0:T(8,128)(2,1)}, u32[]{:S(2)}, u32[]{:S(2)}) collective-permute-start(bf16[1,256,3072]{2,1,0:T(8,128)(2,1)} %get-tuple-element.133), channel_id=1, source_target_pairs={{0,8},{8,0},{1,9},{9,1},{2,10},{10,2},{3,11},{11,3},{4,12},{12,4},... | collective-permute-start | bytes 4718600 | tf_op jit(solution)/shard_map/ppermute | solution.py:433
  19.1 340.0 %collective-permute-start.2 = (bf16[1,256,3072]{2,1,0:T(8,128)(2,1)}, bf16[1,256,3072]{2,1,0:T(8,128)(2,1)}, u32[]{:S(2)}, u32[]{:S(2)}) collective-permute-start(bf16[1,256,3072]{2,1,0:T(8,128)(2,1)} %get-tuple-element.134), channel_id=1, source_target_pairs={{0,8},{8,0},{1,9},{9,1},{2,10},{10,2},{3,11},{11,3},{4,12},{12,4},... | collective-permute-start | bytes 4718600 | tf_op jit(solution)/shard_map/ppermute | solution.py:433
  21.0 134.7 %collective-permute-start.1 = (bf16[2,256,3072]{2,1,0:T(8,128)(2,1)}, bf16[2,256,3072]{2,1,0:T(8,128)(2,1)}, u32[]{:S(2)}, u32[]{:S(2)}) collective-permute-start(bf16[2,256,3072]{2,1,0:T(8,128)(2,1)} %slice.63), channel_id=1, source_target_pairs={{0,8},{8,0},{1,9},{9,1},{2,10},{10,2},{3,11},{11,3},{4,12},{12,4},... | collective-permute-start | bytes 9437192 | tf_op jit(solution)/shard_map/ppermute | solution.py:433
  24.8 198.2 %collective-permute-start = (bf16[2,256,3072]{2,1,0:T(8,128)(2,1)}, bf16[2,256,3072]{2,1,0:T(8,128)(2,1)S(1)}, u32[]{:S(2)}, u32[]{:S(2)}) collective-permute-start(bf16[2,256,3072]{2,1,0:T(8,128)(2,1)} %slice.64), channel_id=1, source_target_pairs={{0,8},{8,0},{1,9},{9,1},{2,10},{10,2},{3,11},{11,3},{4,12},{12,4},... | collective-permute-start | bytes 9437192 | tf_op jit(solution)/shard_map/ppermute | solution.py:433
  26.8 262.9 %collective-permute-start.4 = (bf16[2,256,3072]{2,1,0:T(8,128)(2,1)}, bf16[2,256,3072]{2,1,0:T(8,128)(2,1)}, u32[]{:S(2)}, u32[]{:S(2)}) collective-permute-start(bf16[2,256,3072]{2,1,0:T(8,128)(2,1)} %slice.69), channel_id=1, source_target_pairs={{0,8},{8,0},{1,9},{9,1},{2,10},{10,2},{3,11},{11,3},{4,12},{12,4},... | collective-permute-start | bytes 9437192 | tf_op jit(solution)/shard_map/ppermute | solution.py:433
  38.1 352.2 %copy-start.15 = (f32[8,1,384]{2,1,0:T(1,128)}, f32[8,1,384]{2,1,0:T(1,128)S(1)}, u32[]{:S(2)}) copy-start(f32[8,1,384]{2,1,0:T(1,128)S(1)} %convert_element_type.96) | copy-start | bytes 36868
  434.1 50.5 %collective-permute-start.5 = (f32[1536,1280]{1,0:T(8,128)}, f32[1536,1280]{1,0:T(8,128)}, u32[]{:S(2)}, u32[]{:S(2)}) collective-permute-start(f32[1536,1280]{1,0:T(8,128)} %convolution_bitcast_fusion.3), channel_id=1, source_target_pairs={{0,1},{1,0},{2,3},{3,2},{4,5},{5,4},{6,7},{7,6},{8,9},{9,8},{10,11... | collective-permute-start | bytes 23592968 | tf_op jit(solution)/shard_map/ppermute | solution.py:514
  434.2 136.4 %collective-permute-start.10 = (bf16[2,256,3072]{2,1,0:T(8,128)(2,1)}, bf16[2,256,3072]{2,1,0:T(8,128)(2,1)}, u32[]{:S(2)}, u32[]{:S(2)}) collective-permute-start(bf16[2,256,3072]{2,1,0:T(8,128)(2,1)} %fusion.74), channel_id=1, source_target_pairs={{0,8},{8,0},{1,9},{9,1},{2,10},{10,2},{3,11},{11,3},{4,12},{12,4},... | collective-permute-start | bytes 9437192 | tf_op jit(solution)/shard_map/ppermute | solution.py:433
  435.9 136.9 %collective-permute-start.9 = (bf16[2,256,3072]{2,1,0:T(8,128)(2,1)}, bf16[2,256,3072]{2,1,0:T(8,128)(2,1)S(1)}, u32[]{:S(2)}, u32[]{:S(2)}) collective-permute-start(bf16[2,256,3072]{2,1,0:T(8,128)(2,1)} %fusion.77), channel_id=1, source_target_pairs={{0,8},{8,0},{1,9},{9,1},{2,10},{10,2},{3,11},{11,3},{4,12},{12,4},... | collective-permute-start | bytes 9437192 | tf_op jit(solution)/shard_map/ppermute | solution.py:433
  450.6 52.5 %collective-permute-start.6 = (f32[1536,1280]{1,0:T(8,128)}, f32[1536,1280]{1,0:T(8,128)}, u32[]{:S(2)}, u32[]{:S(2)}) collective-permute-start(f32[1536,1280]{1,0:T(8,128)} %convolution_bitcast_fusion.2), channel_id=1, source_target_pairs={{0,1},{1,0},{2,3},{3,2},{4,5},{5,4},{6,7},{7,6},{8,9},{9,8},{10,11... | collective-permute-start | bytes 23592968 | tf_op jit(solution)/shard_map/ppermute | solution.py:514
  478.8 161.5 %collective-permute-start.14 = (bf16[2,256,3072]{2,1,0:T(8,128)(2,1)}, bf16[2,256,3072]{2,1,0:T(8,128)(2,1)}, u32[]{:S(2)}, u32[]{:S(2)}) collective-permute-start(bf16[2,256,3072]{2,1,0:T(8,128)(2,1)} %fusion.68), channel_id=1, source_target_pairs={{0,8},{8,0},{1,9},{9,1},{2,10},{10,2},{3,11},{11,3},{4,12},{12,4},... | collective-permute-start | bytes 9437192 | tf_op jit(solution)/shard_map/ppermute | solution.py:433
  501.6 45.2 %collective-permute-start.7 = (f32[2,384,640]{2,1,0:T(8,128)}, f32[2,384,640]{2,1,0:T(8,128)}, u32[]{:S(2)}, u32[]{:S(2)}) collective-permute-start(f32[2,384,640]{2,1,0:T(8,128)} %dynamic-slice_bitcast_fusion.3), channel_id=1, source_target_pairs={{0,2},{1,3},{2,0},{3,1},{4,6},{5,7},{6,4},{7,5},{8,10},{9,11},{10,... | collective-permute-start | bytes 5898248 | tf_op jit(solution)/shard_map/ppermute | solution.py:514
  503.1 45.2 %collective-permute-start.8 = (f32[2,384,640]{2,1,0:T(8,128)}, f32[2,384,640]{2,1,0:T(8,128)}, u32[]{:S(2)}, u32[]{:S(2)}) collective-permute-start(f32[2,384,640]{2,1,0:T(8,128)} %dynamic-slice_bitcast_fusion.2), channel_id=1, source_target_pairs={{0,4},{1,5},{2,6},{3,7},{4,0},{5,1},{6,2},{7,3},{8,12},{9,13},{10,... | collective-permute-start | bytes 5898248 | tf_op jit(solution)/shard_map/ppermute | solution.py:514
  546.8 44.3 %collective-permute-start.11 = (f32[2,384,640]{2,1,0:T(8,128)}, f32[2,384,640]{2,1,0:T(8,128)S(1)}, u32[]{:S(2)}, u32[]{:S(2)}) collective-permute-start(f32[2,384,640]{2,1,0:T(8,128)} %dynamic-slice_bitcast_fusion.1), channel_id=1, source_target_pairs={{0,2},{1,3},{2,0},{3,1},{4,6},{5,7},{6,4},{7,5},{8,10},{9,11},{10,... | collective-permute-start | bytes 5898248 | tf_op jit(solution)/shard_map/ppermute | solution.py:514
  548.3 59.3 %collective-permute-start.12 = (f32[2,384,640]{2,1,0:T(8,128)}, f32[2,384,640]{2,1,0:T(8,128)}, u32[]{:S(2)}, u32[]{:S(2)}) collective-permute-start(f32[2,384,640]{2,1,0:T(8,128)} %dynamic-slice_bitcast_fusion), channel_id=1, source_target_pairs={{0,4},{1,5},{2,6},{3,7},{4,0},{5,1},{6,2},{7,3},{8,12},{9,13},{10,... | collective-permute-start | bytes 5898248 | tf_op jit(solution)/shard_map/ppermute | solution.py:514
  570.5 103.5 %collective-permute-start.17 = (bf16[1,256,3072]{2,1,0:T(8,128)(2,1)}, bf16[1,256,3072]{2,1,0:T(8,128)(2,1)}, u32[]{:S(2)}, u32[]{:S(2)}) collective-permute-start(bf16[1,256,3072]{2,1,0:T(8,128)(2,1)} %get-tuple-element.135), channel_id=1, source_target_pairs={{0,8},{8,0},{1,9},{9,1},{2,10},{10,2},{3,11},{11,3},{4,12},{12,4},... | collective-permute-start | bytes 4718600 | tf_op jit(solution)/shard_map/ppermute | solution.py:433
  572.7 134.4 %collective-permute-start.16 = (bf16[1,256,3072]{2,1,0:T(8,128)(2,1)}, bf16[1,256,3072]{2,1,0:T(8,128)(2,1)S(1)}, u32[]{:S(2)}, u32[]{:S(2)}) collective-permute-start(bf16[1,256,3072]{2,1,0:T(8,128)(2,1)} %get-tuple-element.136), channel_id=1, source_target_pairs={{0,8},{8,0},{1,9},{9,1},{2,10},{10,2},{3,11},{11,3},{4,12},{12,4},... | collective-permute-start | bytes 4718600 | tf_op jit(solution)/shard_map/ppermute | solution.py:433
  592.4 49.6 %collective-permute-start.15 = (f32[384,640]{1,0:T(8,128)}, f32[384,640]{1,0:T(8,128)}, u32[]{:S(2)}, u32[]{:S(2)}) collective-permute-start(f32[384,640]{1,0:T(8,128)} %dynamic-slice_bitcast_fusion.10), channel_id=1, source_target_pairs={{0,2},{1,3},{2,0},{3,1},{4,6},{5,7},{6,4},{7,5},{8,10},{9,11},{10,... | collective-permute-start | bytes 2949128 | tf_op jit(solution)/shard_map/ppermute | solution.py:514
  607.6 50.1 %collective-permute-start.13 = (f32[384,640]{1,0:T(8,128)}, f32[384,640]{1,0:T(8,128)}, u32[]{:S(2)}, u32[]{:S(2)}) collective-permute-start(f32[384,640]{1,0:T(8,128)} %dynamic-slice_bitcast_fusion.11), channel_id=1, source_target_pairs={{0,4},{1,5},{2,6},{3,7},{4,0},{5,1},{6,2},{7,3},{8,12},{9,13},{10,... | collective-permute-start | bytes 2949128 | tf_op jit(solution)/shard_map/ppermute | solution.py:514
  640.3 80.2 %collective-permute-start.18 = (f32[384,640]{1,0:T(8,128)}, f32[384,640]{1,0:T(8,128)}, u32[]{:S(2)}, u32[]{:S(2)}) collective-permute-start(f32[384,640]{1,0:T(8,128)} %dynamic-slice_bitcast_fusion.9), channel_id=1, source_target_pairs={{0,4},{1,5},{2,6},{3,7},{4,0},{5,1},{6,2},{7,3},{8,12},{9,13},{10,... | collective-permute-start | bytes 2949128 | tf_op jit(solution)/shard_map/ppermute | solution.py:514
  642.0 78.5 %collective-permute-start.19 = (f32[384,640]{1,0:T(8,128)}, f32[384,640]{1,0:T(8,128)}, u32[]{:S(2)}, u32[]{:S(2)}) collective-permute-start(f32[384,640]{1,0:T(8,128)} %dynamic-slice_bitcast_fusion.8), channel_id=1, source_target_pairs={{0,2},{1,3},{2,0},{3,1},{4,6},{5,7},{6,4},{7,5},{8,10},{9,11},{10,... | collective-permute-start | bytes 2949128 | tf_op jit(solution)/shard_map/ppermute | solution.py:514
  (42 other events, 983.2 us)
Sparse Core Ops, SparseCore 0:
  11.2 84.3 all-gather.3
  97.4 56.7 all-gather.5
  378.6 121.8 reduce-scatter.1

commit v5 on v4

--- a/solution.py
+++ b/solution.py
@@ -53,7 +53,7 @@
 
 
 def attention_fwd_kernel(group_size, tp_ref, own_ref, rec_ref, cos_ref, sin_ref, *rest):
-    out_own_ref, out_rec_ref = rest[-2:]
+    out_ref = rest[-1]
     half = own_ref.shape[1]
     first = tp_ref[0] == 0
     lower, upper = pick_halves(first, own_ref[0], rec_ref[0])
@@ -77,7 +77,7 @@
     a_up = dot((p_a * inv).astype(BF16), v_lo, NN) + dot((p_b * inv).astype(BF16), v_up, NN)
     for i in range(group_size):
         part = slice(i * half, (i + 1) * half)
-        store_halves(first, out_own_ref, out_rec_ref, slice(i * HEAD_DIM, (i + 1) * HEAD_DIM), a_lo[part], a_up[part])
+        store_halves(first, out_ref.at[0], out_ref.at[1], slice(i * HEAD_DIM, (i + 1) * HEAD_DIM), a_lo[part], a_up[part])
 
 
 def attention_bwd_kernel(group_size, tp_ref, own_ref, rec_ref, cos_ref, sin_ref, ga_own_ref, ga_rec_ref, *rest):
@@ -144,25 +144,25 @@
     count = qkv_rec.shape[0]
     block = width // groups
     out_block = group_size * HEAD_DIM
-    shape = jax.ShapeDtypeStruct((batch, half, groups * out_block), BF16)
+    shape = jax.ShapeDtypeStruct((2, batch, half, groups * out_block), BF16)
     spec = lambda columns, offset: pl.BlockSpec((1, half, columns), lambda b, g, tp: (b + offset, 0, g))
     table = pl.BlockSpec((2 * half, HEAD_DIM), lambda b, g, tp: (0, 0))
     in_specs = [spec(block, start), spec(block, 0), table, table]
     args = [tp_index, qkv_own, qkv_rec, *tables]
     aliases = {}
     if held is not None:
-        in_specs += [pl.BlockSpec(memory_space=pl.ANY)] * 2
-        aliases = {len(args): 0, len(args) + 1: 1}
-        args += list(held)
+        in_specs.append(pl.BlockSpec(memory_space=pl.ANY))
+        aliases = {len(args): 0}
+        args.append(held)
     work = count * groups * group_size * half * half
     return pl.pallas_call(
         functools.partial(attention_fwd_kernel, group_size),
-        out_shape=(shape, shape),
+        out_shape=shape,
         grid_spec=pltpu.PrefetchScalarGridSpec(
             num_scalar_prefetch=1,
             grid=(count, groups),
             in_specs=in_specs,
-            out_specs=(spec(out_block, start), spec(out_block, start)),
+            out_specs=pl.BlockSpec((2, 1, half, out_block), lambda b, g, tp: (0, b + start, 0, g)),
         ),
         input_output_aliases=aliases,
         compiler_params=pltpu.CompilerParams(vmem_limit_bytes=48 * 2**20),
@@ -203,12 +203,13 @@
     )(*args)
 
 
-def split_norm_kernel(core_ref, gain_ref, source_ref, *rest):
+def split_kernel(normalise, core_ref, gain_ref, source_ref, *rest):
     mine_ref, sent_ref = rest[-2:]
     first = core_ref[0] == 0
-    values = source_ref[0].astype(F32)
-    inv_rms = lax.rsqrt(jnp.mean(values * values, axis=-1, keepdims=True) + NORM_EPS)
-    normed = values * inv_rms * gain_ref[...]
+    normed = source_ref[0].astype(F32)
+    if normalise:
+        inv_rms = lax.rsqrt(jnp.mean(normed * normed, axis=-1, keepdims=True) + NORM_EPS)
+        normed = normed * inv_rms * gain_ref[...]
     rows = normed.shape[1] // 8
     for i in range(4):
         even = normed[:, 2 * i * rows:(2 * i + 1) * rows]
@@ -217,7 +218,7 @@
         sent_ref[0, 0, :, i * rows:(i + 1) * rows] = jnp.where(first, odd, even).astype(BF16)
 
 
-def split_norm(core_index, gain, source, kind, start, batch, held, row_block=128):
+def split_columns(core_index, gain, source, kind, start, batch, held, normalise, row_block=128):
     count, half, width = source.shape
     row_block = min(row_block, half)
     out = jax.ShapeDtypeStruct((2, batch, half, width // 2), BF16)
@@ -230,7 +231,7 @@
         aliases = {len(args): 0, len(args) + 1: 1}
         args += list(held)
     return pl.pallas_call(
-        split_norm_kernel,
+        functools.partial(split_kernel, normalise),
         out_shape=(out, out),
         grid_spec=pltpu.PrefetchScalarGridSpec(
             num_scalar_prefetch=1, grid=(count, half // row_block), in_specs=in_specs, out_specs=(out_spec, out_spec)
@@ -238,8 +239,48 @@
         input_output_aliases=aliases,
         compiler_params=pltpu.CompilerParams(vmem_limit_bytes=32 * 2**20),
         cost_estimate=cost(count * half * width * 400, 0, source, source),
-        name="split_norm",
+        name="split_norm" if normalise else "split_plain",
     )(*args)
+
+
+def join_kernel(axis, place_ref, *refs):
+    out_ref = refs[-1]
+    relative = pl.program_id(0) ^ place_ref[0]
+    own = pl.program_id(1) == place_ref[1]
+
+    def put(values):
+        out_ref[...] = values.reshape(out_ref.shape)
+
+    for side, here in ((refs[:5], own), (refs[5:10], jnp.logical_not(own))):
+        for index, source in ((0, 0), (1, 2), (2, 1)):
+
+            @pl.when(here & (relative == index))
+            def _(source=source, side=side):
+                put(side[source][...])
+
+        @pl.when(here & (relative == 3))
+        def _(side=side):
+            put(jnp.concatenate([side[3][...], side[4][...]], axis=axis))
+
+
+def join(place, near, far, axis):
+    rows, columns = near[0].shape
+    whole = lambda array: pl.BlockSpec(array.shape, lambda j, c, place: (0, 0))
+    if axis == 1:
+        out, out_spec = (8 * rows, columns), pl.BlockSpec((rows, columns), lambda j, c, place: (2 * j + c, 0))
+    else:
+        out, out_spec = (rows, 8 * columns), pl.BlockSpec((rows, columns), lambda j, c, place: (0, 2 * j + c))
+    out = jax.ShapeDtypeStruct(out, BF16)
+    return pl.pallas_call(
+        functools.partial(join_kernel, axis),
+        out_shape=out,
+        grid_spec=pltpu.PrefetchScalarGridSpec(
+            num_scalar_prefetch=1, grid=(4, 2), in_specs=[whole(array) for array in (*near, *far)], out_specs=out_spec
+        ),
+        compiler_params=pltpu.CompilerParams(vmem_limit_bytes=48 * 2**20),
+        cost_estimate=cost(out.size * 400, 0, out, out),
+        name="join",
+    )(place, *near, *far)
 
 
 def gain_sum_kernel(tp_size, dp_size, part_ref, out_ref, slots, send_sem, recv_sem):
@@ -455,9 +496,32 @@
         for start, count in pieces:
             grad_rec.append(exchange(grad_out[start:start + count]))
 
+        place = lax.axis_index("dp").astype(jnp.uint32)
+        core, along_x, along_y = place & 1, (place >> 1) & 1, place >> 2
+        core_index = core.astype(jnp.int32).reshape(1)
+
+        def pass_on(values, bit):
+            return lax.ppermute(values, "dp", [(i, i ^ bit) for i in range(8)])
+
+        cut, cut_o = groups // 2 * block, w_out.shape[0] // 2
+        chip_core = jnp.stack([place >> 1, core]).astype(jnp.int32)
+
+        def gather(piece, axis, before=()):
+            from_y = pass_on(piece, 4)
+            from_x = pass_on(piece, 2)
+            from_y, from_x = after((from_y, from_x), *before)
+            middle = piece.shape[axis] // 2
+            diagonal = (
+                pass_on(lax.slice_in_dim(from_y, 0, middle, axis=axis), 2),
+                pass_on(lax.slice_in_dim(from_x, middle, None, axis=axis), 4),
+            )
+            near = (piece, from_y, from_x, *diagonal)
+            far = [pass_on(part, 1) for part in near]
+            return join(chip_core, near, far, axis)
+
         w_qkv = regroup(w_query, w_key, w_value)
-        w_qkv = lax.all_gather(w_qkv, "dp", axis=0, tiled=True)
-        w_o = lax.all_gather(w_out, "dp", axis=1, tiled=True)
+        w_qkv = gather(w_qkv, 1)
+        w_o = gather(w_out, 0, [w_qkv])
         gain = lax.all_gather(norm_gain, "dp", axis=0, tiled=True).astype(F32)
 
         def norm(values):
@@ -465,13 +529,14 @@
             inv_rms = lax.rsqrt(jnp.mean(values * values, axis=-1, keepdims=True) + NORM_EPS)
             return (values * inv_rms * gain).astype(BF16)
 
-        place = lax.axis_index("dp").astype(jnp.uint32)
-        core, along_x, along_y = place & 1, (place >> 1) & 1, place >> 2
-        core_index = core.astype(jnp.int32).reshape(1)
-        split = split_norm(core_index, gain, hidden, 0, 0, batch, None)
+        split = split_columns(core_index, gain, hidden, 0, 0, batch, None, True)
         for i in range(CHUNKS):
-            split = split_norm(core_index, gain, hidden_rec[i], 1, i * step, batch, split)
+            split = split_columns(core_index, gain, hidden_rec[i], 1, i * step, batch, split, True)
         normed_mine, normed_sent = split
+        split = split_columns(core_index, gain, grad_out, 0, 0, batch, None, False)
+        for i, (start, _) in enumerate(pieces):
+            split = split_columns(core_index, gain, grad_rec[i], 1, start, batch, split, False)
+        dy_mine, dy_sent = split
 
         normed_own = norm(hidden)
         qkv_own = mm("bsd,de->bse", normed_own, w_qkv).astype(BF16)
@@ -482,26 +547,41 @@
             rec = norm(after(hidden_rec[i], before))
             qkv_rec.append(mm("bsd,de->bse", rec, w_qkv).astype(BF16))
             attn = attention_fwd(tp_index, qkv_own, qkv_rec[i], tables, i * step, attn, groups, group_size)
-            before = attn[0]
-        attn_own, attn_rec = attn
+            before = attn
 
         out_send = []
         for i in range(CHUNKS):
-            out_send.append(lax.optimization_barrier(mm("bse,ed->bsd", attn_rec[i * step:(i + 1) * step], w_o).astype(BF16)))
+            out_send.append(lax.optimization_barrier(mm("bse,ed->bsd", attn[1][i * step:(i + 1) * step], w_o).astype(BF16)))
 
         ga_own = mm("bsd,ed->bse", after(grad_out, *out_send), w_o).astype(BF16)
         gqkv = None
         before = ga_own
         for i, (start, count) in enumerate(pieces):
             if i == len(pieces) - 1:
-                grad_wo = mm("bse,bsd->ed", attn_own, after(grad_out, gqkv)) + mm("bse,bsd->ed", attn_rec, jnp.concatenate(grad_rec, axis=0))
-                before = grad_wo
+                out_grad_sent = mm("hbse,hbsd->ed", after(attn, gqkv), dy_sent)
+                out_grad_far = pass_on(out_grad_sent, 1)
+                before = out_grad_sent
             ga_rec = mm("bsd,ed->bse", after(grad_rec[i], before), w_o).astype(BF16)
             gqkv = attention_bwd(tp_index, qkv_own, qkv_rec[start // step], tables, ga_own, ga_rec, start, start % step, gqkv, groups, group_size)
             before = gqkv
-        grad_wo = lax.psum_scatter(grad_wo, "dp", scatter_dimension=1, tiled=True)
-
-        cut = groups // 2 * block
+
+        def column_pick(values, pieces_at, row=0, wide=1):
+            cuts = [lax.dynamic_slice(values, (jnp.uint32(row), at * rows_loc), (cut_o, wide * rows_loc)) for at in pieces_at]
+            return cuts[0] if len(cuts) == 1 else jnp.concatenate(cuts, axis=1)
+
+        total = mm("hbse,hbsd->ed", after(attn, gqkv), dy_mine) + out_grad_far
+        o_sent = column_pick(total, [along_x ^ 1, 2 + (along_x ^ 1)]), column_pick(total, [2 * (along_y ^ 1)], cut_o, 2)
+        o_sent, total = lax.optimization_barrier((o_sent, total))
+        o_mine = column_pick(total, [along_x, 2 + along_x]), column_pick(total, [2 * along_y], cut_o, 2)
+        o_far = pass_on(o_sent[0], 2), pass_on(o_sent[1], 4)
+
+        def second_stage_o(before):
+            far = after(o_far, *before)
+            total = o_mine[0] + far[0], o_mine[1] + far[1]
+            sent = column_pick(total[0], [along_y ^ 1]), column_pick(total[1], [along_x ^ 1])
+            sent, total = lax.optimization_barrier((sent, total))
+            mine = column_pick(total[0], [along_y]), column_pick(total[1], [along_x])
+            return sent, mine, (pass_on(sent[0], 4), pass_on(sent[1], 2))
 
         def pick(values, axis, coordinate, columns=0):
             at = [jnp.uint32(0)] * values.ndim
@@ -510,14 +590,11 @@
             size[axis] = 1
             return lax.squeeze(lax.dynamic_slice(values, at, size), [axis])
 
-        def pass_on(values, bit):
-            return lax.ppermute(values, "dp", [(i, i ^ bit) for i in range(8)])
-
         def weight_grad(normed, columns, before):
             return mm("hbsd,hbse->de", normed, after(gqkv, *before)[..., columns])
 
         late, early = slice(cut, 2 * cut), slice(0, cut)
-        late_sent = weight_grad(normed_sent, late, [])
+        late_sent = weight_grad(normed_sent, late, o_sent)
         late_far = pass_on(late_sent, 1)
         early_sent = weight_grad(normed_sent, early, [late_sent])
         early_far = pass_on(early_sent, 1)
@@ -549,11 +626,12 @@
         for i in range(3):
             dn_far.append(exchange(dn_sent[i]))
 
-        late_sent, late_mine, late_far = first_stage(weight_grad(normed_mine, late, dn_send), late_far)
+        o_sent, o_mine, o_far = second_stage_o(dn_send)
+        late_sent, late_mine, late_far = first_stage(weight_grad(normed_mine, late, o_sent), late_far)
         early_sent, early_mine, early_far = first_stage(weight_grad(normed_mine, early, late_sent), early_far)
 
-        attn_own, gqkv = after((attn_own, gqkv), *early_sent)
-        out_near = lax.optimization_barrier(mm("bse,ed->bsd", attn_own, w_o).astype(BF16))
+        attn, gqkv = after((attn, gqkv), *early_sent)
+        out_near = lax.optimization_barrier(mm("bse,ed->bsd", attn[0], w_o).astype(BF16))
         dn_near = lax.optimization_barrier(mm("bse,de->bsd", gqkv[0], w_qkv).astype(BF16))
         late_sent, late_terms = second_stage(late_mine, late_far, [out_near, dn_near])
         hidden_out = None
@@ -569,11 +647,15 @@
                 finish_grad_kernel, [hidden, grad_out, dn_near], [dn_far[i]], start, grad_hidden, gain
             )
             gain_parts.append(part)
+            if i == 1:
+                w_grads = ungroup([(mine, after(far, grad_hidden)) for mine, far in early_terms], 0, groups, w_grads)
+                dn_near = after(dn_near, *w_grads)
             if i == 0:
                 w_grads = ungroup([(mine, after(far, grad_hidden)) for mine, far in late_terms], groups // 2, groups, None)
                 dn_near = after(dn_near, *w_grads)
         grad_gain = gain_sum(jnp.sum(sum(gain_parts), axis=0), mesh.shape["tp"], mesh.shape["dp"])
-        grad_wq, grad_wk, grad_wv = ungroup([(mine, after(far, grad_gain)) for mine, far in early_terms], 0, groups, w_grads)
+        grad_wq, grad_wk, grad_wv = w_grads
+        grad_wo = jnp.concatenate([o_mine[0] + after(o_far[0], hidden_out), o_mine[1] + after(o_far[1], hidden_out)], axis=0)
         return hidden_out, grad_hidden, grad_gain, grad_wq, grad_wk, grad_wv, grad_wo
 
     act_spec = P("dp", "tp", None)

time: 736 us -> 847 us (1.15)
  waiting for transfers between devices: 215 us -> 262 us
  local copies, waits for them, and re-layouts: 46.1 us -> 88.7 us
  Pallas kernels: 145 us -> 171 us
  matrix products: 256 us -> 241 us
  between operations: 14.5 us -> 1.65 us
  starting transfers between devices: 26.5 us -> 38.2 us
    ppermute x10 -> x33, waiting for transfers between devices: 16.6 us -> 105 us  [pass_on(): return lax.ppermute(values, 'dp', [(i, i ^ bit) for i in range(8)])]
    all_gather x2 -> x0, waiting for transfers between devices: 51.5 us -> none  [the longest x1 51.5 us: local_block(): w_qkv = lax.all_gather(w_qkv, 'dp', axis=0, tiled=True)]
    pallas_call x3 -> x9, Pallas kernels: 11.3 us -> 36.3 us  [the longest x2 20.3 us: join(): pl.pallas_call(functools.partial(join_kernel, axis), out_shape=out, grid_...]
    unnamed x89 -> x147, local copies, waits for them, and re-layouts: 17.6 us -> 41.7 us
    dot_general x19, matrix products: 256 us -> 241 us  [mm(): return jnp.einsum(eq, a, b, preferred_element_type=F32)]
    ppermute x10 -> x33, starting transfers between devices: 13 us -> 26.7 us  [pass_on(): return lax.ppermute(values, 'dp', [(i, i ^ bit) for i in range(8)])]
    ppermute x10, waiting for transfers between devices: 146 us -> 157 us  [exchange(): return lax.ppermute(values, 'tp', swap)]
    dynamic_slice x0 -> x5, local copies, waits for them, and re-layouts: none -> 9.33 us  [column_pick(): lax.dynamic_slice(values, (jnp.uint32(row), at * rows_loc), (cut_o, wide...]
  transfers between devices with their start and end apart: 23 -> 43, of which waited for: 10 -> 11; matrix products, arithmetic and copies ran while one was open for 39% -> 30% of each run, Pallas kernels for 19% -> 13%
where the time goes in v5:
time: 847 us; the launch traced here: 836 us
  waiting for transfers between devices  262 us (31%)
  matrix products  241 us (28%)
  Pallas kernels  171 us (20%)
  local copies, waits for them, and re-layouts  88.7 us (10%)
  starting transfers between devices  38.2 us (5%)
  other arithmetic  25.7 us (3%)
    dot_general x19, matrix products, mm(): return jnp.einsum(eq, a, b, preferred_element_type=F32)  241 us
    ppermute x10, waiting for transfers between devices, exchange(): return lax.ppermute(values, 'tp', swap)  157 us
    ppermute x33, waiting for transfers between devices, pass_on(): return lax.ppermute(values, 'dp', [(i, i ^ bit) for i in range(8)])  105 us
    pallas_call x3, Pallas kernels, attention_bwd(): pl.pallas_call(functools.partial(attention_bwd_kernel, group_size), out_s...  53.4 us
    unnamed x147, local copies, waits for them, and re-layouts  41.7 us
    pallas_call x2, Pallas kernels, attention_fwd(): pl.pallas_call(functools.partial(attention_fwd_kernel, group_size), out_s...  33.6 us
    pallas_call x5, Pallas kernels, finish(): pl.pallas_call(kernel, out_shape=out_shape, grid=(count, half // row_bloc...  29.6 us
    ppermute x33, starting transfers between devices, pass_on(): return lax.ppermute(values, 'dp', [(i, i ^ bit) for i in range(8)])  26.7 us
  transfers between devices with their start and end apart: 43, of which 11 were waited for; matrix products, arithmetic and copies ran while one was open for 30% of the time, Pallas kernels for 13%

profile of v5, /device:TPU:0, one launch (start us, length us, event | category | flops | bytes accessed | tf_op | source)
XLA Modules:
  0.0 836.4 jit_solution(6770420198021420961)
XLA Ops:
  15.2 35.6 %collective-permute-done.refs_1_ = bf16[384,2560]{1,0:T(8,128)(2,1)} collective-permute-done((bf16[384,2560]{1,0:T(8,128)(2,1)}, bf16[384,2560]{1,0:T(8,128)(2,1)}, u32[]{:S(2)}, u32[]{:S(2)}) %collective-permute-start) | collective-permute-done | bytes 1966112 | tf_op jit(solution)/shard_map/ppermute | solution.py:504
  57.6 60.2 %collective-permute-done.21.source_ref = bf16[1,256,3072]{2,1,0:T(8,128)(2,1)S(1)} collective-permute-done((bf16[1,256,3072]{2,1,0:T(8,128)(2,1)S(1)}, bf16[1,256,3072]{2,1,0:T(8,128)(2,1)S(1)}, u32[]{:S(2)}, u32[]{:S(2)}) %collective-permute-start.21) | collective-permute-done | bytes 1572896 | tf_op jit(solution)/shard_map/ppermute | solution.py:474
  119.5 31.6 %collective-permute-done.20.source_ref = bf16[1,256,3072]{2,1,0:T(8,128)(2,1)S(1)} collective-permute-done((bf16[1,256,3072]{2,1,0:T(8,128)(2,1)S(1)}, bf16[1,256,3072]{2,1,0:T(8,128)(2,1)S(1)}, u32[]{:S(2)}, u32[]{:S(2)}) %collective-permute-start.20) | collective-permute-done | bytes 1572896 | tf_op jit(solution)/shard_map/ppermute | solution.py:474
  222.0 21.4 %fusion.46.own_ref = bf16[4,256,2560]{2,1,0:T(8,128)(2,1)} fusion(bf16[3072,2560]{1,0:T(8,128)(2,1)} %join.2, bf16[4,256,3072]{2,1,0:T(8,128)(2,1)S(1)} %bitcast.152, f32[3072]{0:T(1024)S(1)} %bitcast.173, f32[4,256]{1,0:T(4,128)S(1)} %add_rsqrt_fusion), kind=kOutput, calls=%fused_computation.53 | convolution fusion | flops 16121331712 | bytes 27279360 | tf_op jit(solution)/shard_map/bsd,de->bse/dot_general | solution.py:477
  243.4 32.5 %collective-permute-done.10.source_ref = bf16[2,256,3072]{2,1,0:T(8,128)(2,1)S(1)} collective-permute-done((bf16[2,256,3072]{2,1,0:T(8,128)(2,1)}, bf16[2,256,3072]{2,1,0:T(8,128)(2,1)S(1)}, u32[]{:S(2)}, u32[]{:S(2)}) %collective-permute-start.10) | collective-permute-done | bytes 3145760 | tf_op jit(solution)/shard_map/ppermute | solution.py:474
  292.2 16.7 %attention_fwd.2.rest_0_ = bf16[2,4,256,1536]{3,2,1,0:T(8,128)(2,1)} custom-call(s32[1]{0:T(128)} %bitcast.tp_ref, bf16[4,256,2560]{2,1,0:T(8,128)(2,1)} %fusion.46.own_ref, bf16[2,256,2560]{2,1,0:T(8,128)(2,1)S(1)} %fusion.61.rec_ref, f32[512,128]{1,0:T(8,128)S(1)} %get-tuple-element.188.cos_ref, f32[512,128]{1,0:T(8,128)S(1)} %get-tuple-element.189.sin_ref), custom_call_target="tpu_custom_call" | custom-call | flops 2415919104 | bytes 5242880 | tf_op jit(solution)/shard_map/attention_fwd/pallas_call | solution.py:158
  308.9 33.2 %collective-permute-done.9.source_ref = bf16[2,256,3072]{2,1,0:T(8,128)(2,1)} collective-permute-done((bf16[2,256,3072]{2,1,0:T(8,128)(2,1)}, bf16[2,256,3072]{2,1,0:T(8,128)(2,1)}, u32[]{:S(2)}, u32[]{:S(2)}) %collective-permute-start.9) | collective-permute-done | bytes 3145760 | tf_op jit(solution)/shard_map/ppermute | solution.py:474
  345.2 12.7 %fusion.64.rec_ref = bf16[2,256,2560]{2,1,0:T(8,128)(2,1)S(1)} fusion(bf16[3072,2560]{1,0:T(8,128)(2,1)} %join.2, bf16[2,256,3072]{2,1,0:T(8,128)(2,1)} %collective-permute-done.9.source_ref, f32[2,256]{1,0:T(2,128)S(1)} %add_rsqrt_fusion.1, f32[3072]{0:T(1024)S(1)} %bitcast.175), kind=kOutput, calls=%fused_computation.65 | convolution fusion | flops 8060665856 | bytes 21510144 | tf_op jit(solution)/shard_map/bsd,de->bse/dot_general | solution.py:477
  358.0 17.0 %attention_fwd.3 = bf16[2,4,256,1536]{3,2,1,0:T(8,128)(2,1)} custom-call(s32[1]{0:T(128)} %bitcast.tp_ref, bf16[4,256,2560]{2,1,0:T(8,128)(2,1)} %fusion.46.own_ref, bf16[2,256,2560]{2,1,0:T(8,128)(2,1)S(1)} %fusion.64.rec_ref, f32[512,128]{1,0:T(8,128)S(1)} %get-tuple-element.188.cos_ref, ...), custom_call_target="tpu_custom_call", output_to_operand_aliasing={{}: (5, {})} | custom-call | flops 2415919104 | bytes 5242880 | tf_op jit(solution)/shard_map/attention_fwd/pallas_call | solution.py:158
  402.6 13.7 %fusion.79.ga_own_ref = bf16[4,256,1536]{2,1,0:T(8,128)(2,1)} fusion(bf16[4,256,3072]{2,1,0:T(8,128)(2,1)S(1)} %bitcast.156, bf16[1536,3072]{1,0:T(8,128)(2,1)} %join.3), kind=kOutput, calls=%fused_computation.70 | convolution fusion | flops 9665249280 | bytes 18874368 | tf_op jit(solution)/shard_map/bsd,ed->bse/dot_general | solution.py:477
  425.8 26.0 %attention_bwd.3.rest_0_ = bf16[2,4,256,2560]{3,2,1,0:T(8,128)(2,1)} custom-call(s32[1]{0:T(128)} %bitcast.tp_ref, bf16[4,256,2560]{2,1,0:T(8,128)(2,1)} %fusion.46.own_ref, bf16[2,256,2560]{2,1,0:T(8,128)(2,1)S(1)} %fusion.61.rec_ref, f32[512,128]{1,0:T(8,128)S(1)} %get-tuple-element.188.cos_ref, f32[512,128]{1,0:T(8,128)S(1)} %get-tuple-element.189.sin_ref, ...), custom_call_target="tpu_custom_call" | custom-call | flops 6039797760 | bytes 6291456 | tf_op jit(solution)/shard_map/attention_bwd/pallas_call | solution.py:190
  458.4 13.7 %attention_bwd.4.rest_0_ = bf16[2,4,256,2560]{3,2,1,0:T(8,128)(2,1)} custom-call(s32[1]{0:T(128)} %bitcast.tp_ref, bf16[4,256,2560]{2,1,0:T(8,128)(2,1)} %fusion.46.own_ref, bf16[2,256,2560]{2,1,0:T(8,128)(2,1)S(1)} %fusion.64.rec_ref, f32[512,128]{1,0:T(8,128)S(1)} %get-tuple-element.188.cos_ref, ...), custom_call_target="tpu_custom_call", output_to_operand_aliasing={{}: (7, {})} | custom-call | flops 3019898880 | bytes 3145728 | tf_op jit(solution)/shard_map/attention_bwd/pallas_call | solution.py:190
  472.2 14.0 %convolution_bitcast_fusion.4 = f32[1536,1536]{1,0:T(8,128)} fusion(bf16[2,4,256,1536]{3,2,1,0:T(8,128)(2,1)} %attention_fwd.3, bf16[2,4,256,1536]{3,2,1,0:T(8,128)(2,1)S(1)} %bitcast.164), kind=kOutput, calls=%fused_computation.34 | convolution fusion | flops 9663676416 | bytes 22020096 | tf_op jit(solution)/shard_map/hbse,hbsd->ed/dot_general | solution.py:477
  512.7 13.7 %attention_bwd.5 = bf16[2,4,256,2560]{3,2,1,0:T(8,128)(2,1)} custom-call(s32[1]{0:T(128)} %bitcast.tp_ref, bf16[4,256,2560]{2,1,0:T(8,128)(2,1)} %fusion.46.own_ref, bf16[2,256,2560]{2,1,0:T(8,128)(2,1)S(1)} %copy-done.13, f32[512,128]{1,0:T(8,128)S(1)} %copy-done.17, f32[512,128]{1,0:T(8,128)S(1)} %copy-done.19, ...), custom_call_target="tpu_custom_call", output_to_operand_aliasing={{}: (7, {})} | custom-call | flops 3019898880 | bytes 3145728 | tf_op jit(solution)/shard_map/attention_bwd/pallas_call | solution.py:190
  526.5 16.0 %bitcast_add_fusion = f32[1536,1536]{1,0:T(8,128)} fusion(f32[1536,1536]{1,0:T(8,128)} %collective-permute-done.23, bf16[2,4,256,1536]{3,2,1,0:T(8,128)(2,1)S(1)} %bitcast.162, bf16[2,4,256,1536]{3,2,1,0:T(8,128)(2,1)} %attention_fwd.3), kind=kOutput, calls=%fused_computation.17 | convolution fusion | flops 9666035712 | bytes 31457280 | tf_op jit(solution)/shard_map/hbse,hbsd->ed/dot_general | solution.py:477
  550.1 13.6 %convolution_bitcast_fusion.3 = f32[1536,1280]{1,0:T(8,128)} fusion(bf16[2,4,256,1536]{3,2,1,0:T(8,128)(2,1)S(1)} %bitcast.168, bf16[2,4,256,2560]{3,2,1,0:T(8,128)(2,1)} %attention_bwd.5), kind=kOutput, calls=%fused_computation.33 | convolution fusion | flops 8053063680 | bytes 19398656 | tf_op jit(solution)/shard_map/hbsd,hbse->de/dot_general | solution.py:477
  575.1 12.6 %fusion.70 = bf16[2,256,3072]{2,1,0:T(8,128)(2,1)S(1)} fusion(bf16[3072,2560]{1,0:T(8,128)(2,1)} %join.2, bf16[2,4,256,2560]{3,2,1,0:T(8,128)(2,1)} %attention_bwd.5), kind=kOutput, calls=%fused_computation.67 | convolution fusion | flops 8054636544 | bytes 21495808 | tf_op jit(solution)/shard_map/bse,de->bsd/dot_general | solution.py:477
  587.8 14.2 %fusion.67 = bf16[2,256,3072]{2,1,0:T(8,128)(2,1)} fusion(bf16[3072,2560]{1,0:T(8,128)(2,1)} %join.2, bf16[2,4,256,2560]{3,2,1,0:T(8,128)(2,1)} %attention_bwd.5), kind=kOutput, calls=%fused_computation.66 | convolution fusion | flops 8054636544 | bytes 21495808 | tf_op jit(solution)/shard_map/bse,de->bsd/dot_general | solution.py:477
  617.5 12.2 %fusion.26 = f32[1536,1280]{1,0:T(8,128)} fusion(f32[1536,1280]{1,0:T(8,128)} %collective-permute-done.26, bf16[2,4,256,1536]{3,2,1,0:T(8,128)(2,1)S(1)} %get-tuple-element.113, bf16[2,4,256,2560]{3,2,1,0:T(8,128)(2,1)S(1)} %bitcast.185), kind=kOutput, calls=%fused_computation.31 | convolution fusion | flops 8055029760 | bytes 27262976 | tf_op jit(solution)/shard_map/hbsd,hbse->de/dot_general | solution.py:477
  656.1 22.4 %fusion.43.near_ref = bf16[4,256,3072]{2,1,0:T(8,128)(2,1)} fusion(bf16[3072,2560]{1,0:T(8,128)(2,1)} %join.2, bf16[2,4,256,2560]{3,2,1,0:T(8,128)(2,1)} %attention_bwd.5), kind=kOutput, calls=%fused_computation.52 | convolution fusion | flops 16109273088 | bytes 27262976 | tf_op jit(solution)/shard_map/bse,de->bsd/dot_general | solution.py:477
  678.6 20.0 %collective-permute-done.28 = f32[2,384,640]{2,1,0:T(8,128)} collective-permute-done((f32[2,384,640]{2,1,0:T(8,128)}, f32[2,384,640]{2,1,0:T(8,128)}, u32[]{:S(2)}, u32[]{:S(2)}) %collective-permute-start.28) | collective-permute-done | bytes 1966112 | tf_op jit(solution)/shard_map/ppermute | solution.py:504
  700.6 12.4 %fusion.40.near_ref = bf16[4,256,3072]{2,1,0:T(8,128)(2,1)S(1)} fusion(bf16[1536,3072]{1,0:T(8,128)(2,1)} %join.3, bf16[2,4,256,1536]{3,2,1,0:T(8,128)(2,1)S(1)} %bitcast.187), kind=kOutput, calls=%fused_computation.51 | convolution fusion | flops 9666822144 | bytes 18874368 | tf_op jit(solution)/shard_map/bse,ed->bsd/dot_general | solution.py:477
  753.0 15.8 %collective-permute-done.41 = f32[768,384]{1,0:T(8,128)} collective-permute-done((f32[768,384]{1,0:T(8,128)}, f32[768,384]{1,0:T(8,128)}, u32[]{:S(2)}, u32[]{:S(2)}) %collective-permute-start.41) | collective-permute-done | bytes 1179680 | tf_op jit(solution)/shard_map/ppermute | solution.py:504
  771.4 19.5 %collective-permute-done.36.refs_3_ = f32[384,640]{1,0:T(8,128)S(1)} collective-permute-done((f32[384,640]{1,0:T(8,128)}, f32[384,640]{1,0:T(8,128)S(1)}, u32[]{:S(2)}, u32[]{:S(2)}) %collective-permute-start.36) | collective-permute-done | bytes 983072 | tf_op jit(solution)/shard_map/ppermute | solution.py:504
  (313 shorter events, 334.1 us)
Async XLA Ops:
  9.2 143.1 %collective-permute-start.4 = (bf16[384,2560]{1,0:T(8,128)(2,1)}, bf16[384,2560]{1,0:T(8,128)(2,1)S(1)}, u32[]{:S(2)}, u32[]{:S(2)}) collective-permute-start(bf16[384,2560]{1,0:T(8,128)(2,1)} %regroup.1.refs_0_), channel_id=1, source_target_pairs={{0,1},{1,0},{2,3},{3,2},{4,5},{5,4},{6,7},{7,6},{8,9},{9,8},{10,11... | collective-permute-start | bytes 5898248 | tf_op jit(solution)/shard_map/ppermute | solution.py:504
  12.9 160.5 %collective-permute-start.22 = (bf16[2,256,3072]{2,1,0:T(8,128)(2,1)}, bf16[2,256,3072]{2,1,0:T(8,128)(2,1)}, u32[]{:S(2)}, u32[]{:S(2)}) collective-permute-start(bf16[2,256,3072]{2,1,0:T(8,128)(2,1)} %slice.100), channel_id=1, source_target_pairs={{0,8},{8,0},{1,9},{9,1},{2,10},{10,2},{3,11},{11,3},{4,12},{12,4},... | collective-permute-start | bytes 9437192 | tf_op jit(solution)/shard_map/ppermute | solution.py:474
  14.7 103.1 %collective-permute-start.21 = (bf16[1,256,3072]{2,1,0:T(8,128)(2,1)S(1)}, bf16[1,256,3072]{2,1,0:T(8,128)(2,1)S(1)}, u32[]{:S(2)}, u32[]{:S(2)}) collective-permute-start(bf16[1,256,3072]{2,1,0:T(8,128)(2,1)S(1)} %get-tuple-element.181), channel_id=1, source_target_pairs={{0,8},{8,0},{1,9},{9,1},{2,10},{10,2},{3,11},{11,3},{4,12},{12,4},... | collective-permute-start | bytes 4718600 | tf_op jit(solution)/shard_map/ppermute | solution.py:474
  50.8 100.3 %collective-permute-start.20 = (bf16[1,256,3072]{2,1,0:T(8,128)(2,1)S(1)}, bf16[1,256,3072]{2,1,0:T(8,128)(2,1)S(1)}, u32[]{:S(2)}, u32[]{:S(2)}) collective-permute-start(bf16[1,256,3072]{2,1,0:T(8,128)(2,1)S(1)} %get-tuple-element.182), channel_id=1, source_target_pairs={{0,8},{8,0},{1,9},{9,1},{2,10},{10,2},{3,11},{11,3},{4,12},{12,4},... | collective-permute-start | bytes 4718600 | tf_op jit(solution)/shard_map/ppermute | solution.py:474
  53.9 98.9 %collective-permute-start.2 = (bf16[384,1280]{1,0:T(8,128)(2,1)S(1)}, bf16[384,1280]{1,0:T(8,128)(2,1)S(1)}, u32[]{:S(2)}, u32[]{:S(2)}) collective-permute-start(bf16[384,1280]{1,0:T(8,128)(2,1)S(1)} %slice.88), channel_id=1, source_target_pairs={{0,2},{1,3},{2,0},{3,1},{4,6},{5,7},{6,4},{7,5},{8,10},{9,11},{10,... | collective-permute-start | bytes 2949128 | tf_op jit(solution)/shard_map/ppermute | solution.py:504
  152.2 54.1 %collective-permute-start.5 = (bf16[384,2560]{1,0:T(8,128)(2,1)}, bf16[384,2560]{1,0:T(8,128)(2,1)}, u32[]{:S(2)}, u32[]{:S(2)}) collective-permute-start(bf16[384,2560]{1,0:T(8,128)(2,1)} %collective-permute-done.refs_1_), channel_id=1, source_target_pairs={{0,1},{1,0},{2,3},{3,2},{4,5},{5,4},{6,7},{7,6},{8,9},{9,8},{10,11... | collective-permute-start | bytes 5898248 | tf_op jit(solution)/shard_map/ppermute | solution.py:504
  152.2 54.1 %collective-permute-start.6 = (bf16[384,2560]{1,0:T(8,128)(2,1)}, bf16[384,2560]{1,0:T(8,128)(2,1)}, u32[]{:S(2)}, u32[]{:S(2)}) collective-permute-start(bf16[384,2560]{1,0:T(8,128)(2,1)} %collective-permute-done.1.refs_2_), channel_id=1, source_target_pairs={{0,1},{1,0},{2,3},{3,2},{4,5},{5,4},{6,7},{7,6},{8,9},{9,8},{10,11... | collective-permute-start | bytes 5898248 | tf_op jit(solution)/shard_map/ppermute | solution.py:504
  204.7 71.2 %collective-permute-start.10 = (bf16[2,256,3072]{2,1,0:T(8,128)(2,1)}, bf16[2,256,3072]{2,1,0:T(8,128)(2,1)S(1)}, u32[]{:S(2)}, u32[]{:S(2)}) collective-permute-start(bf16[2,256,3072]{2,1,0:T(8,128)(2,1)} %slice.90), channel_id=1, source_target_pairs={{0,8},{8,0},{1,9},{9,1},{2,10},{10,2},{3,11},{11,3},{4,12},{12,4},... | collective-permute-start | bytes 9437192 | tf_op jit(solution)/shard_map/ppermute | solution.py:474
  206.3 168.7 %collective-permute-start.15 = (bf16[1536,384]{1,0:T(8,128)(2,1)}, bf16[1536,384]{1,0:T(8,128)(2,1)}, u32[]{:S(2)}, u32[]{:S(2)}) collective-permute-start(bf16[1536,384]{1,0:T(8,128)(2,1)} %refs_0_.1), channel_id=1, source_target_pairs={{0,1},{1,0},{2,3},{3,2},{4,5},{5,4},{6,7},{7,6},{8,9},{9,8},{10,11... | collective-permute-start | bytes 3538952 | tf_op jit(solution)/shard_map/ppermute | solution.py:504
  206.3 135.7 %collective-permute-start.9 = (bf16[2,256,3072]{2,1,0:T(8,128)(2,1)}, bf16[2,256,3072]{2,1,0:T(8,128)(2,1)}, u32[]{:S(2)}, u32[]{:S(2)}) collective-permute-start(bf16[2,256,3072]{2,1,0:T(8,128)(2,1)} %slice.91), channel_id=1, source_target_pairs={{0,8},{8,0},{1,9},{9,1},{2,10},{10,2},{3,11},{11,3},{4,12},{12,4},... | collective-permute-start | bytes 9437192 | tf_op jit(solution)/shard_map/ppermute | solution.py:474
  221.7 153.2 %collective-permute-start.16 = (bf16[1536,384]{1,0:T(8,128)(2,1)}, bf16[1536,384]{1,0:T(8,128)(2,1)}, u32[]{:S(2)}, u32[]{:S(2)}) collective-permute-start(bf16[1536,384]{1,0:T(8,128)(2,1)} %collective-permute-done.11.refs_1_), channel_id=1, source_target_pairs={{0,1},{1,0},{2,3},{3,2},{4,5},{5,4},{6,7},{7,6},{8,9},{9,8},{10,11... | collective-permute-start | bytes 3538952 | tf_op jit(solution)/shard_map/ppermute | solution.py:504
  275.9 68.7 %collective-permute-start.13 = (bf16[768,384]{1,0:T(8,128)(2,1)S(1)}, bf16[768,384]{1,0:T(8,128)(2,1)S(1)}, u32[]{:S(2)}, u32[]{:S(2)}) collective-permute-start(bf16[768,384]{1,0:T(8,128)(2,1)S(1)} %slice.94), channel_id=1, source_target_pairs={{0,2},{1,3},{2,0},{3,1},{4,6},{5,7},{6,4},{7,5},{8,10},{9,11},{10,... | collective-permute-start | bytes 1769480 | tf_op jit(solution)/shard_map/ppermute | solution.py:504
  278.5 66.7 %collective-permute-start.14 = (bf16[768,384]{1,0:T(8,128)(2,1)S(1)}, bf16[768,384]{1,0:T(8,128)(2,1)S(1)}, u32[]{:S(2)}, u32[]{:S(2)}) collective-permute-start(bf16[768,384]{1,0:T(8,128)(2,1)S(1)} %slice.95), channel_id=1, source_target_pairs={{0,4},{1,5},{2,6},{3,7},{4,0},{5,1},{6,2},{7,3},{8,12},{9,13},{10,... | collective-permute-start | bytes 1769480 | tf_op jit(solution)/shard_map/ppermute | solution.py:504
  504.5 214.9 %collective-permute-start.31 = (bf16[2,256,3072]{2,1,0:T(8,128)(2,1)}, bf16[2,256,3072]{2,1,0:T(8,128)(2,1)}, u32[]{:S(2)}, u32[]{:S(2)}) collective-permute-start(bf16[2,256,3072]{2,1,0:T(8,128)(2,1)} %fusion.73), channel_id=1, source_target_pairs={{0,8},{8,0},{1,9},{9,1},{2,10},{10,2},{3,11},{11,3},{4,12},{12,4},... | collective-permute-start | bytes 9437192 | tf_op jit(solution)/shard_map/ppermute | solution.py:474
  548.0 57.5 %collective-permute-start.24 = (f32[768,768]{1,0:T(8,128)S(1)}, f32[768,768]{1,0:T(8,128)}, u32[]{:S(2)}, u32[]{:S(2)}) collective-permute-start(f32[768,768]{1,0:T(8,128)S(1)} %pad_maximum_fusion), channel_id=1, source_target_pairs={{0,2},{1,3},{2,0},{3,1},{4,6},{5,7},{6,4},{7,5},{8,10},{9,11},{10,... | collective-permute-start | bytes 7077896 | tf_op jit(solution)/shard_map/ppermute | solution.py:504
  549.5 56.5 %collective-permute-start.25 = (f32[768,768]{1,0:T(8,128)}, f32[768,768]{1,0:T(8,128)}, u32[]{:S(2)}, u32[]{:S(2)}) collective-permute-start(f32[768,768]{1,0:T(8,128)} %constant_dynamic-slice_fusion.6), channel_id=1, source_target_pairs={{0,4},{1,5},{2,6},{3,7},{4,0},{5,1},{6,2},{7,3},{8,12},{9,13},{10,... | collective-permute-start | bytes 7077896 | tf_op jit(solution)/shard_map/ppermute | solution.py:504
  563.7 53.8 %collective-permute-start.26 = (f32[1536,1280]{1,0:T(8,128)}, f32[1536,1280]{1,0:T(8,128)}, u32[]{:S(2)}, u32[]{:S(2)}) collective-permute-start(f32[1536,1280]{1,0:T(8,128)} %convolution_bitcast_fusion.3), channel_id=1, source_target_pairs={{0,1},{1,0},{2,3},{3,2},{4,5},{5,4},{6,7},{7,6},{8,9},{9,8},{10,11... | collective-permute-start | bytes 23592968 | tf_op jit(solution)/shard_map/ppermute | solution.py:504
  574.6 61.0 %collective-permute-start.27 = (f32[1536,1280]{1,0:T(8,128)}, f32[1536,1280]{1,0:T(8,128)}, u32[]{:S(2)}, u32[]{:S(2)}) collective-permute-start(f32[1536,1280]{1,0:T(8,128)} %convolution_bitcast_fusion.2), channel_id=1, source_target_pairs={{0,1},{1,0},{2,3},{3,2},{4,5},{5,4},{6,7},{7,6},{8,9},{9,8},{10,11... | collective-permute-start | bytes 23592968 | tf_op jit(solution)/shard_map/ppermute | solution.py:504
  605.5 115.3 %collective-permute-start.30 = (bf16[2,256,3072]{2,1,0:T(8,128)(2,1)}, bf16[2,256,3072]{2,1,0:T(8,128)(2,1)S(1)}, u32[]{:S(2)}, u32[]{:S(2)}) collective-permute-start(bf16[2,256,3072]{2,1,0:T(8,128)(2,1)} %fusion.76), channel_id=1, source_target_pairs={{0,8},{8,0},{1,9},{9,1},{2,10},{10,2},{3,11},{11,3},{4,12},{12,4},... | collective-permute-start | bytes 9437192 | tf_op jit(solution)/shard_map/ppermute | solution.py:474
  606.1 144.2 %collective-permute-start.35 = (bf16[2,256,3072]{2,1,0:T(8,128)(2,1)}, bf16[2,256,3072]{2,1,0:T(8,128)(2,1)}, u32[]{:S(2)}, u32[]{:S(2)}) collective-permute-start(bf16[2,256,3072]{2,1,0:T(8,128)(2,1)} %fusion.67), channel_id=1, source_target_pairs={{0,8},{8,0},{1,9},{9,1},{2,10},{10,2},{3,11},{11,3},{4,12},{12,4},... | collective-permute-start | bytes 9437192 | tf_op jit(solution)/shard_map/ppermute | solution.py:474
  719.4 49.3 %collective-permute-start.41 = (f32[768,384]{1,0:T(8,128)}, f32[768,384]{1,0:T(8,128)}, u32[]{:S(2)}, u32[]{:S(2)}) collective-permute-start(f32[768,384]{1,0:T(8,128)} %constant_dynamic-slice_fusion.1), channel_id=1, source_target_pairs={{0,4},{1,5},{2,6},{3,7},{4,0},{5,1},{6,2},{7,3},{8,12},{9,13},{10,... | collective-permute-start | bytes 3538952 | tf_op jit(solution)/shard_map/ppermute | solution.py:504
  720.8 49.0 %collective-permute-start.42 = (f32[768,384]{1,0:T(8,128)}, f32[768,384]{1,0:T(8,128)}, u32[]{:S(2)}, u32[]{:S(2)}) collective-permute-start(f32[768,384]{1,0:T(8,128)} %constant_dynamic-slice_fusion), channel_id=1, source_target_pairs={{0,2},{1,3},{2,0},{3,1},{4,6},{5,7},{6,4},{7,5},{8,10},{9,11},{10,... | collective-permute-start | bytes 3538952 | tf_op jit(solution)/shard_map/ppermute | solution.py:504
  744.6 68.8 %collective-permute-start.38 = (bf16[1,256,3072]{2,1,0:T(8,128)(2,1)}, bf16[1,256,3072]{2,1,0:T(8,128)(2,1)}, u32[]{:S(2)}, u32[]{:S(2)}) collective-permute-start(bf16[1,256,3072]{2,1,0:T(8,128)(2,1)} %get-tuple-element.184), channel_id=1, source_target_pairs={{0,8},{8,0},{1,9},{9,1},{2,10},{10,2},{3,11},{11,3},{4,12},{12,4},... | collective-permute-start | bytes 4718600 | tf_op jit(solution)/shard_map/ppermute | solution.py:474
  750.2 72.0 %collective-permute-start.40 = (bf16[1,256,3072]{2,1,0:T(8,128)(2,1)}, bf16[1,256,3072]{2,1,0:T(8,128)(2,1)}, u32[]{:S(2)}, u32[]{:S(2)}) collective-permute-start(bf16[1,256,3072]{2,1,0:T(8,128)(2,1)} %get-tuple-element.183), channel_id=1, source_target_pairs={{0,8},{8,0},{1,9},{9,1},{2,10},{10,2},{3,11},{11,3},{4,12},{12,4},... | collective-permute-start | bytes 4718600 | tf_op jit(solution)/shard_map/ppermute | solution.py:474
  (91 other events, 2443.0 us)

commit v6 on v4

--- a/solution.py
+++ b/solution.py
@@ -274,7 +274,8 @@
     result = slots[0]
     for i in range(1, total):
         result = result + slots[i]
-    out_ref[...] = result
+    for i in range(out_ref.shape[1] // HEAD_DIM):
+        out_ref[:, i * HEAD_DIM:(i + 1) * HEAD_DIM] = result[i:i + 1]
 
 
 def gain_sum(part, tp_size, dp_size):
@@ -285,7 +286,7 @@
     total = tp_size * dp_size
     result = pl.pallas_call(
         functools.partial(gain_sum_kernel, tp_size, dp_size),
-        out_shape=jax.ShapeDtypeStruct((sublanes, HEAD_DIM), F32),
+        out_shape=jax.ShapeDtypeStruct((1, rows), F32),
         in_specs=[pl.BlockSpec(memory_space=pltpu.VMEM)],
         out_specs=pl.BlockSpec(memory_space=pltpu.VMEM),
         scratch_shapes=[
@@ -296,7 +297,7 @@
         compiler_params=pltpu.CompilerParams(collective_id=0, has_side_effects=True),
         name="gain_sum",
     )(padded)
-    return result.reshape(-1)[:rows]
+    return result.reshape(rows)
 
 
 def finish_out_kernel(x_ref, near_ref, far_ref, *rest):
@@ -447,10 +448,11 @@
         step = batch // CHUNKS
         hidden_rec, grad_rec = [], []
         source = hidden
-        for i in range(CHUNKS):
-            piece = lax.optimization_barrier(source[i * step:(i + 1) * step])
+        for start, count in [(0, 1), (1, 1), (2, 2)]:
+            piece = lax.optimization_barrier(source[start:start + count])
             source = after(hidden, piece)
             hidden_rec.append(exchange(piece))
+        hidden_rec = [jnp.concatenate(hidden_rec[:2], axis=0), hidden_rec[2]]
         pieces = [(0, 2), (2, 1), (3, 1)]
         for start, count in pieces:
             grad_rec.append(exchange(grad_out[start:start + count]))
@@ -559,21 +561,25 @@
         hidden_out = None
         for i in range(CHUNKS):
             hidden_out = finish(finish_out_kernel, [hidden, after(out_near, *late_sent)], [out_far[i]], i * step, hidden_out)
-        early_sent, early_terms = second_stage(early_mine, early_far, [hidden_out])
-        dn_near = after(dn_near, *early_sent)
-        grad_hidden = None
         gain_parts = []
-        w_grads = None
-        for i, (start, count) in enumerate(pieces):
+
+        def finish_piece(index, dn_near, grad_hidden):
             grad_hidden, part = finish(
-                finish_grad_kernel, [hidden, grad_out, dn_near], [dn_far[i]], start, grad_hidden, gain
+                finish_grad_kernel, [hidden, grad_out, dn_near], [dn_far[index]], pieces[index][0], grad_hidden, gain
             )
             gain_parts.append(part)
-            if i == 0:
-                w_grads = ungroup([(mine, after(far, grad_hidden)) for mine, far in late_terms], groups // 2, groups, None)
-                dn_near = after(dn_near, *w_grads)
+            return grad_hidden
+
+        dn_near = after(dn_near, hidden_out)
+        grad_hidden = finish_piece(0, dn_near, None)
+        early_sent, early_terms = second_stage(early_mine, early_far, [grad_hidden])
+        dn_near = after(dn_near, *early_sent)
+        grad_hidden = finish_piece(1, dn_near, grad_hidden)
+        w_grads = ungroup([(mine, after(far, grad_hidden)) for mine, far in late_terms], groups // 2, groups, None)
+        w_grads = ungroup([(mine, after(far, *w_grads)) for mine, far in early_terms], 0, groups, w_grads)
+        grad_wq, grad_wk, grad_wv = w_grads
+        grad_hidden = finish_piece(2, after(dn_near, *w_grads), grad_hidden)
         grad_gain = gain_sum(jnp.sum(sum(gain_parts), axis=0), mesh.shape["tp"], mesh.shape["dp"])
-        grad_wq, grad_wk, grad_wv = ungroup([(mine, after(far, grad_gain)) for mine, far in early_terms], 0, groups, w_grads)
         return hidden_out, grad_hidden, grad_gain, grad_wq, grad_wk, grad_wv, grad_wo
 
     act_spec = P("dp", "tp", None)

time: 736 us -> 792 us (1.076)
  waiting for transfers between devices: 215 us -> 280 us
  Pallas kernels: 145 us -> 136 us
    ppermute x10 -> x11, waiting for transfers between devices: 146 us -> 256 us  [exchange(): return lax.ppermute(values, 'tp', swap)]
    all_gather x1, waiting for transfers between devices: 51.5 us -> 7.02 us  [local_block(): w_qkv = lax.all_gather(w_qkv, 'dp', axis=0, tiled=True)]
    unnamed x89 -> x76, local copies, waits for them, and re-layouts: 17.6 us -> 14.9 us
  transfers between devices with their start and end apart: 23 -> 24, of which waited for: 10 -> 10; matrix products, arithmetic and copies ran while one was open for 39% -> 37% of each run, Pallas kernels for 19% -> 17%
where the time goes in v6:
time: 792 us; the launch traced here: 787 us
  waiting for transfers between devices  280 us (35%)
  matrix products  256 us (32%)
  Pallas kernels  136 us (17%)
  local copies, waits for them, and re-layouts  50.3 us (6%)
  starting transfers between devices  25.9 us (3%)
  other arithmetic  15.5 us (2%)
  between operations  14.5 us (2%)
  blocking collectives  9.18 us (1%)
    dot_general x19, matrix products, mm(): return jnp.einsum(eq, a, b, preferred_element_type=F32)  256 us
    ppermute x11, waiting for transfers between devices, exchange(): return lax.ppermute(values, 'tp', swap)  256 us
    pallas_call x3, Pallas kernels, attention_bwd(): pl.pallas_call(functools.partial(attention_bwd_kernel, group_size), out_s...  52.8 us
    pallas_call x2, Pallas kernels, attention_fwd(): pl.pallas_call(functools.partial(attention_fwd_kernel, group_size), out_s...  33.6 us
    pallas_call x5, Pallas kernels, finish(): pl.pallas_call(kernel, out_shape=out_shape, grid=(count, half // row_bloc...  24.2 us
    ppermute x10, waiting for transfers between devices, pass_on(): return lax.ppermute(values, 'dp', [(i, i ^ bit) for i in range(8)])  15.9 us
  transfers between devices with their start and end apart: 24, of which 10 were waited for; matrix products, arithmetic and copies ran while one was open for 37% of the time, Pallas kernels for 17%

profile of v6, /device:TPU:0, one launch (start us, length us, event | category | flops | bytes accessed | tf_op | source)
XLA Modules:
  0.0 787.4 jit_solution(5613378219450483542)
XLA Ops:
  56.9 30.2 %collective-permute-done.2 = bf16[1,256,3072]{2,1,0:T(8,128)(2,1)} collective-permute-done((bf16[1,256,3072]{2,1,0:T(8,128)(2,1)}, bf16[1,256,3072]{2,1,0:T(8,128)(2,1)}, u32[]{:S(2)}, u32[]{:S(2)}) %collective-permute-start.2) | collective-permute-done | bytes 1572896 | tf_op jit(solution)/shard_map/ppermute | solution.py:434
  95.6 23.4 %fusion.47.own_ref = bf16[4,256,2560]{2,1,0:T(8,128)(2,1)} fusion(bf16[3072,2560]{1,0:T(8,128)(2,1)} %all-gather.4.cloned.1.call-done, bf16[4,256,3072]{2,1,0:T(8,128)(2,1)} %x_ref.9, f32[3072]{0:T(1024)S(1)} %bitcast.154, f32[4,256]{1,0:T(4,128)S(1)} %add_rsqrt_fusion), kind=kOutput, calls=%fused_computation.53 | convolution fusion | flops 16121331712 | bytes 27279360 | tf_op jit(solution)/shard_map/bsd,de->bse/dot_general | solution.py:437
  119.7 11.9 %fusion.62.rec_ref = bf16[2,256,2560]{2,1,0:T(8,128)(2,1)S(1)} fusion(bf16[3072,2560]{1,0:T(8,128)(2,1)} %all-gather.4.cloned.1.call-done, bf16[2,256,3072]{2,1,0:T(8,128)(2,1)S(1)} %constant_dynamic-update-slice_fusion.source_ref, f32[3072]{0:T(1024)S(1)} %bitcast.155, f32[2,256]{1,0:T(2,128)S(1)} %add_rsqrt_fusion.2), kind=kOutput, calls=%fused_computation.64 | convolution fusion | flops 8060665856 | bytes 21510144 | tf_op jit(solution)/shard_map/bsd,de->bse/dot_general | solution.py:437
  131.6 16.9 %attention_fwd.2 = (bf16[4,256,1536]{2,1,0:T(8,128)(2,1)}, bf16[4,256,1536]{2,1,0:T(8,128)(2,1)}) custom-call(s32[1]{0:T(128)} %bitcast.tp_ref, bf16[4,256,2560]{2,1,0:T(8,128)(2,1)} %fusion.47.own_ref, bf16[2,256,2560]{2,1,0:T(8,128)(2,1)S(1)} %fusion.62.rec_ref, f32[512,128]{1,0:T(8,128)S(1)} %get-tuple-element.144.cos_ref, f32[512,128]{1,0:T(8,128)S(1)} %copy-done.6), custom_call_target="tpu_custom_call" | custom-call | flops 2415919104 | bytes 5242880 | tf_op jit(solution)/shard_map/attention_fwd/pallas_call | solution.py:158
  148.5 139.9 %collective-permute-done.source_ref = bf16[2,256,3072]{2,1,0:T(8,128)(2,1)} collective-permute-done((bf16[2,256,3072]{2,1,0:T(8,128)(2,1)}, bf16[2,256,3072]{2,1,0:T(8,128)(2,1)}, u32[]{:S(2)}, u32[]{:S(2)}) %collective-permute-start) | collective-permute-done | bytes 3145760 | tf_op jit(solution)/shard_map/ppermute | solution.py:434
  291.0 13.0 %fusion.65.rec_ref = bf16[2,256,2560]{2,1,0:T(8,128)(2,1)S(1)} fusion(bf16[3072,2560]{1,0:T(8,128)(2,1)} %all-gather.4.cloned.1.call-done, bf16[2,256,3072]{2,1,0:T(8,128)(2,1)} %collective-permute-done.source_ref, f32[2,256]{1,0:T(2,128)S(1)} %add_rsqrt_fusion.1, f32[3072]{0:T(1024)S(1)} %bitcast.156), kind=kOutput, calls=%fused_computation.65 | convolution fusion | flops 8060665856 | bytes 21510144 | tf_op jit(solution)/shard_map/bsd,de->bse/dot_general | solution.py:437
  304.0 16.7 %attention_fwd.3 = (bf16[4,256,1536]{2,1,0:T(8,128)(2,1)}, bf16[4,256,1536]{2,1,0:T(8,128)(2,1)}) custom-call(s32[1]{0:T(128)} %bitcast.tp_ref, bf16[4,256,2560]{2,1,0:T(8,128)(2,1)} %fusion.47.own_ref, bf16[2,256,2560]{2,1,0:T(8,128)(2,1)S(1)} %fusion.65.rec_ref, ...), custom_call_target="tpu_custom_call", output_to_operand_aliasing={{0}: (5, {}), {1}: (6, {})} | custom-call | flops 2415919104 | bytes 5242880 | tf_op jit(solution)/shard_map/attention_fwd/pallas_call | solution.py:158
  336.8 13.7 %fusion.80.ga_own_ref = bf16[4,256,1536]{2,1,0:T(8,128)(2,1)} fusion(bf16[4,256,3072]{2,1,0:T(8,128)(2,1)S(1)} %bitcast.147, bf16[1536,3072]{1,0:T(8,128)(2,1)} %all-gather.6.cloned.1.call-done), kind=kOutput, calls=%fused_computation.70 | convolution fusion | flops 9665249280 | bytes 18874368 | tf_op jit(solution)/shard_map/bsd,ed->bse/dot_general | solution.py:437
  360.6 25.4 %attention_bwd.3.rest_0_ = bf16[2,4,256,2560]{3,2,1,0:T(8,128)(2,1)} custom-call(s32[1]{0:T(128)} %bitcast.tp_ref, bf16[4,256,2560]{2,1,0:T(8,128)(2,1)} %fusion.47.own_ref, bf16[2,256,2560]{2,1,0:T(8,128)(2,1)S(1)} %copy-done.9, f32[512,128]{1,0:T(8,128)S(1)} %get-tuple-element.144.cos_ref, f32[512,128]{1,0:T(8,128)S(1)} %copy-done.7, ...), custom_call_target="tpu_custom_call" | custom-call | flops 6039797760 | bytes 6291456 | tf_op jit(solution)/shard_map/attention_bwd/pallas_call | solution.py:190
  392.8 13.7 %attention_bwd.4.rest_0_ = bf16[2,4,256,2560]{3,2,1,0:T(8,128)(2,1)} custom-call(s32[1]{0:T(128)} %bitcast.tp_ref, bf16[4,256,2560]{2,1,0:T(8,128)(2,1)} %fusion.47.own_ref, bf16[2,256,2560]{2,1,0:T(8,128)(2,1)S(1)} %fusion.65.rec_ref, f32[512,128]{1,0:T(8,128)S(1)} %get-tuple-element.144.cos_ref, ...), custom_call_target="tpu_custom_call", output_to_operand_aliasing={{}: (7, {})} | custom-call | flops 3019898880 | bytes 3145728 | tf_op jit(solution)/shard_map/attention_bwd/pallas_call | solution.py:190
  406.6 13.3 %fusion.106 = f32[1536,3072,1]{1,0,2:T(8,128)} fusion(bf16[4,256,1536]{2,1,0:T(8,128)(2,1)S(1)} %copy-done.20, bf16[4,256,3072]{2,1,0:T(8,128)(2,1)S(1)} %bitcast.147), kind=kOutput, calls=%fused_computation.120 | convolution fusion | flops 9663676416 | bytes 28311552 | tf_op jit(solution)/shard_map/bse,bsd->ed/dot_general | solution.py:437
  419.9 19.6 %bitcast_add_fusion = f32[1536,3072]{1,0:T(8,128)} fusion(f32[1536,3072,1]{1,0,2:T(8,128)} %fusion.106, bf16[4,256,1536]{2,1,0:T(8,128)(2,1)} %get-tuple-element.77, bf16[1,256,3072]{2,1,0:T(8,128)(2,1)} %collective-permute-done.3, bf16[1,256,3072]{2,1,0:T(8,128)(2,1)} %collective-permute-done.4, bf16[2,256,3072]{2,1,0:T(8,128)(2,1)} %collective-permute-done.5), kind=kOutput, calls=%fused_computation | convolution fusion | flops 9674686464 | bytes 47185920 | tf_op jit(solution)/shard_map/bse,bsd->ed/dot_general | solution.py:437
  467.7 13.6 %attention_bwd.5 = bf16[2,4,256,2560]{3,2,1,0:T(8,128)(2,1)} custom-call(s32[1]{0:T(128)} %bitcast.tp_ref, bf16[4,256,2560]{2,1,0:T(8,128)(2,1)} %fusion.47.own_ref, bf16[2,256,2560]{2,1,0:T(8,128)(2,1)S(1)} %fusion.65.rec_ref, f32[512,128]{1,0:T(8,128)S(1)} %get-tuple-element.144.cos_ref, f32[512,128]{1,0:T(8,128)S(1)} %copy-done.7, ...), custom_call_target="tpu_custom_call", output_to_operand_aliasing={{}: (7, {})} | custom-call | flops 3019898880 | bytes 3145728 | tf_op jit(solution)/shard_map/attention_bwd/pallas_call | solution.py:190
  481.4 13.4 %convolution_bitcast_fusion.3 = f32[1536,1280]{1,0:T(8,128)} fusion(bf16[2,4,256,1536]{3,2,1,0:T(8,128)(2,1)S(1)} %get-tuple-element.88, bf16[2,4,256,2560]{3,2,1,0:T(8,128)(2,1)} %attention_bwd.5), kind=kOutput, calls=%fused_computation.33 | convolution fusion | flops 8053063680 | bytes 19398656 | tf_op jit(solution)/shard_map/hbsd,hbse->de/dot_general | solution.py:437
  496.8 14.6 %convolution_bitcast_fusion.2 = f32[1536,1280]{1,0:T(8,128)} fusion(bf16[2,4,256,1536]{3,2,1,0:T(8,128)(2,1)} %copy-done.3, bf16[2,4,256,2560]{3,2,1,0:T(8,128)(2,1)} %attention_bwd.5), kind=kOutput, calls=%fused_computation.32 | convolution fusion | flops 8053063680 | bytes 19398656 | tf_op jit(solution)/shard_map/hbsd,hbse->de/dot_general | solution.py:437
  511.4 14.1 %fusion.71 = bf16[2,256,3072]{2,1,0:T(8,128)(2,1)} fusion(bf16[3072,2560]{1,0:T(8,128)(2,1)} %all-gather.4.cloned.1.call-done, bf16[2,4,256,2560]{3,2,1,0:T(8,128)(2,1)} %attention_bwd.5), kind=kOutput, calls=%fused_computation.67 | convolution fusion | flops 8054636544 | bytes 21495808 | tf_op jit(solution)/shard_map/bse,de->bsd/dot_general | solution.py:437
  525.5 14.0 %fusion.68 = bf16[2,256,3072]{2,1,0:T(8,128)(2,1)} fusion(bf16[3072,2560]{1,0:T(8,128)(2,1)} %all-gather.4.cloned.1.call-done, bf16[2,4,256,2560]{3,2,1,0:T(8,128)(2,1)} %attention_bwd.5), kind=kOutput, calls=%fused_computation.66 | convolution fusion | flops 8054636544 | bytes 21495808 | tf_op jit(solution)/shard_map/bse,de->bsd/dot_general | solution.py:437
  544.8 13.4 %fusion.26 = f32[1536,1280]{1,0:T(8,128)S(1)} fusion(f32[1536,1280]{1,0:T(8,128)} %collective-permute-done.6, bf16[2,4,256,1536]{3,2,1,0:T(8,128)(2,1)S(1)} %bitcast.153, bf16[2,4,256,2560]{3,2,1,0:T(8,128)(2,1)} %attention_bwd.5), kind=kOutput, calls=%fused_computation.31 | convolution fusion | flops 8055029760 | bytes 27262976 | tf_op jit(solution)/shard_map/hbsd,hbse->de/dot_general | solution.py:437
  564.9 12.9 %fusion.25 = f32[1536,1280]{1,0:T(8,128)S(1)} fusion(f32[1536,1280]{1,0:T(8,128)} %collective-permute-done.7, bf16[2,4,256,1536]{3,2,1,0:T(8,128)(2,1)S(1)} %bitcast.153, bf16[2,4,256,2560]{3,2,1,0:T(8,128)(2,1)} %attention_bwd.5), kind=kOutput, calls=%fused_computation.29 | convolution fusion | flops 8055029760 | bytes 27262976 | tf_op jit(solution)/shard_map/hbsd,hbse->de/dot_general | solution.py:437
  582.9 22.6 %fusion.44.near_ref = bf16[4,256,3072]{2,1,0:T(8,128)(2,1)} fusion(bf16[3072,2560]{1,0:T(8,128)(2,1)} %all-gather.4.cloned.1.call-done, bf16[2,4,256,2560]{3,2,1,0:T(8,128)(2,1)} %attention_bwd.5), kind=kOutput, calls=%fused_computation.52 | convolution fusion | flops 16109273088 | bytes 27262976 | tf_op jit(solution)/shard_map/bse,de->bsd/dot_general | solution.py:437
  609.9 12.4 %fusion.41.near_ref = bf16[4,256,3072]{2,1,0:T(8,128)(2,1)S(1)} fusion(bf16[4,256,1536]{2,1,0:T(8,128)(2,1)S(1)} %copy-done.21, bf16[1536,3072]{1,0:T(8,128)(2,1)} %all-gather.6.cloned.1.call-done), kind=kOutput, calls=%fused_computation.51 | convolution fusion | flops 9666822144 | bytes 18874368 | tf_op jit(solution)/shard_map/bse,ed->bsd/dot_general | solution.py:437
  641.7 59.1 %collective-permute-done.14.far_ref = bf16[2,256,3072]{2,1,0:T(8,128)(2,1)S(1)} collective-permute-done((bf16[2,256,3072]{2,1,0:T(8,128)(2,1)}, bf16[2,256,3072]{2,1,0:T(8,128)(2,1)S(1)}, u32[]{:S(2)}, u32[]{:S(2)}) %collective-permute-start.14) | collective-permute-done | bytes 3145760 | tf_op jit(solution)/shard_map/ppermute | solution.py:434
  720.5 14.0 %collective-permute-done.17.far_ref = bf16[1,256,3072]{2,1,0:T(8,128)(2,1)S(1)} collective-permute-done((bf16[1,256,3072]{2,1,0:T(8,128)(2,1)}, bf16[1,256,3072]{2,1,0:T(8,128)(2,1)S(1)}, u32[]{:S(2)}, u32[]{:S(2)}) %collective-permute-start.17) | collective-permute-done | bytes 1572896 | tf_op jit(solution)/shard_map/ppermute | solution.py:434
  744.9 12.6 %collective-permute-done.19.refs_3_ = f32[384,640]{1,0:T(8,128)S(1)} collective-permute-done((f32[384,640]{1,0:T(8,128)}, f32[384,640]{1,0:T(8,128)S(1)}, u32[]{:S(2)}, u32[]{:S(2)}) %collective-permute-start.19) | collective-permute-done | bytes 983072 | tf_op jit(solution)/shard_map/ppermute | solution.py:516
  (180 shorter events, 218.6 us)
Async XLA Ops:
  7.2 88.4 %all-gather.4.cloned.1.call-start = ((), (), s32[]{:S(2)}) async-start(), calls=%async_computation.1 | async-start | bytes 17694720 | tf_op jit(solution)/shard_map/all_gather | solution.py:461
  11.0 309.6 %all-gather.6.cloned.1.call-start = ((), (), s32[]{:S(2)}) async-start(), calls=%async_computation.2 | async-start | bytes 10616832 | tf_op jit(solution)/shard_map/all_gather | solution.py:462
  11.8 768.9 %reduce-scatter.2.cloned.1.call-start = ((), (), s32[]{:S(2)}) async-start(), calls=%async_computation.3 | async-start | bytes 21233664 | tf_op jit(solution)/shard_map/reduce_scatter | solution.py:504
  14.5 38.8 %collective-permute-start.1 = (bf16[1,256,3072]{2,1,0:T(8,128)(2,1)}, bf16[1,256,3072]{2,1,0:T(8,128)(2,1)}, u32[]{:S(2)}, u32[]{:S(2)}) collective-permute-start(bf16[1,256,3072]{2,1,0:T(8,128)(2,1)} %slice.60), channel_id=1, source_target_pairs={{0,8},{8,0},{1,9},{9,1},{2,10},{10,2},{3,11},{11,3},{4,12},{12,4},... | collective-permute-start | bytes 4718600 | tf_op jit(solution)/shard_map/ppermute | solution.py:434
  20.7 66.4 %collective-permute-start.2 = (bf16[1,256,3072]{2,1,0:T(8,128)(2,1)}, bf16[1,256,3072]{2,1,0:T(8,128)(2,1)}, u32[]{:S(2)}, u32[]{:S(2)}) collective-permute-start(bf16[1,256,3072]{2,1,0:T(8,128)(2,1)} %slice.61), channel_id=1, source_target_pairs={{0,8},{8,0},{1,9},{9,1},{2,10},{10,2},{3,11},{11,3},{4,12},{12,4},... | collective-permute-start | bytes 4718600 | tf_op jit(solution)/shard_map/ppermute | solution.py:434
  24.7 361.3 %collective-permute-start.4 = (bf16[1,256,3072]{2,1,0:T(8,128)(2,1)}, bf16[1,256,3072]{2,1,0:T(8,128)(2,1)}, u32[]{:S(2)}, u32[]{:S(2)}) collective-permute-start(bf16[1,256,3072]{2,1,0:T(8,128)(2,1)} %get-tuple-element.137), channel_id=1, source_target_pairs={{0,8},{8,0},{1,9},{9,1},{2,10},{10,2},{3,11},{11,3},{4,12},{12,4},... | collective-permute-start | bytes 4718600 | tf_op jit(solution)/shard_map/ppermute | solution.py:434
  26.7 393.1 %collective-permute-start.3 = (bf16[1,256,3072]{2,1,0:T(8,128)(2,1)}, bf16[1,256,3072]{2,1,0:T(8,128)(2,1)}, u32[]{:S(2)}, u32[]{:S(2)}) collective-permute-start(bf16[1,256,3072]{2,1,0:T(8,128)(2,1)} %get-tuple-element.138), channel_id=1, source_target_pairs={{0,8},{8,0},{1,9},{9,1},{2,10},{10,2},{3,11},{11,3},{4,12},{12,4},... | collective-permute-start | bytes 4718600 | tf_op jit(solution)/shard_map/ppermute | solution.py:434
  30.7 319.7 %collective-permute-start.5 = (bf16[2,256,3072]{2,1,0:T(8,128)(2,1)}, bf16[2,256,3072]{2,1,0:T(8,128)(2,1)}, u32[]{:S(2)}, u32[]{:S(2)}) collective-permute-start(bf16[2,256,3072]{2,1,0:T(8,128)(2,1)} %slice.67), channel_id=1, source_target_pairs={{0,8},{8,0},{1,9},{9,1},{2,10},{10,2},{3,11},{11,3},{4,12},{12,4},... | collective-permute-start | bytes 9437192 | tf_op jit(solution)/shard_map/ppermute | solution.py:434
  53.3 235.1 %collective-permute-start = (bf16[2,256,3072]{2,1,0:T(8,128)(2,1)}, bf16[2,256,3072]{2,1,0:T(8,128)(2,1)}, u32[]{:S(2)}, u32[]{:S(2)}) collective-permute-start(bf16[2,256,3072]{2,1,0:T(8,128)(2,1)} %slice.62), channel_id=1, source_target_pairs={{0,8},{8,0},{1,9},{9,1},{2,10},{10,2},{3,11},{11,3},{4,12},{12,4},... | collective-permute-start | bytes 9437192 | tf_op jit(solution)/shard_map/ppermute | solution.py:434
  494.8 50.0 %collective-permute-start.6 = (f32[1536,1280]{1,0:T(8,128)}, f32[1536,1280]{1,0:T(8,128)}, u32[]{:S(2)}, u32[]{:S(2)}) collective-permute-start(f32[1536,1280]{1,0:T(8,128)} %convolution_bitcast_fusion.3), channel_id=1, source_target_pairs={{0,1},{1,0},{2,3},{3,2},{4,5},{5,4},{6,7},{7,6},{8,9},{9,8},{10,11... | collective-permute-start | bytes 23592968 | tf_op jit(solution)/shard_map/ppermute | solution.py:516
  494.8 127.6 %collective-permute-start.11 = (bf16[2,256,3072]{2,1,0:T(8,128)(2,1)}, bf16[2,256,3072]{2,1,0:T(8,128)(2,1)}, u32[]{:S(2)}, u32[]{:S(2)}) collective-permute-start(bf16[2,256,3072]{2,1,0:T(8,128)(2,1)} %fusion.74), channel_id=1, source_target_pairs={{0,8},{8,0},{1,9},{9,1},{2,10},{10,2},{3,11},{11,3},{4,12},{12,4},... | collective-permute-start | bytes 9437192 | tf_op jit(solution)/shard_map/ppermute | solution.py:434
  496.4 139.9 %collective-permute-start.10 = (bf16[2,256,3072]{2,1,0:T(8,128)(2,1)}, bf16[2,256,3072]{2,1,0:T(8,128)(2,1)S(1)}, u32[]{:S(2)}, u32[]{:S(2)}) collective-permute-start(bf16[2,256,3072]{2,1,0:T(8,128)(2,1)} %fusion.77), channel_id=1, source_target_pairs={{0,8},{8,0},{1,9},{9,1},{2,10},{10,2},{3,11},{11,3},{4,12},{12,4},... | collective-permute-start | bytes 9437192 | tf_op jit(solution)/shard_map/ppermute | solution.py:434
  511.4 51.8 %collective-permute-start.7 = (f32[1536,1280]{1,0:T(8,128)}, f32[1536,1280]{1,0:T(8,128)}, u32[]{:S(2)}, u32[]{:S(2)}) collective-permute-start(f32[1536,1280]{1,0:T(8,128)} %convolution_bitcast_fusion.2), channel_id=1, source_target_pairs={{0,1},{1,0},{2,3},{3,2},{4,5},{5,4},{6,7},{7,6},{8,9},{9,8},{10,11... | collective-permute-start | bytes 23592968 | tf_op jit(solution)/shard_map/ppermute | solution.py:516
  539.5 161.3 %collective-permute-start.14 = (bf16[2,256,3072]{2,1,0:T(8,128)(2,1)}, bf16[2,256,3072]{2,1,0:T(8,128)(2,1)S(1)}, u32[]{:S(2)}, u32[]{:S(2)}) collective-permute-start(bf16[2,256,3072]{2,1,0:T(8,128)(2,1)} %fusion.68), channel_id=1, source_target_pairs={{0,8},{8,0},{1,9},{9,1},{2,10},{10,2},{3,11},{11,3},{4,12},{12,4},... | collective-permute-start | bytes 9437192 | tf_op jit(solution)/shard_map/ppermute | solution.py:434
  561.7 45.5 %collective-permute-start.8 = (f32[2,384,640]{2,1,0:T(8,128)}, f32[2,384,640]{2,1,0:T(8,128)}, u32[]{:S(2)}, u32[]{:S(2)}) collective-permute-start(f32[2,384,640]{2,1,0:T(8,128)} %dynamic-slice_bitcast_fusion.3), channel_id=1, source_target_pairs={{0,2},{1,3},{2,0},{3,1},{4,6},{5,7},{6,4},{7,5},{8,10},{9,11},{10,... | collective-permute-start | bytes 5898248 | tf_op jit(solution)/shard_map/ppermute | solution.py:516
  563.2 45.5 %collective-permute-start.9 = (f32[2,384,640]{2,1,0:T(8,128)}, f32[2,384,640]{2,1,0:T(8,128)}, u32[]{:S(2)}, u32[]{:S(2)}) collective-permute-start(f32[2,384,640]{2,1,0:T(8,128)} %dynamic-slice_bitcast_fusion.2), channel_id=1, source_target_pairs={{0,4},{1,5},{2,6},{3,7},{4,0},{5,1},{6,2},{7,3},{8,12},{9,13},{10,... | collective-permute-start | bytes 5898248 | tf_op jit(solution)/shard_map/ppermute | solution.py:516
  607.2 104.3 %collective-permute-start.12 = (f32[2,384,640]{2,1,0:T(8,128)}, f32[2,384,640]{2,1,0:T(8,128)}, u32[]{:S(2)}, u32[]{:S(2)}) collective-permute-start(f32[2,384,640]{2,1,0:T(8,128)} %dynamic-slice_bitcast_fusion.1), channel_id=1, source_target_pairs={{0,2},{1,3},{2,0},{3,1},{4,6},{5,7},{6,4},{7,5},{8,10},{9,11},{10,... | collective-permute-start | bytes 5898248 | tf_op jit(solution)/shard_map/ppermute | solution.py:516
  608.7 104.3 %collective-permute-start.13 = (f32[2,384,640]{2,1,0:T(8,128)}, f32[2,384,640]{2,1,0:T(8,128)}, u32[]{:S(2)}, u32[]{:S(2)}) collective-permute-start(f32[2,384,640]{2,1,0:T(8,128)} %dynamic-slice_bitcast_fusion), channel_id=1, source_target_pairs={{0,4},{1,5},{2,6},{3,7},{4,0},{5,1},{6,2},{7,3},{8,12},{9,13},{10,... | collective-permute-start | bytes 5898248 | tf_op jit(solution)/shard_map/ppermute | solution.py:516
  622.4 112.1 %collective-permute-start.17 = (bf16[1,256,3072]{2,1,0:T(8,128)(2,1)}, bf16[1,256,3072]{2,1,0:T(8,128)(2,1)S(1)}, u32[]{:S(2)}, u32[]{:S(2)}) collective-permute-start(bf16[1,256,3072]{2,1,0:T(8,128)(2,1)} %get-tuple-element.140), channel_id=1, source_target_pairs={{0,8},{8,0},{1,9},{9,1},{2,10},{10,2},{3,11},{11,3},{4,12},{12,4},... | collective-permute-start | bytes 4718600 | tf_op jit(solution)/shard_map/ppermute | solution.py:434
  636.3 131.4 %collective-permute-start.20 = (bf16[1,256,3072]{2,1,0:T(8,128)(2,1)}, bf16[1,256,3072]{2,1,0:T(8,128)(2,1)S(1)}, u32[]{:S(2)}, u32[]{:S(2)}) collective-permute-start(bf16[1,256,3072]{2,1,0:T(8,128)(2,1)} %get-tuple-element.139), channel_id=1, source_target_pairs={{0,8},{8,0},{1,9},{9,1},{2,10},{10,2},{3,11},{11,3},{4,12},{12,4},... | collective-permute-start | bytes 4718600 | tf_op jit(solution)/shard_map/ppermute | solution.py:434
  700.8 40.7 %collective-permute-start.16 = (f32[384,640]{1,0:T(8,128)}, f32[384,640]{1,0:T(8,128)S(1)}, u32[]{:S(2)}, u32[]{:S(2)}) collective-permute-start(f32[384,640]{1,0:T(8,128)} %dynamic-slice_bitcast_fusion.11), channel_id=1, source_target_pairs={{0,4},{1,5},{2,6},{3,7},{4,0},{5,1},{6,2},{7,3},{8,12},{9,13},{10,... | collective-permute-start | bytes 2949128 | tf_op jit(solution)/shard_map/ppermute | solution.py:516
  711.5 29.9 %collective-permute-start.18 = (f32[384,640]{1,0:T(8,128)}, f32[384,640]{1,0:T(8,128)S(1)}, u32[]{:S(2)}, u32[]{:S(2)}) collective-permute-start(f32[384,640]{1,0:T(8,128)} %dynamic-slice_bitcast_fusion.10), channel_id=1, source_target_pairs={{0,2},{1,3},{2,0},{3,1},{4,6},{5,7},{6,4},{7,5},{8,10},{9,11},{10,... | collective-permute-start | bytes 2949128 | tf_op jit(solution)/shard_map/ppermute | solution.py:516
  719.9 25.0 %collective-permute-start.15 = (f32[384,640]{1,0:T(8,128)}, f32[384,640]{1,0:T(8,128)S(1)}, u32[]{:S(2)}, u32[]{:S(2)}) collective-permute-start(f32[384,640]{1,0:T(8,128)} %dynamic-slice_bitcast_fusion.9), channel_id=1, source_target_pairs={{0,4},{1,5},{2,6},{3,7},{4,0},{5,1},{6,2},{7,3},{8,12},{9,13},{10,... | collective-permute-start | bytes 2949128 | tf_op jit(solution)/shard_map/ppermute | solution.py:516
  734.5 23.1 %collective-permute-start.19 = (f32[384,640]{1,0:T(8,128)}, f32[384,640]{1,0:T(8,128)S(1)}, u32[]{:S(2)}, u32[]{:S(2)}) collective-permute-start(f32[384,640]{1,0:T(8,128)} %dynamic-slice_bitcast_fusion.8), channel_id=1, source_target_pairs={{0,2},{1,3},{2,0},{3,1},{4,6},{5,7},{6,4},{7,5},{8,10},{9,11},{10,... | collective-permute-start | bytes 2949128 | tf_op jit(solution)/shard_map/ppermute | solution.py:516
  (36 other events, 715.1 us)
Sparse Core Ops, SparseCore 0:
  11.2 84.3 all-gather.3
  97.4 56.7 all-gather.5
  439.7 121.8 reduce-scatter.1

commit v7 on v6

--- a/solution.py
+++ b/solution.py
@@ -539,7 +539,8 @@
             mine = pick(total[0], 0, along_y), pick(total[1], 0, along_x)
             return sent, [(mine[0], pass_on(sent[0], 4)), (mine[1], pass_on(sent[1], 2))]
 
-        gqkv_rec = after(gqkv, early_sent)[1]
+        late_sent, late_mine, late_far = first_stage(weight_grad(normed_mine, late, [early_sent]), late_far)
+        gqkv_rec = after(gqkv, *late_sent)[1]
         dn_send = []
         for i in range(CHUNKS):
             dn_send.append(lax.optimization_barrier(mm("bse,de->bsd", gqkv_rec[i * step:(i + 1) * step], w_qkv).astype(BF16)))
@@ -551,8 +552,7 @@
         for i in range(3):
             dn_far.append(exchange(dn_sent[i]))
 
-        late_sent, late_mine, late_far = first_stage(weight_grad(normed_mine, late, dn_send), late_far)
-        early_sent, early_mine, early_far = first_stage(weight_grad(normed_mine, early, late_sent), early_far)
+        early_sent, early_mine, early_far = first_stage(weight_grad(normed_mine, early, dn_send), early_far)
 
         attn_own, gqkv = after((attn_own, gqkv), *early_sent)
         out_near = lax.optimization_barrier(mm("bse,ed->bsd", attn_own, w_o).astype(BF16))

time: 792 us -> 734 us (0.927)
  waiting for transfers between devices: 280 us -> 222 us
    ppermute x11, waiting for transfers between devices: 256 us -> 197 us  [exchange(): return lax.ppermute(values, 'tp', swap)]
    ppermute x10, waiting for transfers between devices: 15.9 us -> 24.4 us  [pass_on(): return lax.ppermute(values, 'dp', [(i, i ^ bit) for i in range(8)])]
    unnamed x76 -> x80, local copies, waits for them, and re-layouts: 14.9 us -> 19 us
  transfers between devices with their start and end apart: 24 -> 24, of which waited for: 10 -> 9; matrix products, arithmetic and copies ran while one was open for 37% -> 38% of each run, Pallas kernels for 17% -> 19%
where the time goes in v7:
time: 734 us; the launch traced here: 725 us
  matrix products  250 us (34%)
  waiting for transfers between devices  222 us (30%)
  Pallas kernels  140 us (19%)
  local copies, waits for them, and re-layouts  47.1 us (6%)
  starting transfers between devices  27.4 us (4%)
  other arithmetic  15.7 us (2%)
  between operations  14.7 us (2%)
  blocking collectives  9.22 us (1%)
    dot_general x19, matrix products, mm(): return jnp.einsum(eq, a, b, preferred_element_type=F32)  250 us
    ppermute x11, waiting for transfers between devices, exchange(): return lax.ppermute(values, 'tp', swap)  197 us
    pallas_call x3, Pallas kernels, attention_bwd(): pl.pallas_call(functools.partial(attention_bwd_kernel, group_size), out_s...  53.9 us
    pallas_call x2, Pallas kernels, attention_fwd(): pl.pallas_call(functools.partial(attention_fwd_kernel, group_size), out_s...  34 us
    pallas_call x5, Pallas kernels, finish(): pl.pallas_call(kernel, out_shape=out_shape, grid=(count, half // row_bloc...  26.3 us
    ppermute x10, waiting for transfers between devices, pass_on(): return lax.ppermute(values, 'dp', [(i, i ^ bit) for i in range(8)])  24.4 us
    unnamed x80, local copies, waits for them, and re-layouts  19 us
    ppermute x11, starting transfers between devices, exchange(): return lax.ppermute(values, 'tp', swap)  15.4 us
  transfers between devices with their start and end apart: 24, of which 9 were waited for; matrix products, arithmetic and copies ran while one was open for 38% of the time, Pallas kernels for 19%

profile of v7, /device:TPU:0, one launch (start us, length us, event | category | flops | bytes accessed | tf_op | source)
XLA Modules:
  0.0 725.3 jit_solution(4122193902165910864)
XLA Ops:
  52.1 109.5 %collective-permute-done.1 = bf16[1,256,3072]{2,1,0:T(8,128)(2,1)} collective-permute-done((bf16[1,256,3072]{2,1,0:T(8,128)(2,1)}, bf16[1,256,3072]{2,1,0:T(8,128)(2,1)}, u32[]{:S(2)}, u32[]{:S(2)}) %collective-permute-start.1) | collective-permute-done | bytes 1572896 | tf_op jit(solution)/shard_map/ppermute | solution.py:434
  178.1 23.3 %fusion.47.own_ref = bf16[4,256,2560]{2,1,0:T(8,128)(2,1)} fusion(bf16[3072,2560]{1,0:T(8,128)(2,1)} %all-gather.4.cloned.1.call-done, bf16[4,256,3072]{2,1,0:T(8,128)(2,1)} %x_ref.9, f32[3072]{0:T(1024)S(1)} %bitcast.159, f32[4,256]{1,0:T(4,128)S(1)} %add_rsqrt_fusion), kind=kOutput, calls=%fused_computation.53 | convolution fusion | flops 16121331712 | bytes 27279360 | tf_op jit(solution)/shard_map/bsd,de->bse/dot_general | solution.py:437
  202.1 12.1 %fusion.62.rec_ref = bf16[2,256,2560]{2,1,0:T(8,128)(2,1)S(1)} fusion(bf16[3072,2560]{1,0:T(8,128)(2,1)} %all-gather.4.cloned.1.call-done, bf16[2,256,3072]{2,1,0:T(8,128)(2,1)S(1)} %constant_dynamic-update-slice_fusion.source_ref, f32[3072]{0:T(1024)S(1)} %bitcast.160, f32[2,256]{1,0:T(2,128)S(1)} %add_rsqrt_fusion.2), kind=kOutput, calls=%fused_computation.64 | convolution fusion | flops 8060665856 | bytes 21510144 | tf_op jit(solution)/shard_map/bsd,de->bse/dot_general | solution.py:437
  214.2 17.1 %attention_fwd.2 = (bf16[4,256,1536]{2,1,0:T(8,128)(2,1)}, bf16[4,256,1536]{2,1,0:T(8,128)(2,1)}) custom-call(s32[1]{0:T(128)} %bitcast.tp_ref, bf16[4,256,2560]{2,1,0:T(8,128)(2,1)} %fusion.47.own_ref, bf16[2,256,2560]{2,1,0:T(8,128)(2,1)S(1)} %fusion.62.rec_ref, f32[512,128]{1,0:T(8,128)S(1)} %get-tuple-element.144.cos_ref, f32[512,128]{1,0:T(8,128)S(1)} %copy-done.4), custom_call_target="tpu_custom_call" | custom-call | flops 2415919104 | bytes 5242880 | tf_op jit(solution)/shard_map/attention_fwd/pallas_call | solution.py:158
  233.8 12.7 %fusion.65.rec_ref = bf16[2,256,2560]{2,1,0:T(8,128)(2,1)S(1)} fusion(bf16[3072,2560]{1,0:T(8,128)(2,1)} %all-gather.4.cloned.1.call-done, bf16[2,256,3072]{2,1,0:T(8,128)(2,1)} %collective-permute-done.source_ref, f32[2,256]{1,0:T(2,128)S(1)} %add_rsqrt_fusion.1, f32[3072]{0:T(1024)S(1)} %bitcast.161), kind=kOutput, calls=%fused_computation.65 | convolution fusion | flops 8060665856 | bytes 21510144 | tf_op jit(solution)/shard_map/bsd,de->bse/dot_general | solution.py:437
  246.6 16.9 %attention_fwd.3 = (bf16[4,256,1536]{2,1,0:T(8,128)(2,1)}, bf16[4,256,1536]{2,1,0:T(8,128)(2,1)}) custom-call(s32[1]{0:T(128)} %bitcast.tp_ref, bf16[4,256,2560]{2,1,0:T(8,128)(2,1)} %fusion.47.own_ref, bf16[2,256,2560]{2,1,0:T(8,128)(2,1)S(1)} %fusion.65.rec_ref, ...), custom_call_target="tpu_custom_call", output_to_operand_aliasing={{0}: (5, {}), {1}: (6, {})} | custom-call | flops 2415919104 | bytes 5242880 | tf_op jit(solution)/shard_map/attention_fwd/pallas_call | solution.py:158
  279.9 13.7 %fusion.80.ga_own_ref = bf16[4,256,1536]{2,1,0:T(8,128)(2,1)} fusion(bf16[4,256,3072]{2,1,0:T(8,128)(2,1)S(1)} %bitcast.147, bf16[1536,3072]{1,0:T(8,128)(2,1)} %all-gather.6.cloned.1.call-done), kind=kOutput, calls=%fused_computation.70 | convolution fusion | flops 9665249280 | bytes 18874368 | tf_op jit(solution)/shard_map/bsd,ed->bse/dot_general | solution.py:437
  295.6 9.5 %fusion.89.ga_rec_ref = bf16[2,256,1536]{2,1,0:T(8,128)(2,1)S(1)} fusion(bf16[2,256,3072]{2,1,0:T(8,128)(2,1)} %collective-permute-done.5, bf16[1536,3072]{1,0:T(8,128)(2,1)} %all-gather.6.cloned.1.call-done), kind=kOutput, calls=%fused_computation.75 | convolution fusion | flops 4832624640 | bytes 14155776 | tf_op jit(solution)/shard_map/bsd,ed->bse/dot_general | solution.py:437
  305.1 25.9 %attention_bwd.3.rest_0_ = bf16[2,4,256,2560]{3,2,1,0:T(8,128)(2,1)} custom-call(s32[1]{0:T(128)} %bitcast.tp_ref, bf16[4,256,2560]{2,1,0:T(8,128)(2,1)} %fusion.47.own_ref, bf16[2,256,2560]{2,1,0:T(8,128)(2,1)S(1)} %copy-done.9, f32[512,128]{1,0:T(8,128)S(1)} %get-tuple-element.144.cos_ref, f32[512,128]{1,0:T(8,128)S(1)} %copy-done.5, ...), custom_call_target="tpu_custom_call" | custom-call | flops 6039797760 | bytes 6291456 | tf_op jit(solution)/shard_map/attention_bwd/pallas_call | solution.py:190
  337.8 13.9 %attention_bwd.4.rest_0_ = bf16[2,4,256,2560]{3,2,1,0:T(8,128)(2,1)} custom-call(s32[1]{0:T(128)} %bitcast.tp_ref, bf16[4,256,2560]{2,1,0:T(8,128)(2,1)} %fusion.47.own_ref, bf16[2,256,2560]{2,1,0:T(8,128)(2,1)S(1)} %fusion.65.rec_ref, f32[512,128]{1,0:T(8,128)S(1)} %get-tuple-element.144.cos_ref, ...), custom_call_target="tpu_custom_call", output_to_operand_aliasing={{}: (7, {})} | custom-call | flops 3019898880 | bytes 3145728 | tf_op jit(solution)/shard_map/attention_bwd/pallas_call | solution.py:190
  351.7 13.4 %fusion.106 = f32[1536,3072,1]{1,0,2:T(8,128)} fusion(bf16[4,256,1536]{2,1,0:T(8,128)(2,1)S(1)} %copy-done.20, bf16[4,256,3072]{2,1,0:T(8,128)(2,1)S(1)} %bitcast.147), kind=kOutput, calls=%fused_computation.120 | convolution fusion | flops 9663676416 | bytes 28311552 | tf_op jit(solution)/shard_map/bse,bsd->ed/dot_general | solution.py:437
  365.1 19.8 %bitcast_add_fusion = f32[1536,3072]{1,0:T(8,128)} fusion(f32[1536,3072,1]{1,0,2:T(8,128)} %fusion.106, bf16[4,256,1536]{2,1,0:T(8,128)(2,1)} %get-tuple-element.77, bf16[1,256,3072]{2,1,0:T(8,128)(2,1)} %collective-permute-done.3, bf16[1,256,3072]{2,1,0:T(8,128)(2,1)} %collective-permute-done.4, bf16[2,256,3072]{2,1,0:T(8,128)(2,1)} %collective-permute-done.5), kind=kOutput, calls=%fused_computation | convolution fusion | flops 9674686464 | bytes 47185920 | tf_op jit(solution)/shard_map/bse,bsd->ed/dot_general | solution.py:437
  391.9 14.1 %attention_bwd.5 = bf16[2,4,256,2560]{3,2,1,0:T(8,128)(2,1)} custom-call(s32[1]{0:T(128)} %bitcast.tp_ref, bf16[4,256,2560]{2,1,0:T(8,128)(2,1)} %fusion.47.own_ref, bf16[2,256,2560]{2,1,0:T(8,128)(2,1)S(1)} %fusion.65.rec_ref, f32[512,128]{1,0:T(8,128)S(1)} %get-tuple-element.144.cos_ref, f32[512,128]{1,0:T(8,128)S(1)} %copy-done.5, ...), custom_call_target="tpu_custom_call", output_to_operand_aliasing={{}: (7, {})} | custom-call | flops 3019898880 | bytes 3145728 | tf_op jit(solution)/shard_map/attention_bwd/pallas_call | solution.py:190
  406.0 15.3 %convolution_bitcast_fusion.3 = f32[1536,1280]{1,0:T(8,128)} fusion(bf16[2,4,256,1536]{3,2,1,0:T(8,128)(2,1)S(1)} %bitcast.155, bf16[2,4,256,2560]{3,2,1,0:T(8,128)(2,1)} %attention_bwd.5), kind=kOutput, calls=%fused_computation.33 | convolution fusion | flops 8053063680 | bytes 19398656 | tf_op jit(solution)/shard_map/hbsd,hbse->de/dot_general | solution.py:437
  421.4 10.7 %convolution_bitcast_fusion.2 = f32[1536,1280]{1,0:T(8,128)} fusion(bf16[2,4,256,1536]{3,2,1,0:T(8,128)(2,1)S(1)} %bitcast.155, bf16[2,4,256,2560]{3,2,1,0:T(8,128)(2,1)S(1)} %copy-done.10), kind=kOutput, calls=%fused_computation.32 | convolution fusion | flops 8053063680 | bytes 19398656 | tf_op jit(solution)/shard_map/hbsd,hbse->de/dot_general | solution.py:437
  434.6 14.1 %fusion.26 = f32[1536,1280]{1,0:T(8,128)S(1)} fusion(f32[1536,1280]{1,0:T(8,128)} %collective-permute-done.6, bf16[2,4,256,1536]{3,2,1,0:T(8,128)(2,1)} %copy-done.2, bf16[2,4,256,2560]{3,2,1,0:T(8,128)(2,1)} %attention_bwd.5), kind=kOutput, calls=%fused_computation.31 | convolution fusion | flops 8055029760 | bytes 27262976 | tf_op jit(solution)/shard_map/hbsd,hbse->de/dot_general | solution.py:437
  455.7 12.7 %fusion.71 = bf16[2,256,3072]{2,1,0:T(8,128)(2,1)S(1)} fusion(bf16[3072,2560]{1,0:T(8,128)(2,1)} %all-gather.4.cloned.1.call-done, bf16[2,4,256,2560]{3,2,1,0:T(8,128)(2,1)} %attention_bwd.5), kind=kOutput, calls=%fused_computation.67 | convolution fusion | flops 8054636544 | bytes 21495808 | tf_op jit(solution)/shard_map/bse,de->bsd/dot_general | solution.py:437
  468.4 13.9 %fusion.68 = bf16[2,256,3072]{2,1,0:T(8,128)(2,1)} fusion(bf16[3072,2560]{1,0:T(8,128)(2,1)} %all-gather.4.cloned.1.call-done, bf16[2,4,256,2560]{3,2,1,0:T(8,128)(2,1)} %attention_bwd.5), kind=kOutput, calls=%fused_computation.66 | convolution fusion | flops 8054636544 | bytes 21495808 | tf_op jit(solution)/shard_map/bse,de->bsd/dot_general | solution.py:437
  482.3 13.0 %fusion.25 = f32[1536,1280]{1,0:T(8,128)S(1)} fusion(f32[1536,1280]{1,0:T(8,128)} %collective-permute-done.7, bf16[2,4,256,1536]{3,2,1,0:T(8,128)(2,1)S(1)} %bitcast.153, bf16[2,4,256,2560]{3,2,1,0:T(8,128)(2,1)} %attention_bwd.5), kind=kOutput, calls=%fused_computation.29 | convolution fusion | flops 8055029760 | bytes 27262976 | tf_op jit(solution)/shard_map/hbsd,hbse->de/dot_general | solution.py:437
  501.7 22.2 %fusion.44.near_ref = bf16[4,256,3072]{2,1,0:T(8,128)(2,1)} fusion(bf16[3072,2560]{1,0:T(8,128)(2,1)} %all-gather.4.cloned.1.call-done, bf16[2,4,256,2560]{3,2,1,0:T(8,128)(2,1)} %attention_bwd.5), kind=kOutput, calls=%fused_computation.52 | convolution fusion | flops 16109273088 | bytes 27262976 | tf_op jit(solution)/shard_map/bse,de->bsd/dot_general | solution.py:437
  536.2 13.5 %fusion.41.near_ref = bf16[4,256,3072]{2,1,0:T(8,128)(2,1)S(1)} fusion(bf16[4,256,1536]{2,1,0:T(8,128)(2,1)} %get-tuple-element.97, bf16[1536,3072]{1,0:T(8,128)(2,1)} %all-gather.6.cloned.1.call-done), kind=kOutput, calls=%fused_computation.51 | convolution fusion | flops 9666822144 | bytes 18874368 | tf_op jit(solution)/shard_map/bse,ed->bsd/dot_general | solution.py:437
  576.8 61.8 %collective-permute-done.14.far_ref = bf16[2,256,3072]{2,1,0:T(8,128)(2,1)S(1)} collective-permute-done((bf16[2,256,3072]{2,1,0:T(8,128)(2,1)}, bf16[2,256,3072]{2,1,0:T(8,128)(2,1)S(1)}, u32[]{:S(2)}, u32[]{:S(2)}) %collective-permute-start.14) | collective-permute-done | bytes 3145760 | tf_op jit(solution)/shard_map/ppermute | solution.py:434
  661.8 10.6 %collective-permute-done.17.far_ref = bf16[1,256,3072]{2,1,0:T(8,128)(2,1)} collective-permute-done((bf16[1,256,3072]{2,1,0:T(8,128)(2,1)}, bf16[1,256,3072]{2,1,0:T(8,128)(2,1)}, u32[]{:S(2)}, u32[]{:S(2)}) %collective-permute-start.17) | collective-permute-done | bytes 1572896 | tf_op jit(solution)/shard_map/ppermute | solution.py:434
  683.4 12.9 %collective-permute-done.19.refs_3_ = f32[384,640]{1,0:T(8,128)S(1)} collective-permute-done((f32[384,640]{1,0:T(8,128)}, f32[384,640]{1,0:T(8,128)S(1)}, u32[]{:S(2)}, u32[]{:S(2)}) %collective-permute-start.19) | collective-permute-done | bytes 983072 | tf_op jit(solution)/shard_map/ppermute | solution.py:516
  (185 shorter events, 208.3 us)
Async XLA Ops:
  7.2 170.9 %all-gather.4.cloned.1.call-start = ((), (), s32[]{:S(2)}) async-start(), calls=%async_computation.1 | async-start | bytes 17694720 | tf_op jit(solution)/shard_map/all_gather | solution.py:461
  11.0 252.4 %all-gather.6.cloned.1.call-start = ((), (), s32[]{:S(2)}) async-start(), calls=%async_computation.2 | async-start | bytes 10616832 | tf_op jit(solution)/shard_map/all_gather | solution.py:462
  11.8 706.6 %reduce-scatter.2.cloned.1.call-start = ((), (), s32[]{:S(2)}) async-start(), calls=%async_computation.3 | async-start | bytes 21233664 | tf_op jit(solution)/shard_map/reduce_scatter | solution.py:504
  21.5 147.3 %collective-permute-start = (bf16[2,256,3072]{2,1,0:T(8,128)(2,1)}, bf16[2,256,3072]{2,1,0:T(8,128)(2,1)}, u32[]{:S(2)}, u32[]{:S(2)}) collective-permute-start(bf16[2,256,3072]{2,1,0:T(8,128)(2,1)} %slice.62), channel_id=1, source_target_pairs={{0,8},{8,0},{1,9},{9,1},{2,10},{10,2},{3,11},{11,3},{4,12},{12,4},... | collective-permute-start | bytes 9437192 | tf_op jit(solution)/shard_map/ppermute | solution.py:434
  24.9 140.2 %collective-permute-start.2 = (bf16[1,256,3072]{2,1,0:T(8,128)(2,1)}, bf16[1,256,3072]{2,1,0:T(8,128)(2,1)}, u32[]{:S(2)}, u32[]{:S(2)}) collective-permute-start(bf16[1,256,3072]{2,1,0:T(8,128)(2,1)} %slice.61), channel_id=1, source_target_pairs={{0,8},{8,0},{1,9},{9,1},{2,10},{10,2},{3,11},{11,3},{4,12},{12,4},... | collective-permute-start | bytes 4718600 | tf_op jit(solution)/shard_map/ppermute | solution.py:434
  24.9 136.7 %collective-permute-start.1 = (bf16[1,256,3072]{2,1,0:T(8,128)(2,1)}, bf16[1,256,3072]{2,1,0:T(8,128)(2,1)}, u32[]{:S(2)}, u32[]{:S(2)}) collective-permute-start(bf16[1,256,3072]{2,1,0:T(8,128)(2,1)} %slice.60), channel_id=1, source_target_pairs={{0,8},{8,0},{1,9},{9,1},{2,10},{10,2},{3,11},{11,3},{4,12},{12,4},... | collective-permute-start | bytes 4718600 | tf_op jit(solution)/shard_map/ppermute | solution.py:434
  28.8 302.2 %collective-permute-start.4 = (bf16[1,256,3072]{2,1,0:T(8,128)(2,1)}, bf16[1,256,3072]{2,1,0:T(8,128)(2,1)}, u32[]{:S(2)}, u32[]{:S(2)}) collective-permute-start(bf16[1,256,3072]{2,1,0:T(8,128)(2,1)} %get-tuple-element.137), channel_id=1, source_target_pairs={{0,8},{8,0},{1,9},{9,1},{2,10},{10,2},{3,11},{11,3},{4,12},{12,4},... | collective-permute-start | bytes 4718600 | tf_op jit(solution)/shard_map/ppermute | solution.py:434
  28.8 336.2 %collective-permute-start.3 = (bf16[1,256,3072]{2,1,0:T(8,128)(2,1)}, bf16[1,256,3072]{2,1,0:T(8,128)(2,1)}, u32[]{:S(2)}, u32[]{:S(2)}) collective-permute-start(bf16[1,256,3072]{2,1,0:T(8,128)(2,1)} %get-tuple-element.138), channel_id=1, source_target_pairs={{0,8},{8,0},{1,9},{9,1},{2,10},{10,2},{3,11},{11,3},{4,12},{12,4},... | collective-permute-start | bytes 4718600 | tf_op jit(solution)/shard_map/ppermute | solution.py:434
  161.6 134.0 %collective-permute-start.5 = (bf16[2,256,3072]{2,1,0:T(8,128)(2,1)}, bf16[2,256,3072]{2,1,0:T(8,128)(2,1)}, u32[]{:S(2)}, u32[]{:S(2)}) collective-permute-start(bf16[2,256,3072]{2,1,0:T(8,128)(2,1)} %slice.67), channel_id=1, source_target_pairs={{0,8},{8,0},{1,9},{9,1},{2,10},{10,2},{3,11},{11,3},{4,12},{12,4},... | collective-permute-start | bytes 9437192 | tf_op jit(solution)/shard_map/ppermute | solution.py:434
  421.4 13.2 %collective-permute-start.6 = (f32[1536,1280]{1,0:T(8,128)}, f32[1536,1280]{1,0:T(8,128)}, u32[]{:S(2)}, u32[]{:S(2)}) collective-permute-start(f32[1536,1280]{1,0:T(8,128)} %convolution_bitcast_fusion.3), channel_id=1, source_target_pairs={{0,1},{1,0},{2,3},{3,2},{4,5},{5,4},{6,7},{7,6},{8,9},{9,8},{10,11... | collective-permute-start | bytes 23592968 | tf_op jit(solution)/shard_map/ppermute | solution.py:516
  432.0 50.2 %collective-permute-start.7 = (f32[1536,1280]{1,0:T(8,128)}, f32[1536,1280]{1,0:T(8,128)}, u32[]{:S(2)}, u32[]{:S(2)}) collective-permute-start(f32[1536,1280]{1,0:T(8,128)} %convolution_bitcast_fusion.2), channel_id=1, source_target_pairs={{0,1},{1,0},{2,3},{3,2},{4,5},{5,4},{6,7},{7,6},{8,9},{9,8},{10,11... | collective-permute-start | bytes 23592968 | tf_op jit(solution)/shard_map/ppermute | solution.py:516
  432.5 119.1 %collective-permute-start.11 = (bf16[2,256,3072]{2,1,0:T(8,128)(2,1)}, bf16[2,256,3072]{2,1,0:T(8,128)(2,1)}, u32[]{:S(2)}, u32[]{:S(2)}) collective-permute-start(bf16[2,256,3072]{2,1,0:T(8,128)(2,1)} %fusion.74), channel_id=1, source_target_pairs={{0,8},{8,0},{1,9},{9,1},{2,10},{10,2},{3,11},{11,3},{4,12},{12,4},... | collective-permute-start | bytes 9437192 | tf_op jit(solution)/shard_map/ppermute | solution.py:434
  434.3 136.8 %collective-permute-start.10 = (bf16[2,256,3072]{2,1,0:T(8,128)(2,1)}, bf16[2,256,3072]{2,1,0:T(8,128)(2,1)S(1)}, u32[]{:S(2)}, u32[]{:S(2)}) collective-permute-start(bf16[2,256,3072]{2,1,0:T(8,128)(2,1)} %fusion.77), channel_id=1, source_target_pairs={{0,8},{8,0},{1,9},{9,1},{2,10},{10,2},{3,11},{11,3},{4,12},{12,4},... | collective-permute-start | bytes 9437192 | tf_op jit(solution)/shard_map/ppermute | solution.py:434
  452.2 81.1 %collective-permute-start.8 = (f32[2,384,640]{2,1,0:T(8,128)}, f32[2,384,640]{2,1,0:T(8,128)}, u32[]{:S(2)}, u32[]{:S(2)}) collective-permute-start(f32[2,384,640]{2,1,0:T(8,128)} %dynamic-slice_bitcast_fusion.3), channel_id=1, source_target_pairs={{0,2},{1,3},{2,0},{3,1},{4,6},{5,7},{6,4},{7,5},{8,10},{9,11},{10,... | collective-permute-start | bytes 5898248 | tf_op jit(solution)/shard_map/ppermute | solution.py:516
  453.9 80.9 %collective-permute-start.9 = (f32[2,384,640]{2,1,0:T(8,128)}, f32[2,384,640]{2,1,0:T(8,128)}, u32[]{:S(2)}, u32[]{:S(2)}) collective-permute-start(f32[2,384,640]{2,1,0:T(8,128)} %dynamic-slice_bitcast_fusion.2), channel_id=1, source_target_pairs={{0,4},{1,5},{2,6},{3,7},{4,0},{5,1},{6,2},{7,3},{8,12},{9,13},{10,... | collective-permute-start | bytes 5898248 | tf_op jit(solution)/shard_map/ppermute | solution.py:516
  500.5 152.9 %collective-permute-start.12 = (f32[2,384,640]{2,1,0:T(8,128)}, f32[2,384,640]{2,1,0:T(8,128)}, u32[]{:S(2)}, u32[]{:S(2)}) collective-permute-start(f32[2,384,640]{2,1,0:T(8,128)} %dynamic-slice_bitcast_fusion.1), channel_id=1, source_target_pairs={{0,2},{1,3},{2,0},{3,1},{4,6},{5,7},{6,4},{7,5},{8,10},{9,11},{10,... | collective-permute-start | bytes 5898248 | tf_op jit(solution)/shard_map/ppermute | solution.py:516
  533.3 121.5 %collective-permute-start.13 = (f32[2,384,640]{2,1,0:T(8,128)}, f32[2,384,640]{2,1,0:T(8,128)}, u32[]{:S(2)}, u32[]{:S(2)}) collective-permute-start(f32[2,384,640]{2,1,0:T(8,128)} %dynamic-slice_bitcast_fusion), channel_id=1, source_target_pairs={{0,4},{1,5},{2,6},{3,7},{4,0},{5,1},{6,2},{7,3},{8,12},{9,13},{10,... | collective-permute-start | bytes 5898248 | tf_op jit(solution)/shard_map/ppermute | solution.py:516
  534.8 103.8 %collective-permute-start.14 = (bf16[2,256,3072]{2,1,0:T(8,128)(2,1)}, bf16[2,256,3072]{2,1,0:T(8,128)(2,1)S(1)}, u32[]{:S(2)}, u32[]{:S(2)}) collective-permute-start(bf16[2,256,3072]{2,1,0:T(8,128)(2,1)} %fusion.68), channel_id=1, source_target_pairs={{0,8},{8,0},{1,9},{9,1},{2,10},{10,2},{3,11},{11,3},{4,12},{12,4},... | collective-permute-start | bytes 9437192 | tf_op jit(solution)/shard_map/ppermute | solution.py:434
  551.7 120.7 %collective-permute-start.17 = (bf16[1,256,3072]{2,1,0:T(8,128)(2,1)}, bf16[1,256,3072]{2,1,0:T(8,128)(2,1)}, u32[]{:S(2)}, u32[]{:S(2)}) collective-permute-start(bf16[1,256,3072]{2,1,0:T(8,128)(2,1)} %get-tuple-element.140), channel_id=1, source_target_pairs={{0,8},{8,0},{1,9},{9,1},{2,10},{10,2},{3,11},{11,3},{4,12},{12,4},... | collective-permute-start | bytes 4718600 | tf_op jit(solution)/shard_map/ppermute | solution.py:434
  571.1 133.9 %collective-permute-start.20 = (bf16[1,256,3072]{2,1,0:T(8,128)(2,1)S(1)}, bf16[1,256,3072]{2,1,0:T(8,128)(2,1)S(1)}, u32[]{:S(2)}, u32[]{:S(2)}) collective-permute-start(bf16[1,256,3072]{2,1,0:T(8,128)(2,1)S(1)} %copy-done.21), channel_id=1, source_target_pairs={{0,8},{8,0},{1,9},{9,1},{2,10},{10,2},{3,11},{11,3},{4,12},{12,4},... | collective-permute-start | bytes 4718600 | tf_op jit(solution)/shard_map/ppermute | solution.py:434
  640.2 39.1 %collective-permute-start.16 = (f32[384,640]{1,0:T(8,128)}, f32[384,640]{1,0:T(8,128)S(1)}, u32[]{:S(2)}, u32[]{:S(2)}) collective-permute-start(f32[384,640]{1,0:T(8,128)} %dynamic-slice_bitcast_fusion.11), channel_id=1, source_target_pairs={{0,4},{1,5},{2,6},{3,7},{4,0},{5,1},{6,2},{7,3},{8,12},{9,13},{10,... | collective-permute-start | bytes 2949128 | tf_op jit(solution)/shard_map/ppermute | solution.py:516
  653.4 25.9 %collective-permute-start.18 = (f32[384,640]{1,0:T(8,128)}, f32[384,640]{1,0:T(8,128)S(1)}, u32[]{:S(2)}, u32[]{:S(2)}) collective-permute-start(f32[384,640]{1,0:T(8,128)} %dynamic-slice_bitcast_fusion.10), channel_id=1, source_target_pairs={{0,2},{1,3},{2,0},{3,1},{4,6},{5,7},{6,4},{7,5},{8,10},{9,11},{10,... | collective-permute-start | bytes 2949128 | tf_op jit(solution)/shard_map/ppermute | solution.py:516
  661.3 22.1 %collective-permute-start.15 = (f32[384,640]{1,0:T(8,128)}, f32[384,640]{1,0:T(8,128)S(1)}, u32[]{:S(2)}, u32[]{:S(2)}) collective-permute-start(f32[384,640]{1,0:T(8,128)} %dynamic-slice_bitcast_fusion.9), channel_id=1, source_target_pairs={{0,4},{1,5},{2,6},{3,7},{4,0},{5,1},{6,2},{7,3},{8,12},{9,13},{10,... | collective-permute-start | bytes 2949128 | tf_op jit(solution)/shard_map/ppermute | solution.py:516
  672.4 23.9 %collective-permute-start.19 = (f32[384,640]{1,0:T(8,128)}, f32[384,640]{1,0:T(8,128)S(1)}, u32[]{:S(2)}, u32[]{:S(2)}) collective-permute-start(f32[384,640]{1,0:T(8,128)} %dynamic-slice_bitcast_fusion.8), channel_id=1, source_target_pairs={{0,2},{1,3},{2,0},{3,1},{4,6},{5,7},{6,4},{7,5},{8,10},{9,11},{10,... | collective-permute-start | bytes 2949128 | tf_op jit(solution)/shard_map/ppermute | solution.py:516
  (38 other events, 546.6 us)
Sparse Core Ops, SparseCore 0:
  11.2 84.3 all-gather.3
  97.4 56.7 all-gather.5
  385.0 164.8 reduce-scatter.1
